TPU v7x, 512 devices: a 8x2x16 block of a 8x8x16 slice. The times are simulated.
512 devices in a mesh: groups: 2 (over y), gx: 128 (over z, x), gy: 2 (over core).
Axes of the slice: x: 8, y: 2, z: 16, core: 2. Of those that a mesh axis runs over, the one named last changes fastest.
The devices are a block of a 8x8x16 slice.
Arguments:
- forcing: float32 [2, 8192, 3072], P(None, ('groups', 'gx'), 'gy'), parts along dimension 1, may hold values from -6 to 6
- viscosity: float32 [8192, 3072], P(('groups', 'gx'), 'gy'), parts along dimension 0, may hold values from 0.25 to 8
- mass: float32 [8192, 3072], P(('groups', 'gx'), 'gy'), parts along dimension 0, may hold values from 0.5 to 2
- coriolis: float32 [3072], P('gy'), may hold values from 0.1 to 0.45
- land: int32 [4096, 3072], P('gx', 'gy'), may hold values 0 or 1
- ice_tiles: int32 [64, 24], P('groups'), parts along dimension 0, may hold values 0 or 1
Outputs:
- velocity: float32 [2, 8192, 3072], P(None, ('groups', 'gx'), 'gy'), parts along dimension 1
There are 2 independent parts, one for each index of `groups`. A program takes and returns all parts, laid end to end along the dimension named above; an argument that names none is the same for every part. Nothing has to cross between parts.
Inputs may be any that keep to these rules, and one draw needn't show every extreme that they name: 1 marks land. `ice_tiles`: 1 marks a tile with ice.
All inputs are finite; a program needn't handle non-finite values. No bound on the sum of `land` on one device may be relied on, other than what follows from the above.
Results may differ from a plain program's by a relative error of at most 0.00005.
Values sent between devices are 32-bit elements; how exact they have to be, the bound alone decides.
No kernel may reach another device: no remote copies, remote signals or barrier semaphores. Data moves between devices by JAX's collectives and lax.ppermute only.
A program may use at most 64 MiB of HBM per device.

v0:
```python
import jax
import jax.numpy as jnp
from jax import lax
from jax.sharding import PartitionSpec as P

TILE = 128
LEVELS = 4
PRE = 1
POST = 1
CSWEEPS = 3


relax_weight = 0.8
land_mass = 4.0


def swapped(value, axis, bit):
    return lax.ppermute(value, axis, [(i, i ^ 1 << bit) for i in range(lax.axis_size(axis))])


def padded_2(value, sides, width):
    edges = {}
    for axis, dim in sides:
        size, length = (lax.axis_size(axis), value.shape[dim])
        up = [(i, (i + 1) % size) for i in range(size)]
        last = lax.slice_in_dim(value, length - width, length, axis=dim)
        first = lax.slice_in_dim(value, 0, width, axis=dim)
        edges[dim] = (
            lax.ppermute(last, axis, up),
            lax.ppermute(first, axis, [(b, a) for a, b in up]),
        )
    done = []
    for _, dim in sides:
        low, high = edges[dim]
        around = [(width, width) if d in done else (0, 0) for d in range(value.ndim)]
        value = jnp.concatenate([jnp.pad(low, around), value, jnp.pad(high, around)], axis=dim)
        done.append(dim)
    return value


def pair_mean(values):
    return 0.25 * (
        values[..., 0::2, 0::2]
        + values[..., 1::2, 0::2]
        + values[..., 0::2, 1::2]
        + values[..., 1::2, 1::2]
    )


def combine(field, east_nb, west_nb, north_nb, south_nb, stencil):
    east, west, north, south, diagonal, rotation = stencil
    turned = jnp.stack([-field[1], field[0]]) * rotation
    return (
        diagonal * field
        - east * east_nb
        - west * west_nb
        - north * north_nb
        - south * south_nb
        + turned
    )


def mirror_row(field):
    partner = field[:, :, -1]
    for bit in range(lax.axis_size("gx").bit_length() - 1):
        partner = swapped(partner, "gx", bit)
    return -partner[:, ::-1]


def spread_apply(field, stencil, at_top, at_bottom):
    padded = padded_2(field, (("gx", 1), ("gy", 2)), 1)
    mirrored = mirror_row(field)
    north_edge = jnp.where(at_top, mirrored[:, :, None], padded[:, 1:-1, -1:])
    south_edge = jnp.where(at_bottom, 0.0, padded[:, 1:-1, :1])
    east_nb = padded[:, 2:, 1:-1]
    west_nb = padded[:, :-2, 1:-1]
    north_nb = jnp.concatenate([field[:, :, 1:], north_edge], 2)
    south_nb = jnp.concatenate([south_edge, field[:, :, :-1]], 2)
    return combine(field, east_nb, west_nb, north_nb, south_nb, stencil)


def smooth(field, source, stencil, count, from_zero, applier):
    for sweep in range(count):
        if from_zero and sweep == 0:
            field = relax_weight * source / stencil[4]
        else:
            field = field + relax_weight * (source - applier(field, stencil)) / stencil[4]
    return field


def local(forcing, viscosity, mass, coriolis, land, ice_tiles):
    col_index = lax.axis_index("gx")
    row_index = lax.axis_index("gy")
    at_top = row_index == lax.axis_size("gy") - 1
    at_bottom = row_index == 0
    width_x = viscosity.shape[0]
    width_y = viscosity.shape[1]
    land_float = land.astype(jnp.float32)
    ocean = 1.0 - land_float
    tile_x = (col_index * width_x + jnp.arange(width_x, dtype=jnp.int32)) // TILE
    tile_y = (row_index * width_y + jnp.arange(width_y, dtype=jnp.int32)) // TILE
    pick_x = (tile_x[:, None] == jnp.arange(ice_tiles.shape[0], dtype=jnp.int32)[None, :]).astype(
        jnp.float32
    )
    pick_y = (tile_y[:, None] == jnp.arange(ice_tiles.shape[1], dtype=jnp.int32)[None, :]).astype(
        jnp.float32
    )
    ice_rows = jnp.dot(pick_x, ice_tiles.astype(jnp.float32), precision=lax.Precision.HIGHEST)
    ice = jnp.dot(ice_rows, pick_y.T, precision=lax.Precision.HIGHEST)
    visc_eff = viscosity * ice * ocean
    mass_eff = mass * ocean + land_mass * land_float
    source = forcing * ocean
    visc_pad = padded_2(visc_eff, (("gx", 0), ("gy", 1)), 1)
    visc_partner = visc_eff[:, -1]
    for bit in range(lax.axis_size("gx").bit_length() - 1):
        visc_partner = swapped(visc_partner, "gx", bit)
    mirror_visc = visc_partner[::-1]
    east = 0.5 * (visc_eff + visc_pad[2:, 1:-1])
    west = 0.5 * (visc_pad[:-2, 1:-1] + visc_eff)
    north_last = jnp.where(
        at_top, 0.5 * (visc_eff[:, -1] + mirror_visc), 0.5 * (visc_eff[:, -1] + visc_pad[1:-1, -1])
    )
    north = jnp.concatenate([0.5 * (visc_eff[:, :-1] + visc_eff[:, 1:]), north_last[:, None]], 1)
    south_first = jnp.where(at_bottom, visc_eff[:, 0], 0.5 * (visc_pad[1:-1, 0] + visc_eff[:, 0]))
    south = jnp.concatenate([south_first[:, None], north[:, :-1]], 1)
    mass_now = mass_eff
    rotation = coriolis
    levels = []
    for level in range(LEVELS):
        if level > 0:
            east = 0.25 * (east[1::2, 0::2] + east[1::2, 1::2])
            west = 0.25 * (west[0::2, 0::2] + west[0::2, 1::2])
            north = 0.25 * (north[0::2, 1::2] + north[1::2, 1::2])
            south = 0.25 * (south[0::2, 0::2] + south[1::2, 0::2])
            mass_now = pair_mean(mass_now)
            rotation = 0.5 * (rotation[0::2] + rotation[1::2])
        diagonal = mass_now + east + west + north + south
        levels.append((east, west, north, south, diagonal, rotation))

    def spread_fn(field, stencil):
        return spread_apply(field, stencil, at_top, at_bottom)

    def vcycle(level, right_side, field, from_zero):
        stencil = levels[level]
        if level == LEVELS - 1:
            return smooth(None, right_side, stencil, CSWEEPS, True, spread_fn)
        field = smooth(field, right_side, stencil, PRE, from_zero, spread_fn)
        residue = right_side - spread_fn(field, stencil)
        coarse = vcycle(level + 1, pair_mean(residue), None, True)
        field = field + jnp.repeat(jnp.repeat(coarse, 2, 1), 2, 2)
        return smooth(field, right_side, stencil, POST, False, spread_fn)

    field = None
    field = vcycle(0, source, field, 0 == 0)
    return field


def solution(mesh):
    return jax.shard_map(
        local,
        mesh=mesh,
        in_specs=(
            P(None, ("groups", "gx"), "gy"),
            P(("groups", "gx"), "gy"),
            P(("groups", "gx"), "gy"),
            P("gy"),
            P("gx", "gy"),
            P("groups", None),
        ),
        out_specs=P(None, ("groups", "gx"), "gy"),
        check_vma=False,
    )
```

profile of v0, /device:TPU:65, one launch (start us, length us, event | category | flops | bytes accessed | tf_op | source)
XLA Modules:
  0.0 671.7 jit_solution(10363884882420592323)
XLA Ops:
  2.8 43.5 %collective-permute-start.10 = (f32[32,1]{1,0:T(8,128)S(1)}, f32[32,1]{1,0:T(8,128)S(1)}, u32[]{:S(2)}, u32[]{:S(2)}) collective-permute-start(f32[32,1]{1,0:T(8,128)S(1)} %slice.621), channel_id=1, source_target_pairs={{0,1},{1,0},{2,3},{3,2},{4,5},{5,4},{6,7},{7,6},{8,9},{9,8},{10,11... | collective-permute-start | bytes 392 | tf_op jit(solution)/shard_map/ppermute | solution.py:29
  46.4 7.0 %collective-permute-start = (f32[1,1536]{1,0:T(1,128)S(1)}, f32[1,1536]{1,0:T(1,128)S(1)}, u32[]{:S(2)}, u32[]{:S(2)}) collective-permute-start(f32[1,1536]{1,0:T(1,128)S(1)} %get-tuple-element.57), channel_id=1, source_target_pairs={{2,0},{4,2},{6,4},{8,6},{10,8},{12,10},{14,12},{16,14},{18,16},{20... | collective-permute-start | bytes 18440 | tf_op jit(solution)/shard_map/ppermute | solution.py:30
  69.7 5.8 collective-permute-done.4
  87.1 7.7 %collective-permute-start.9 = (f32[32,1]{1,0:T(8,128)S(1)}, f32[32,1]{1,0:T(8,128)S(1)}, u32[]{:S(2)}, u32[]{:S(2)}) collective-permute-start(f32[32,1]{1,0:T(8,128)S(1)} %get-tuple-element.54), channel_id=1, source_target_pairs={{1,0},{0,1},{3,2},{2,3},{5,4},{4,5},{7,6},{6,7},{9,8},{8,9},{11,10... | collective-permute-start | bytes 392 | tf_op jit(solution)/shard_map/ppermute | solution.py:30
  94.8 5.6 collective-permute-start.8
  100.5 7.4 %collective-permute-done.8 = f32[32]{0:T(128)S(1)} collective-permute-done((f32[32]{0:T(128)S(1)}, f32[32]{0:T(128)S(1)}, u32[]{:S(2)}, u32[]{:S(2)}) %collective-permute-start.8) | collective-permute-done | bytes 160 | tf_op jit(solution)/shard_map/ppermute | solution.py:18
  157.5 5.6 collective-permute-done.15
  165.3 12.0 %collective-permute-start.20 = (f32[2,32,1]{2,1,0:T(8,128)}, f32[2,32,1]{2,1,0:T(8,128)S(1)}, u32[]{:S(2)}, u32[]{:S(2)}) collective-permute-start(f32[2,32,1]{2,1,0:T(8,128)} %get-tuple-element.47), channel_id=1, source_target_pairs={{1,0},{0,1},{3,2},{2,3},{5,4},{4,5},{7,6},{6,7},{9,8},{8,9},{11,10... | collective-permute-start | bytes 776 | tf_op jit(solution)/shard_map/ppermute | solution.py:30
  182.0 7.0 %collective-permute-start.11 = (f32[2,1,1536]{2,0,1:T(2,128)S(1)}, f32[2,1,1536]{2,0,1:T(2,128)S(1)}, u32[]{:S(2)}, u32[]{:S(2)}) collective-permute-start(f32[2,1,1536]{2,0,1:T(2,128)S(1)} %copy.551), channel_id=1, source_target_pairs={{2,0},{4,2},{6,4},{8,6},{10,8},{12,10},{14,12},{16,14},{18,16},{20... | collective-permute-start | bytes 36872 | tf_op jit(solution)/shard_map/ppermute | solution.py:30
  194.9 5.7 collective-permute-done.18
  203.3 10.3 %collective-permute-done.19 = f32[2,32]{1,0:T(2,128)S(1)} collective-permute-done((f32[2,32]{1,0:T(2,128)S(1)}, f32[2,32]{1,0:T(2,128)S(1)}, u32[]{:S(2)}, u32[]{:S(2)}) %collective-permute-start.19) | collective-permute-done | bytes 288 | tf_op jit(solution)/shard_map/ppermute | solution.py:18
  242.0 7.3 %collective-permute-start.31 = (f32[2,16,1]{2,1,0:T(8,128)S(1)}, f32[2,16,1]{2,1,0:T(8,128)S(1)}, u32[]{:S(2)}, u32[]{:S(2)}) collective-permute-start(f32[2,16,1]{2,1,0:T(8,128)S(1)} %get-tuple-element.71), channel_id=1, source_target_pairs={{1,0},{0,1},{3,2},{2,3},{5,4},{4,5},{7,6},{6,7},{9,8},{8,9},{11,10... | collective-permute-start | bytes 392 | tf_op jit(solution)/shard_map/ppermute | solution.py:30
  251.3 7.4 %collective-permute-start.32 = (f32[2,16,1]{2,1,0:T(8,128)S(1)}, f32[2,16,1]{2,1,0:T(8,128)S(1)}, u32[]{:S(2)}, u32[]{:S(2)}) collective-permute-start(f32[2,16,1]{2,1,0:T(8,128)S(1)} %get-tuple-element.69), channel_id=1, source_target_pairs={{0,1},{1,0},{2,3},{3,2},{4,5},{5,4},{6,7},{7,6},{8,9},{9,8},{10,11... | collective-permute-start | bytes 392 | tf_op jit(solution)/shard_map/ppermute | solution.py:29
  262.0 9.1 %collective-permute-start.22 = (f32[2,1,768]{2,0,1:T(2,128)S(1)}, f32[2,1,768]{2,0,1:T(2,128)S(1)}, u32[]{:S(2)}, u32[]{:S(2)}) collective-permute-start(f32[2,1,768]{2,0,1:T(2,128)S(1)} %copy.556), channel_id=1, source_target_pairs={{2,0},{4,2},{6,4},{8,6},{10,8},{12,10},{14,12},{16,14},{18,16},{20... | collective-permute-start | bytes 18440 | tf_op jit(solution)/shard_map/ppermute | solution.py:30
  275.1 4.3 collective-permute-done.29
  282.3 10.1 %collective-permute-done.30 = f32[2,16]{1,0:T(2,128)S(1)} collective-permute-done((f32[2,16]{1,0:T(2,128)S(1)}, f32[2,16]{1,0:T(2,128)S(1)}, u32[]{:S(2)}, u32[]{:S(2)}) %collective-permute-start.30) | collective-permute-done | bytes 160 | tf_op jit(solution)/shard_map/ppermute | solution.py:18
  308.2 7.1 %collective-permute-start.42 = (f32[2,8,1]{2,1,0:T(8,128)S(1)}, f32[2,8,1]{2,1,0:T(8,128)S(1)}, u32[]{:S(2)}, u32[]{:S(2)}) collective-permute-start(f32[2,8,1]{2,1,0:T(8,128)S(1)} %get-tuple-element.89), channel_id=1, source_target_pairs={{1,0},{0,1},{3,2},{2,3},{5,4},{4,5},{7,6},{6,7},{9,8},{8,9},{11,10... | collective-permute-start | bytes 200 | tf_op jit(solution)/shard_map/ppermute | solution.py:30
  317.3 7.4 %collective-permute-start.43 = (f32[2,8,1]{2,1,0:T(8,128)S(1)}, f32[2,8,1]{2,1,0:T(8,128)S(1)}, u32[]{:S(2)}, u32[]{:S(2)}) collective-permute-start(f32[2,8,1]{2,1,0:T(8,128)S(1)} %get-tuple-element.87), channel_id=1, source_target_pairs={{0,1},{1,0},{2,3},{3,2},{4,5},{5,4},{6,7},{7,6},{8,9},{9,8},{10,11... | collective-permute-start | bytes 200 | tf_op jit(solution)/shard_map/ppermute | solution.py:29
  326.7 5.4 collective-permute-start.33
  340.3 5.5 collective-permute-start.41
  345.9 7.5 %collective-permute-done.41 = f32[2,8]{1,0:T(2,128)S(1)} collective-permute-done((f32[2,8]{1,0:T(2,128)S(1)}, f32[2,8]{1,0:T(2,128)S(1)}, u32[]{:S(2)}, u32[]{:S(2)}) %collective-permute-start.41) | collective-permute-done | bytes 96 | tf_op jit(solution)/shard_map/ppermute | solution.py:18
  357.1 4.8 collective-permute-start.53
  363.9 4.8 collective-permute-start.44
  378.6 5.6 collective-permute-done.48
  402.1 6.6 collective-permute-start.52
  408.6 6.5 collective-permute-done.52
  418.0 10.1 %collective-permute-start.64 = (f32[2,4,1]{2,1,0:T(4,128)S(1)}, f32[2,4,1]{2,1,0:T(4,128)S(1)}, u32[]{:S(2)}, u32[]{:S(2)}) collective-permute-start(f32[2,4,1]{2,1,0:T(4,128)S(1)} %get-tuple-element.98), channel_id=1, source_target_pairs={{1,0},{0,1},{3,2},{2,3},{5,4},{4,5},{7,6},{6,7},{9,8},{8,9},{11,10... | collective-permute-start | bytes 104 | tf_op jit(solution)/shard_map/ppermute | solution.py:30
  430.1 6.2 collective-permute-start.55
  445.4 6.3 collective-permute-done.59
  461.3 4.3 collective-permute-start.62
  469.5 6.6 collective-permute-start.63
  476.1 6.5 collective-permute-done.63
  496.3 11.1 %collective-permute-start.75 = (f32[2,8,1]{2,1,0:T(8,128)S(1)}, f32[2,8,1]{2,1,0:T(8,128)S(1)}, u32[]{:S(2)}, u32[]{:S(2)}) collective-permute-start(f32[2,8,1]{2,1,0:T(8,128)S(1)} %get-tuple-element.80), channel_id=1, source_target_pairs={{1,0},{0,1},{3,2},{2,3},{5,4},{4,5},{7,6},{6,7},{9,8},{8,9},{11,10... | collective-permute-start | bytes 200 | tf_op jit(solution)/shard_map/ppermute | solution.py:30
  511.1 5.3 collective-permute-start.76
  518.6 6.8 %collective-permute-start.66 = (f32[2,1,384]{2,1,0:T(1,128)S(1)}, f32[2,1,384]{2,1,0:T(1,128)S(1)}, u32[]{:S(2)}, u32[]{:S(2)}) collective-permute-start(f32[2,1,384]{2,1,0:T(1,128)S(1)} %get-tuple-element.83), channel_id=1, source_target_pairs={{2,0},{4,2},{6,4},{8,6},{10,8},{12,10},{14,12},{16,14},{18,16},{20... | collective-permute-start | bytes 9224 | tf_op jit(solution)/shard_map/ppermute | solution.py:30
  525.4 4.3 collective-permute-start.73
  533.7 6.6 collective-permute-start.74
  540.3 6.4 collective-permute-done.74
  561.6 6.5 collective-permute-start.86
  571.2 7.1 %collective-permute-start.87 = (f32[2,16,1]{2,1,0:T(8,128)S(1)}, f32[2,16,1]{2,1,0:T(8,128)S(1)}, u32[]{:S(2)}, u32[]{:S(2)}) collective-permute-start(f32[2,16,1]{2,1,0:T(8,128)S(1)} %get-tuple-element.60), channel_id=1, source_target_pairs={{0,1},{1,0},{2,3},{3,2},{4,5},{5,4},{6,7},{7,6},{8,9},{9,8},{10,11... | collective-permute-start | bytes 392 | tf_op jit(solution)/shard_map/ppermute | solution.py:29
  584.1 5.8 collective-permute-start.84
  592.4 8.5 %collective-permute-start.85 = (f32[2,16]{1,0:T(2,128)S(1)}, f32[2,16]{1,0:T(2,128)S(1)}, u32[]{:S(2)}, u32[]{:S(2)}) collective-permute-start(f32[2,16]{1,0:T(2,128)S(1)} %collective-permute-done.84), channel_id=1, source_target_pairs={{0,128},{2,130},{4,132},{6,134},{8,136},{10,138},{12,140},{14,142}... | collective-permute-start | bytes 392 | tf_op jit(solution)/shard_map/ppermute | solution.py:18
  600.9 4.8 collective-permute-done.85
  621.0 4.7 collective-permute-done.92
  633.6 11.2 %collective-permute-start.97 = (f32[2,32,1]{2,1,0:T(8,128)S(1)}, f32[2,32,1]{2,1,0:T(8,128)S(1)}, u32[]{:S(2)}, u32[]{:S(2)}) collective-permute-start(f32[2,32,1]{2,1,0:T(8,128)S(1)} %get-tuple-element.38), channel_id=1, source_target_pairs={{1,0},{0,1},{3,2},{2,3},{5,4},{4,5},{7,6},{6,7},{9,8},{8,9},{11,10... | collective-permute-start | bytes 776 | tf_op jit(solution)/shard_map/ppermute | solution.py:30
  650.6 4.3 collective-permute-start.88
  656.9 6.6 collective-permute-start.96
  663.5 6.4 collective-permute-done.96
  (415 shorter events, 305.7 us)
Async XLA Ops:
  2.8 54.4 %collective-permute-start.10 = (f32[32,1]{1,0:T(8,128)S(1)}, f32[32,1]{1,0:T(8,128)S(1)}, u32[]{:S(2)}, u32[]{:S(2)}) collective-permute-start(f32[32,1]{1,0:T(8,128)S(1)} %slice.621), channel_id=1, source_target_pairs={{0,1},{1,0},{2,3},{3,2},{4,5},{5,4},{6,7},{7,6},{8,9},{9,8},{10,11... | collective-permute-start | bytes 392 | tf_op jit(solution)/shard_map/ppermute | solution.py:29
  46.4 61.7 %collective-permute-start = (f32[1,1536]{1,0:T(1,128)S(1)}, f32[1,1536]{1,0:T(1,128)S(1)}, u32[]{:S(2)}, u32[]{:S(2)}) collective-permute-start(f32[1,1536]{1,0:T(1,128)S(1)} %get-tuple-element.57), channel_id=1, source_target_pairs={{2,0},{4,2},{6,4},{8,6},{10,8},{12,10},{14,12},{16,14},{18,16},{20... | collective-permute-start | bytes 18440 | tf_op jit(solution)/shard_map/ppermute | solution.py:30
  53.4 54.7 %collective-permute-start.1 = (f32[1,1536]{1,0:T(1,128)S(1)}, f32[1,1536]{1,0:T(1,128)S(1)}, u32[]{:S(2)}, u32[]{:S(2)}) collective-permute-start(f32[1,1536]{1,0:T(1,128)S(1)} %get-tuple-element.56), channel_id=1, source_target_pairs={{0,2},{2,4},{4,6},{6,8},{8,10},{10,12},{12,14},{14,16},{16,18},{18... | collective-permute-start | bytes 18440 | tf_op jit(solution)/shard_map/ppermute | solution.py:29
  87.1 13.3 %collective-permute-start.9 = (f32[32,1]{1,0:T(8,128)S(1)}, f32[32,1]{1,0:T(8,128)S(1)}, u32[]{:S(2)}, u32[]{:S(2)}) collective-permute-start(f32[32,1]{1,0:T(8,128)S(1)} %get-tuple-element.54), channel_id=1, source_target_pairs={{1,0},{0,1},{3,2},{2,3},{5,4},{4,5},{7,6},{6,7},{9,8},{8,9},{11,10... | collective-permute-start | bytes 392 | tf_op jit(solution)/shard_map/ppermute | solution.py:30
  94.8 13.1 %collective-permute-start.8 = (f32[32]{0:T(128)S(1)}, f32[32]{0:T(128)S(1)}, u32[]{:S(2)}, u32[]{:S(2)}) collective-permute-start(f32[32]{0:T(128)S(1)} %collective-permute-done.7), channel_id=1, source_target_pairs={{0,128},{2,130},{4,132},{6,134},{8,136},{10,138},{12,140},{14,142}... | collective-permute-start | bytes 392 | tf_op jit(solution)/shard_map/ppermute | solution.py:18
  163.2 16.1 %collective-permute-start.16 = (f32[2,32]{1,0:T(2,128)S(1)}, f32[2,32]{1,0:T(2,128)S(1)}, u32[]{:S(2)}, u32[]{:S(2)}) collective-permute-start(f32[2,32]{1,0:T(2,128)S(1)} %collective-permute-done.15), channel_id=1, source_target_pairs={{0,16},{2,18},{4,20},{6,22},{8,24},{10,26},{12,28},{14,30},{16,0},... | collective-permute-start | bytes 776 | tf_op jit(solution)/shard_map/ppermute | solution.py:18
  165.3 48.4 %collective-permute-start.20 = (f32[2,32,1]{2,1,0:T(8,128)}, f32[2,32,1]{2,1,0:T(8,128)S(1)}, u32[]{:S(2)}, u32[]{:S(2)}) collective-permute-start(f32[2,32,1]{2,1,0:T(8,128)} %get-tuple-element.47), channel_id=1, source_target_pairs={{1,0},{0,1},{3,2},{2,3},{5,4},{4,5},{7,6},{6,7},{9,8},{8,9},{11,10... | collective-permute-start | bytes 776 | tf_op jit(solution)/shard_map/ppermute | solution.py:30
  177.4 25.3 %collective-permute-start.21 = (f32[2,32,1]{2,1,0:T(8,128)}, f32[2,32,1]{2,1,0:T(8,128)S(1)}, u32[]{:S(2)}, u32[]{:S(2)}) collective-permute-start(f32[2,32,1]{2,1,0:T(8,128)} %get-tuple-element.45), channel_id=1, source_target_pairs={{0,1},{1,0},{2,3},{3,2},{4,5},{5,4},{6,7},{7,6},{8,9},{9,8},{10,11... | collective-permute-start | bytes 776 | tf_op jit(solution)/shard_map/ppermute | solution.py:29
  182.0 31.8 %collective-permute-start.11 = (f32[2,1,1536]{2,0,1:T(2,128)S(1)}, f32[2,1,1536]{2,0,1:T(2,128)S(1)}, u32[]{:S(2)}, u32[]{:S(2)}) collective-permute-start(f32[2,1,1536]{2,0,1:T(2,128)S(1)} %copy.551), channel_id=1, source_target_pairs={{2,0},{4,2},{6,4},{8,6},{10,8},{12,10},{14,12},{16,14},{18,16},{20... | collective-permute-start | bytes 36872 | tf_op jit(solution)/shard_map/ppermute | solution.py:30
  190.3 23.5 %collective-permute-start.12 = (f32[2,1,1536]{2,0,1:T(2,128)}, f32[2,1,1536]{2,0,1:T(2,128)}, u32[]{:S(2)}, u32[]{:S(2)}) collective-permute-start(f32[2,1,1536]{2,0,1:T(2,128)} %copy.553), channel_id=1, source_target_pairs={{0,2},{2,4},{4,6},{6,8},{8,10},{10,12},{12,14},{14,16},{16,18},{18... | collective-permute-start | bytes 36872 | tf_op jit(solution)/shard_map/ppermute | solution.py:29
  200.5 13.1 %collective-permute-start.19 = (f32[2,32]{1,0:T(2,128)S(1)}, f32[2,32]{1,0:T(2,128)S(1)}, u32[]{:S(2)}, u32[]{:S(2)}) collective-permute-start(f32[2,32]{1,0:T(2,128)S(1)} %collective-permute-done.18), channel_id=1, source_target_pairs={{0,128},{2,130},{4,132},{6,134},{8,136},{10,138},{12,140},{14,142}... | collective-permute-start | bytes 776 | tf_op jit(solution)/shard_map/ppermute | solution.py:18
  242.0 50.6 %collective-permute-start.31 = (f32[2,16,1]{2,1,0:T(8,128)S(1)}, f32[2,16,1]{2,1,0:T(8,128)S(1)}, u32[]{:S(2)}, u32[]{:S(2)}) collective-permute-start(f32[2,16,1]{2,1,0:T(8,128)S(1)} %get-tuple-element.71), channel_id=1, source_target_pairs={{1,0},{0,1},{3,2},{2,3},{5,4},{4,5},{7,6},{6,7},{9,8},{8,9},{11,10... | collective-permute-start | bytes 392 | tf_op jit(solution)/shard_map/ppermute | solution.py:30
  251.3 31.0 %collective-permute-start.32 = (f32[2,16,1]{2,1,0:T(8,128)S(1)}, f32[2,16,1]{2,1,0:T(8,128)S(1)}, u32[]{:S(2)}, u32[]{:S(2)}) collective-permute-start(f32[2,16,1]{2,1,0:T(8,128)S(1)} %get-tuple-element.69), channel_id=1, source_target_pairs={{0,1},{1,0},{2,3},{3,2},{4,5},{5,4},{6,7},{7,6},{8,9},{9,8},{10,11... | collective-permute-start | bytes 392 | tf_op jit(solution)/shard_map/ppermute | solution.py:29
  262.0 30.6 %collective-permute-start.22 = (f32[2,1,768]{2,0,1:T(2,128)S(1)}, f32[2,1,768]{2,0,1:T(2,128)S(1)}, u32[]{:S(2)}, u32[]{:S(2)}) collective-permute-start(f32[2,1,768]{2,0,1:T(2,128)S(1)} %copy.556), channel_id=1, source_target_pairs={{2,0},{4,2},{6,4},{8,6},{10,8},{12,10},{14,12},{16,14},{18,16},{20... | collective-permute-start | bytes 18440 | tf_op jit(solution)/shard_map/ppermute | solution.py:30
  273.1 19.6 %collective-permute-start.23 = (f32[2,1,768]{2,0,1:T(2,128)S(1)}, f32[2,1,768]{2,0,1:T(2,128)S(1)}, u32[]{:S(2)}, u32[]{:S(2)}) collective-permute-start(f32[2,1,768]{2,0,1:T(2,128)S(1)} %copy.558), channel_id=1, source_target_pairs={{0,2},{2,4},{4,6},{6,8},{8,10},{10,12},{12,14},{14,16},{16,18},{18... | collective-permute-start | bytes 18440 | tf_op jit(solution)/shard_map/ppermute | solution.py:29
  279.4 13.1 %collective-permute-start.30 = (f32[2,16]{1,0:T(2,128)S(1)}, f32[2,16]{1,0:T(2,128)S(1)}, u32[]{:S(2)}, u32[]{:S(2)}) collective-permute-start(f32[2,16]{1,0:T(2,128)S(1)} %collective-permute-done.29), channel_id=1, source_target_pairs={{0,128},{2,130},{4,132},{6,134},{8,136},{10,138},{12,140},{14,142}... | collective-permute-start | bytes 392 | tf_op jit(solution)/shard_map/ppermute | solution.py:18
  308.2 45.4 %collective-permute-start.42 = (f32[2,8,1]{2,1,0:T(8,128)S(1)}, f32[2,8,1]{2,1,0:T(8,128)S(1)}, u32[]{:S(2)}, u32[]{:S(2)}) collective-permute-start(f32[2,8,1]{2,1,0:T(8,128)S(1)} %get-tuple-element.89), channel_id=1, source_target_pairs={{1,0},{0,1},{3,2},{2,3},{5,4},{4,5},{7,6},{6,7},{9,8},{8,9},{11,10... | collective-permute-start | bytes 200 | tf_op jit(solution)/shard_map/ppermute | solution.py:30
  317.3 28.6 %collective-permute-start.43 = (f32[2,8,1]{2,1,0:T(8,128)S(1)}, f32[2,8,1]{2,1,0:T(8,128)S(1)}, u32[]{:S(2)}, u32[]{:S(2)}) collective-permute-start(f32[2,8,1]{2,1,0:T(8,128)S(1)} %get-tuple-element.87), channel_id=1, source_target_pairs={{0,1},{1,0},{2,3},{3,2},{4,5},{5,4},{6,7},{7,6},{8,9},{9,8},{10,11... | collective-permute-start | bytes 200 | tf_op jit(solution)/shard_map/ppermute | solution.py:29
  326.7 26.9 %collective-permute-start.33 = (f32[2,1,384]{2,1,0:T(1,128)S(1)}, f32[2,1,384]{2,1,0:T(1,128)S(1)}, u32[]{:S(2)}, u32[]{:S(2)}) collective-permute-start(f32[2,1,384]{2,1,0:T(1,128)S(1)} %get-tuple-element.92), channel_id=1, source_target_pairs={{2,0},{4,2},{6,4},{8,6},{10,8},{12,10},{14,12},{16,14},{18,16},{20... | collective-permute-start | bytes 9224 | tf_op jit(solution)/shard_map/ppermute | solution.py:30
  335.8 17.8 %collective-permute-start.34 = (f32[2,1,384]{2,1,0:T(1,128)S(1)}, f32[2,1,384]{2,1,0:T(1,128)S(1)}, u32[]{:S(2)}, u32[]{:S(2)}) collective-permute-start(f32[2,1,384]{2,1,0:T(1,128)S(1)} %get-tuple-element.93), channel_id=1, source_target_pairs={{0,2},{2,4},{4,6},{6,8},{8,10},{10,12},{12,14},{14,16},{16,18},{18... | collective-permute-start | bytes 9224 | tf_op jit(solution)/shard_map/ppermute | solution.py:29
  340.3 13.1 %collective-permute-start.41 = (f32[2,8]{1,0:T(2,128)S(1)}, f32[2,8]{1,0:T(2,128)S(1)}, u32[]{:S(2)}, u32[]{:S(2)}) collective-permute-start(f32[2,8]{1,0:T(2,128)S(1)} %collective-permute-done.40), channel_id=1, source_target_pairs={{0,128},{2,130},{4,132},{6,134},{8,136},{10,138},{12,140},{14,142}... | collective-permute-start | bytes 200 | tf_op jit(solution)/shard_map/ppermute | solution.py:18
  355.2 15.6 %collective-permute-start.46 = (f32[2,4]{1,0:T(2,128)S(1)}, f32[2,4]{1,0:T(2,128)S(1)}, u32[]{:S(2)}, u32[]{:S(2)}) collective-permute-start(f32[2,4]{1,0:T(2,128)S(1)} %get-tuple-element.106), channel_id=1, source_target_pairs={{0,2},{2,0},{4,6},{6,4},{8,10},{10,8},{12,14},{14,12},{16,18},{18,... | collective-permute-start | bytes 104 | tf_op jit(solution)/shard_map/ppermute | solution.py:18
  357.1 58.2 %collective-permute-start.53 = (f32[2,4,1]{2,1,0:T(4,128)S(1)}, f32[2,4,1]{2,1,0:T(4,128)S(1)}, u32[]{:S(2)}, u32[]{:S(2)}) collective-permute-start(f32[2,4,1]{2,1,0:T(4,128)S(1)} %get-tuple-element.107), channel_id=1, source_target_pairs={{1,0},{0,1},{3,2},{2,3},{5,4},{4,5},{7,6},{6,7},{9,8},{8,9},{11,10... | collective-permute-start | bytes 104 | tf_op jit(solution)/shard_map/ppermute | solution.py:30
  363.9 51.4 %collective-permute-start.44 = (f32[2,1,192]{2,1,0:T(1,128)S(1)}, f32[2,1,192]{2,1,0:T(1,128)S(1)}, u32[]{:S(2)}, u32[]{:S(2)}) collective-permute-start(f32[2,1,192]{2,1,0:T(1,128)S(1)} %get-tuple-element.110), channel_id=1, source_target_pairs={{2,0},{4,2},{6,4},{8,6},{10,8},{12,10},{14,12},{16,14},{18,16},{20... | collective-permute-start | bytes 4616 | tf_op jit(solution)/shard_map/ppermute | solution.py:30
  368.8 46.6 %collective-permute-start.45 = (f32[2,1,192]{2,1,0:T(1,128)S(1)}, f32[2,1,192]{2,1,0:T(1,128)S(1)}, u32[]{:S(2)}, u32[]{:S(2)}) collective-permute-start(f32[2,1,192]{2,1,0:T(1,128)S(1)} %get-tuple-element.111), channel_id=1, source_target_pairs={{0,2},{2,4},{4,6},{6,8},{8,10},{10,12},{12,14},{14,16},{16,18},{18... | collective-permute-start | bytes 4616 | tf_op jit(solution)/shard_map/ppermute | solution.py:29
  402.1 13.1 %collective-permute-start.52 = (f32[2,4]{1,0:T(2,128)S(1)}, f32[2,4]{1,0:T(2,128)S(1)}, u32[]{:S(2)}, u32[]{:S(2)}) collective-permute-start(f32[2,4]{1,0:T(2,128)S(1)} %collective-permute-done.51), channel_id=1, source_target_pairs={{0,128},{2,130},{4,132},{6,134},{8,136},{10,138},{12,140},{14,142}... | collective-permute-start | bytes 104 | tf_op jit(solution)/shard_map/ppermute | solution.py:18
  415.7 22.5 %collective-permute-start.57 = (f32[2,4]{1,0:T(2,128)S(1)}, f32[2,4]{1,0:T(2,128)S(1)}, u32[]{:S(2)}, u32[]{:S(2)}) collective-permute-start(f32[2,4]{1,0:T(2,128)S(1)} %get-tuple-element.97), channel_id=1, source_target_pairs={{0,2},{2,0},{4,6},{6,4},{8,10},{10,8},{12,14},{14,12},{16,18},{18,... | collective-permute-start | bytes 104 | tf_op jit(solution)/shard_map/ppermute | solution.py:18
  418.0 64.8 %collective-permute-start.64 = (f32[2,4,1]{2,1,0:T(4,128)S(1)}, f32[2,4,1]{2,1,0:T(4,128)S(1)}, u32[]{:S(2)}, u32[]{:S(2)}) collective-permute-start(f32[2,4,1]{2,1,0:T(4,128)S(1)} %get-tuple-element.98), channel_id=1, source_target_pairs={{1,0},{0,1},{3,2},{2,3},{5,4},{4,5},{7,6},{6,7},{9,8},{8,9},{11,10... | collective-permute-start | bytes 104 | tf_op jit(solution)/shard_map/ppermute | solution.py:30
  430.1 52.7 %collective-permute-start.55 = (f32[2,1,192]{2,1,0:T(1,128)S(1)}, f32[2,1,192]{2,1,0:T(1,128)S(1)}, u32[]{:S(2)}, u32[]{:S(2)}) collective-permute-start(f32[2,1,192]{2,1,0:T(1,128)S(1)} %get-tuple-element.101), channel_id=1, source_target_pairs={{2,0},{4,2},{6,4},{8,6},{10,8},{12,10},{14,12},{16,14},{18,16},{20... | collective-permute-start | bytes 4616 | tf_op jit(solution)/shard_map/ppermute | solution.py:30
  436.3 46.6 %collective-permute-start.56 = (f32[2,1,192]{2,1,0:T(1,128)S(1)}, f32[2,1,192]{2,1,0:T(1,128)S(1)}, u32[]{:S(2)}, u32[]{:S(2)}) collective-permute-start(f32[2,1,192]{2,1,0:T(1,128)S(1)} %get-tuple-element.102), channel_id=1, source_target_pairs={{0,2},{2,4},{4,6},{6,8},{8,10},{10,12},{12,14},{14,16},{16,18},{18... | collective-permute-start | bytes 4616 | tf_op jit(solution)/shard_map/ppermute | solution.py:29
  469.5 13.1 %collective-permute-start.63 = (f32[2,4]{1,0:T(2,128)S(1)}, f32[2,4]{1,0:T(2,128)S(1)}, u32[]{:S(2)}, u32[]{:S(2)}) collective-permute-start(f32[2,4]{1,0:T(2,128)S(1)} %collective-permute-done.62), channel_id=1, source_target_pairs={{0,128},{2,130},{4,132},{6,134},{8,136},{10,138},{12,140},{14,142}... | collective-permute-start | bytes 104 | tf_op jit(solution)/shard_map/ppermute | solution.py:18
  493.5 13.9 %collective-permute-start.70 = (f32[2,8]{1,0:T(2,128)S(1)}, f32[2,8]{1,0:T(2,128)S(1)}, u32[]{:S(2)}, u32[]{:S(2)}) collective-permute-start(f32[2,8]{1,0:T(2,128)S(1)} %collective-permute-done.69), channel_id=1, source_target_pairs={{0,8},{2,10},{4,12},{6,14},{8,0},{10,2},{12,4},{14,6},{16,24},{18,... | collective-permute-start | bytes 200 | tf_op jit(solution)/shard_map/ppermute | solution.py:18
  496.3 50.6 %collective-permute-start.75 = (f32[2,8,1]{2,1,0:T(8,128)S(1)}, f32[2,8,1]{2,1,0:T(8,128)S(1)}, u32[]{:S(2)}, u32[]{:S(2)}) collective-permute-start(f32[2,8,1]{2,1,0:T(8,128)S(1)} %get-tuple-element.80), channel_id=1, source_target_pairs={{1,0},{0,1},{3,2},{2,3},{5,4},{4,5},{7,6},{6,7},{9,8},{8,9},{11,10... | collective-permute-start | bytes 200 | tf_op jit(solution)/shard_map/ppermute | solution.py:30
  511.1 29.2 %collective-permute-start.76 = (f32[2,8,1]{2,1,0:T(8,128)S(1)}, f32[2,8,1]{2,1,0:T(8,128)S(1)}, u32[]{:S(2)}, u32[]{:S(2)}) collective-permute-start(f32[2,8,1]{2,1,0:T(8,128)S(1)} %get-tuple-element.78), channel_id=1, source_target_pairs={{0,1},{1,0},{2,3},{3,2},{4,5},{5,4},{6,7},{7,6},{8,9},{9,8},{10,11... | collective-permute-start | bytes 200 | tf_op jit(solution)/shard_map/ppermute | solution.py:29
  518.6 28.3 %collective-permute-start.66 = (f32[2,1,384]{2,1,0:T(1,128)S(1)}, f32[2,1,384]{2,1,0:T(1,128)S(1)}, u32[]{:S(2)}, u32[]{:S(2)}) collective-permute-start(f32[2,1,384]{2,1,0:T(1,128)S(1)} %get-tuple-element.83), channel_id=1, source_target_pairs={{2,0},{4,2},{6,4},{8,6},{10,8},{12,10},{14,12},{16,14},{18,16},{20... | collective-permute-start | bytes 9224 | tf_op jit(solution)/shard_map/ppermute | solution.py:30
  529.7 17.2 %collective-permute-start.67 = (f32[2,1,384]{2,1,0:T(1,128)S(1)}, f32[2,1,384]{2,1,0:T(1,128)S(1)}, u32[]{:S(2)}, u32[]{:S(2)}) collective-permute-start(f32[2,1,384]{2,1,0:T(1,128)S(1)} %get-tuple-element.84), channel_id=1, source_target_pairs={{0,2},{2,4},{4,6},{6,8},{8,10},{10,12},{12,14},{14,16},{16,18},{18... | collective-permute-start | bytes 9224 | tf_op jit(solution)/shard_map/ppermute | solution.py:29
  533.7 13.1 %collective-permute-start.74 = (f32[2,8]{1,0:T(2,128)S(1)}, f32[2,8]{1,0:T(2,128)S(1)}, u32[]{:S(2)}, u32[]{:S(2)}) collective-permute-start(f32[2,8]{1,0:T(2,128)S(1)} %collective-permute-done.73), channel_id=1, source_target_pairs={{0,128},{2,130},{4,132},{6,134},{8,136},{10,138},{12,140},{14,142}... | collective-permute-start | bytes 200 | tf_op jit(solution)/shard_map/ppermute | solution.py:18
  561.6 44.3 %collective-permute-start.86 = (f32[2,16,1]{2,1,0:T(8,128)S(1)}, f32[2,16,1]{2,1,0:T(8,128)S(1)}, u32[]{:S(2)}, u32[]{:S(2)}) collective-permute-start(f32[2,16,1]{2,1,0:T(8,128)S(1)} %get-tuple-element.62), channel_id=1, source_target_pairs={{1,0},{0,1},{3,2},{2,3},{5,4},{4,5},{7,6},{6,7},{9,8},{8,9},{11,10... | collective-permute-start | bytes 392 | tf_op jit(solution)/shard_map/ppermute | solution.py:30
  571.2 29.7 %collective-permute-start.87 = (f32[2,16,1]{2,1,0:T(8,128)S(1)}, f32[2,16,1]{2,1,0:T(8,128)S(1)}, u32[]{:S(2)}, u32[]{:S(2)}) collective-permute-start(f32[2,16,1]{2,1,0:T(8,128)S(1)} %get-tuple-element.60), channel_id=1, source_target_pairs={{0,1},{1,0},{2,3},{3,2},{4,5},{5,4},{6,7},{7,6},{8,9},{9,8},{10,11... | collective-permute-start | bytes 392 | tf_op jit(solution)/shard_map/ppermute | solution.py:29
  581.0 24.9 %collective-permute-start.77 = (f32[2,1,768]{2,0,1:T(2,128)S(1)}, f32[2,1,768]{2,0,1:T(2,128)S(1)}, u32[]{:S(2)}, u32[]{:S(2)}) collective-permute-start(f32[2,1,768]{2,0,1:T(2,128)S(1)} %copy.571), channel_id=1, source_target_pairs={{2,0},{4,2},{6,4},{8,6},{10,8},{12,10},{14,12},{16,14},{18,16},{20... | collective-permute-start | bytes 18440 | tf_op jit(solution)/shard_map/ppermute | solution.py:30
  589.9 16.0 %collective-permute-start.78 = (f32[2,1,768]{2,0,1:T(2,128)S(1)}, f32[2,1,768]{2,0,1:T(2,128)S(1)}, u32[]{:S(2)}, u32[]{:S(2)}) collective-permute-start(f32[2,1,768]{2,0,1:T(2,128)S(1)} %copy.573), channel_id=1, source_target_pairs={{0,2},{2,4},{4,6},{6,8},{8,10},{10,12},{12,14},{14,16},{16,18},{18... | collective-permute-start | bytes 18440 | tf_op jit(solution)/shard_map/ppermute | solution.py:29
  592.4 13.3 %collective-permute-start.85 = (f32[2,16]{1,0:T(2,128)S(1)}, f32[2,16]{1,0:T(2,128)S(1)}, u32[]{:S(2)}, u32[]{:S(2)}) collective-permute-start(f32[2,16]{1,0:T(2,128)S(1)} %collective-permute-done.84), channel_id=1, source_target_pairs={{0,128},{2,130},{4,132},{6,134},{8,136},{10,138},{12,140},{14,142}... | collective-permute-start | bytes 392 | tf_op jit(solution)/shard_map/ppermute | solution.py:18
  630.9 15.8 %collective-permute-start.94 = (f32[2,32]{1,0:T(2,128)S(1)}, f32[2,32]{1,0:T(2,128)S(1)}, u32[]{:S(2)}, u32[]{:S(2)}) collective-permute-start(f32[2,32]{1,0:T(2,128)S(1)} %collective-permute-done.93), channel_id=1, source_target_pairs={{0,32},{2,34},{4,36},{6,38},{8,40},{10,42},{12,44},{14,46},{16,48}... | collective-permute-start | bytes 776 | tf_op jit(solution)/shard_map/ppermute | solution.py:18
  633.6 36.6 %collective-permute-start.97 = (f32[2,32,1]{2,1,0:T(8,128)S(1)}, f32[2,32,1]{2,1,0:T(8,128)S(1)}, u32[]{:S(2)}, u32[]{:S(2)}) collective-permute-start(f32[2,32,1]{2,1,0:T(8,128)S(1)} %get-tuple-element.38), channel_id=1, source_target_pairs={{1,0},{0,1},{3,2},{2,3},{5,4},{4,5},{7,6},{6,7},{9,8},{8,9},{11,10... | collective-permute-start | bytes 776 | tf_op jit(solution)/shard_map/ppermute | solution.py:30
  644.8 18.8 %collective-permute-start.98 = (f32[2,32,1]{2,1,0:T(8,128)S(1)}, f32[2,32,1]{2,1,0:T(8,128)S(1)}, u32[]{:S(2)}, u32[]{:S(2)}) collective-permute-start(f32[2,32,1]{2,1,0:T(8,128)S(1)} %get-tuple-element.36), channel_id=1, source_target_pairs={{0,1},{1,0},{2,3},{3,2},{4,5},{5,4},{6,7},{7,6},{8,9},{9,8},{10,11... | collective-permute-start | bytes 776 | tf_op jit(solution)/shard_map/ppermute | solution.py:29
  650.6 19.6 %collective-permute-start.88 = (f32[2,1,1536]{2,0,1:T(2,128)S(1)}, f32[2,1,1536]{2,0,1:T(2,128)S(1)}, u32[]{:S(2)}, u32[]{:S(2)}) collective-permute-start(f32[2,1,1536]{2,0,1:T(2,128)S(1)} %copy.579), channel_id=1, source_target_pairs={{2,0},{4,2},{6,4},{8,6},{10,8},{12,10},{14,12},{16,14},{18,16},{20... | collective-permute-start | bytes 36872 | tf_op jit(solution)/shard_map/ppermute | solution.py:30
  654.9 15.3 %collective-permute-start.89 = (f32[2,1,1536]{2,0,1:T(2,128)S(1)}, f32[2,1,1536]{2,0,1:T(2,128)S(1)}, u32[]{:S(2)}, u32[]{:S(2)}) collective-permute-start(f32[2,1,1536]{2,0,1:T(2,128)S(1)} %copy.581), channel_id=1, source_target_pairs={{0,2},{2,4},{4,6},{6,8},{8,10},{10,12},{12,14},{14,16},{16,18},{18... | collective-permute-start | bytes 36872 | tf_op jit(solution)/shard_map/ppermute | solution.py:29
  656.9 13.1 %collective-permute-start.96 = (f32[2,32]{1,0:T(2,128)S(1)}, f32[2,32]{1,0:T(2,128)S(1)}, u32[]{:S(2)}, u32[]{:S(2)}) collective-permute-start(f32[2,32]{1,0:T(2,128)S(1)} %collective-permute-done.95), channel_id=1, source_target_pairs={{0,128},{2,130},{4,132},{6,134},{8,136},{10,138},{12,140},{14,142}... | collective-permute-start | bytes 776 | tf_op jit(solution)/shard_map/ppermute | solution.py:18
  (88 other events, 4121.0 us)
where the time goes:
time: 678 us; the launch traced here: 672 us
  starting transfers between devices  413 us (61%)
  waiting for transfers between devices  178 us (26%)
  local copies, waits for them, and re-layouts  67.3 us (10%)
  other arithmetic  8.82 us (1%)
    ppermute x63, starting transfers between devices, swapped(): lax.ppermute(value, axis, [(i, i ^ 1 << bit) for i in range(lax.axis_size...  185 us
    ppermute x63, waiting for transfers between devices, swapped(): lax.ppermute(value, axis, [(i, i ^ 1 << bit) for i in range(lax.axis_size...  178 us
    ppermute x18, starting transfers between devices, padded_2(): lax.ppermute(first, axis, [(b, a) for a, b in up])  131 us
    ppermute x18, starting transfers between devices, padded_2(): lax.ppermute(last, axis, up)  96.2 us
  transfers between devices with their start and end apart: 99, of which 44 were waited for; matrix products, arithmetic and copies ran while one was open for 2% of the time, Pallas kernels for 0%

commit v1 on v0

v1 whole, which is shorter than its diff:
```python
import functools

import jax
import jax.numpy as jnp
from jax import lax
from jax.experimental import pallas as pl
from jax.experimental.pallas import tpu as pltpu
from jax.sharding import PartitionSpec as P

TILE = 128
LEVELS = 4
LANES = 128
SEGS = 4
HALF = LANES // 2
GROUP = 8

relax_weight = 0.8
land_mass = 4.0
f32 = jnp.float32
exact = lax.Precision.HIGHEST


def iota(shape, axis):
    return lax.broadcasted_iota(jnp.int32, shape, axis)


def prepare_kernel(
    ice_ref, forcing_ref, visc_ref, mass_ref, land_ref, cor_ref, packed_ref, edge_ref, mirror_ref, wall_ref
):
    width = visc_ref.shape[0]
    tiles = visc_ref.shape[1] // LANES
    tps = tiles // SEGS
    tile_x = lax.axis_index("gx") * width // TILE
    tile_y = lax.axis_index("gy") * tiles
    lane = iota((8, LANES), 1)
    for i in range(width // 8):
        rows = slice(8 * i, 8 * i + 8)
        ends = []
        for t in range(tiles):
            s, k = divmod(t, tps)
            cols = slice(t * LANES, (t + 1) * LANES)
            ice = ice_ref[tile_x, tile_y + t].astype(f32)
            land = land_ref[rows, cols].astype(f32)
            ocean = 1.0 - land
            values = (
                visc_ref[rows, cols] * ice * ocean,
                mass_ref[rows, cols] * ocean + land_mass * land,
                forcing_ref[0, rows, cols] * ocean,
                forcing_ref[1, rows, cols] * ocean,
            )
            for a, value in enumerate(values):
                tile = 8 * i * 2 * tps + (a // 2) * tps + k
                start = tile * 8 + (a % 2) * SEGS + s
                packed_ref[pl.ds(start, 8, stride=2 * tps * 8), :] = value
            if t in (0, tiles - 1):
                ends.append(values)
        for a in range(4):
            start = 8 * i * 4 + a
            edge_ref[pl.ds(start, 8, stride=4), :] = jnp.where(lane < HALF, ends[0][a], ends[1][a])
            if a == 0:
                wall = jnp.broadcast_to(ends[0][0][:, :1], (8, LANES))
            else:
                wall = jnp.full((8, LANES), 1.0 if a == 1 else 0.0, f32)
            wall_ref[pl.ds(start, 8, stride=4), :] = wall
    main = 4 * width
    first, last = cor_ref[0:1, :], cor_ref[tiles - 1 : tiles, :]
    edge_ref[main : main + 8, :] = jnp.broadcast_to(
        jnp.where(lane[:1] < HALF, first, last), (8, LANES)
    )
    wall_ref[main : main + 8, :] = jnp.zeros((8, LANES), f32)
    flip = (iota((LANES, LANES), 0) + iota((LANES, LANES), 1) == LANES - 1).astype(f32)
    row, col = iota((main, main), 0), iota((main, main), 1)
    sign = jnp.where(row & 2 == 0, 1.0, -1.0)
    turn = jnp.where((row & 3 == col & 3) & ((row >> 2) + (col >> 2) == width - 1), sign, 0.0)
    turned = jnp.dot(turn, edge_ref[0:main, :], precision=exact, preferred_element_type=f32)
    mirror_ref[0:main, :] = jnp.dot(turned, flip, precision=exact, preferred_element_type=f32)
    mirror_ref[main : main + 8, :] = jnp.dot(
        edge_ref[main : main + 8, :], flip, precision=exact, preferred_element_type=f32
    )


def solve_kernel(own_ref, left_ref, right_ref, cor_ref, out_ref, *scratch):
    packed, sems, flat = scratch[:3]
    store = scratch[3:]
    size = own_ref.shape[0]
    width = out_ref.shape[1]
    tiles = cor_ref.shape[0]
    tps = tiles // SEGS
    span = (tps + 1) * LANES
    shape = (8, span)
    copies = [
        pltpu.make_async_copy(ref, packed.at[pl.ds(n * size, size), :], sems.at[n])
        for n, ref in enumerate((left_ref, own_ref, right_ref))
    ]
    for copy in copies:
        copy.start()

    sub1, lane1 = iota((8, LANES), 0), iota((8, LANES), 1)
    low = sub1 < SEGS
    at_north = (sub1 & (SEGS - 1) == SEGS - 1) & (lane1 < HALF)
    at_south = (sub1 & (SEGS - 1) == 0) & (lane1 >= HALF)
    outer = at_north | at_south
    lane = iota(shape, 1)
    bottom = lax.axis_index("gy") == 0
    wall = (iota(shape, 0) & (SEGS - 1) == 0) & (lane >= tps * LANES + HALF) & bottom
    weight = jnp.where(wall, 0.0, relax_weight)

    def roll(value, shift):
        return pltpu.roll(value, shift % span, 1)

    def other(value):
        return pltpu.roll(value, SEGS, 0)

    def pair(value, step, odd):
        return value + jnp.where(odd, roll(value, step), roll(value, -step))

    def with_halo(parts, outside):
        inside = jnp.where(lane1 < HALF, pltpu.roll(parts[0], 7, 0), pltpu.roll(parts[-1], 1, 0))
        return parts + [jnp.where(outer, outside, inside)]

    for copy in copies:
        copy.wait()

    names = ("visc", "north", "mass", "right", "east", "scale", "field", "done")
    levels = []
    place = 0
    for level in range(LEVELS):
        levels.append(dict(zip(names, store[place : place + len(names)])))
        place += len(names)

    line = packed[pl.ds(size + size - 8, 8), :][:1]
    parts = [cor_ref[pl.ds(k, SEGS, stride=tps), :] for k in range(tps)]
    parts = [jnp.concatenate([part, -part], 0) for part in parts]
    line8 = jnp.where(low, jnp.broadcast_to(line, (8, LANES)), -jnp.broadcast_to(line, (8, LANES)))
    rotation = jnp.concatenate(with_halo(parts, line8), 1)

    top = levels[0]

    def unpack(group, carry):
        for j in range(GROUP):
            x = group * GROUP + j
            third = group * GROUP // width
            xi = x - third * width
            base = pl.multiple_of(third * size + xi * (2 * tps * 8), 8)
            if j % 2 == 0:
                ext = packed[pl.ds(pl.multiple_of(third * size + width * 2 * tps * 8 + xi * 4, 8), 8), :]
            rows = [
                jnp.broadcast_to(ext[(j % 2) * 4 + a : (j % 2) * 4 + a + 1], (8, LANES)) for a in range(4)
            ]
            both = with_halo(
                [packed[pl.ds(base + 8 * k, 8), :] for k in range(tps)], jnp.where(low, rows[0], rows[1])
            )
            turned = [other(part) for part in both]
            visc = jnp.concatenate([jnp.where(low, a, b) for a, b in zip(both, turned)], 1)
            mass = jnp.concatenate([jnp.where(low, b, a) for a, b in zip(both, turned)], 1)
            right = jnp.concatenate(
                with_halo(
                    [packed[pl.ds(base + 8 * (tps + k), 8), :] for k in range(tps)],
                    jnp.where(low, rows[2], rows[3]),
                ),
                1,
            )
            top["visc"][x + 1] = visc
            top["mass"][x] = mass
            top["right"][x] = right
            top["north"][x] = 0.5 * (visc + roll(visc, -1))
        return carry

    lax.fori_loop(0, 3 * width // GROUP, unpack, 0)

    def loop(count, body):
        group = GROUP
        while count % group:
            group //= 2
        if count == group:
            body(0, group)
        else:
            lax.fori_loop(0, count // group, lambda g, c: (body(g * group, group), c)[1], 0)

    rotations = []
    for level in range(LEVELS):
        now = levels[level]
        step = 1 << level
        count = 3 * width >> level
        rotations.append(rotation)

        def coefficients(first, group, now=now, step=step, level=level):
            if level == 0:
                visc = [now["visc"][first + j] for j in range(group + 2)]
                east = [0.5 * (visc[j] + visc[j + 1]) for j in range(group + 1)]
                for j in range(group):
                    now["east"][first + j + 1] = east[j + 1]
            else:
                east = [now["east"][first + j] for j in range(group + 1)]
            for j in range(group):
                x = first + j
                north = now["north"][x]
                diag = now["mass"][x] + east[j + 1] + east[j] + north + roll(north, step)
                scale = weight / diag
                now["scale"][x] = scale
                now["field"][x + 1] = scale * now["right"][x]

        loop(count, coefficients)
        if level == LEVELS - 1:
            break
        coarse = levels[level + 1]
        odd = lane & step != 0

        def restrict(first, group, now=now, coarse=coarse, step=step, odd=odd, rotation=rotation):
            first = first * 2
            field = [now["field"][first + j] for j in range(2 * group + 2)]
            east = [now["east"][first + j] for j in range(2 * group + 1)]
            rest = []
            for j in range(2 * group):
                x = first + j
                north = now["north"][x]
                w = field[j + 1]
                rest.append(
                    (1.0 - relax_weight) * now["right"][x]
                    + east[j + 1] * field[j + 2]
                    + east[j] * field[j]
                    + north * roll(w, -step)
                    + roll(north * w, step)
                    + rotation * other(w)
                )
            for j in range(group):
                half = first // 2 + j
                x = first + 2 * j
                coarse["right"][half] = 0.25 * pair(rest[2 * j] + rest[2 * j + 1], step, odd)
                coarse["east"][half + 1] = 0.25 * pair(east[2 * j + 2], step, odd)
                coarse["mass"][half] = 0.25 * pair(now["mass"][x] + now["mass"][x + 1], step, odd)
                north = now["north"][x] + now["north"][x + 1]
                coarse["north"][half] = 0.25 * jnp.where(odd, north, roll(north, -step))

        loop(count // 2, restrict)
        rotation = 0.5 * pair(rotation, step, odd)

    def sweep(level, first, group, value, target, offset):
        now = levels[level]
        step = 1 << level
        field = [value(first + j - 1) for j in range(group + 2)]
        east = [now["east"][first + j] for j in range(group + 1)]
        for j in range(group):
            x = first + j
            north = now["north"][x]
            w = field[j + 1]
            around = (
                now["right"][x]
                + east[j + 1] * field[j + 2]
                + east[j] * field[j]
                + north * roll(w, -step)
                + roll(north * w, step)
                + rotations[level] * other(w)
            )
            result = (1.0 - relax_weight) * w + now["scale"][x] * around
            if target is None:
                for k in range(tps):
                    row = pl.multiple_of(((x - offset) * tps + k) * 8, 8)
                    flat[pl.ds(row, 8), :] = result[:, k * LANES : (k + 1) * LANES]
            else:
                target[x + 1] = result

    last = levels[-1]
    own = width >> (LEVELS - 1)
    sweep(LEVELS - 1, own - 2, own + 4, lambda x: last["field"][x + 1], last["done"], 0)
    sweep(LEVELS - 1, own - 1, own + 2, lambda x: last["done"][x + 1], last["field"], 0)
    solved = last["field"]
    for level in reversed(range(LEVELS - 1)):
        now = levels[level]
        own = width >> level

        def value(x, now=now, solved=solved):
            return now["field"][x + 1] + solved[lax.div(x, 2) + 1]

        if level > 0:
            start, count, target = own - 1, own + 2, now["done"]
        else:
            start, count, target = own, own, None
        loop(
            count,
            lambda first, group, level=level, start=start, value=value, target=target: sweep(
                level, start + first, group, value, target, start
            ),
        )
        solved = now["done"]

    for c in range(2):
        for i in range(width // 8):
            for t in range(tiles):
                s, k = divmod(t, tps)
                row = (8 * i * tps + k) * 8 + c * SEGS + s
                out_ref[c, 8 * i : 8 * i + 8, t * LANES : (t + 1) * LANES] = flat[
                    pl.ds(row, 8, stride=tps * 8), :
                ]


def local(forcing, viscosity, mass, coriolis, land, ice_tiles):
    width, height = viscosity.shape
    tiles = height // LANES
    tps = tiles // SEGS
    main = width * 2 * tps * 8
    outside = 4 * width + 8
    gx, gy = lax.axis_size("gx"), lax.axis_size("gy")
    is_top = lax.axis_index("gy") == gy - 1
    lines = coriolis.reshape(tiles, LANES)
    vmem = pl.BlockSpec(memory_space=pltpu.VMEM)
    anywhere = pl.BlockSpec(memory_space=pl.ANY)

    packed, edge, mirror, wall = pl.pallas_call(
        prepare_kernel,
        out_shape=(
            jax.ShapeDtypeStruct((main + outside, LANES), f32),
            jax.ShapeDtypeStruct((outside, LANES), f32),
            jax.ShapeDtypeStruct((outside, LANES), f32),
            jax.ShapeDtypeStruct((outside, LANES), f32),
        ),
        in_specs=[pl.BlockSpec(memory_space=pltpu.SMEM)] + [vmem] * 5,
        out_specs=(vmem,) * 4,
    )(ice_tiles, forcing, viscosity, mass, land, lines)

    top = gy - 1
    swap = lax.ppermute(edge, "gy", [(i, gy - 1 - i) for i in range(gy)])
    folded = lax.ppermute(
        mirror, ("gx", "gy"), [(i * gy + top, (gx - 1 - i) * gy + top) for i in range(gx)]
    )
    north = iota((outside, LANES), 1) < HALF
    beyond = jnp.where(north, jnp.where(is_top, folded, swap), jnp.where(is_top, swap, wall))
    packed = lax.dynamic_update_slice(packed, beyond, (main, 0))
    up = [(i, (i + 1) % gx) for i in range(gx)]
    from_left = lax.ppermute(packed, "gx", up)
    from_right = lax.ppermute(packed, "gx", [(b, a) for a, b in up])

    store = []
    for level in range(LEVELS):
        columns = (3 * width >> level) + 2
        store += [pltpu.VMEM((columns, 8, (tps + 1) * LANES), f32)] * 8
    return pl.pallas_call(
        solve_kernel,
        out_shape=jax.ShapeDtypeStruct((2, width, height), f32),
        in_specs=[anywhere] * 3 + [vmem],
        out_specs=vmem,
        scratch_shapes=[
            pltpu.VMEM((3 * (main + outside), LANES), f32),
            pltpu.SemaphoreType.DMA((3,)),
            pltpu.VMEM((width * tps * 8, LANES), f32),
        ]
        + store,
        compiler_params=pltpu.CompilerParams(vmem_limit_bytes=48 * 1024 * 1024),
    )(packed, from_left, from_right, lines)


def solution(mesh):
    return jax.shard_map(
        local,
        mesh=mesh,
        in_specs=(
            P(None, ("groups", "gx"), "gy"),
            P(("groups", "gx"), "gy"),
            P(("groups", "gx"), "gy"),
            P("gy"),
            P("gx", "gy"),
            P("groups", None),
        ),
        out_specs=P(None, ("groups", "gx"), "gy"),
        check_vma=False,
    )
```

time: 678 us -> 99.8 us (0.15)
  starting transfers between devices: 413 us -> 56.9 us
  waiting for transfers between devices: 178 us -> 24.2 us
  local copies, waits for them, and re-layouts: 67.3 us -> 2.55 us
  Pallas kernels: 0 us -> 15.1 us
  other arithmetic: 8.82 us -> 0.65 us
    ppermute x99 -> x4, starting transfers between devices: 413 us -> 56.9 us  [the longest x1 47.8 us: local(): lax.ppermute(mirror, ('gx', 'gy'), [(i * gy + top, (gx - 1 - i) * gy + to...]
    ppermute x99 -> x4, waiting for transfers between devices: 178 us -> 24.2 us  [the longest x1 15.4 us: local(): from_right = lax.ppermute(packed, 'gx', [(b, a) for a, b in up])]
    slice x88 -> x0, local copies, waits for them, and re-layouts: 62.1 us -> none  [the longest x6 7.68 us: pair_mean(): values[..., 1::2, 1::2]]
    pallas_call x0 -> x2, Pallas kernels: none -> 15.1 us  [the longest x1 12.5 us: local(): pl.pallas_call(solve_kernel, out_shape=jax.ShapeDtypeStruct((2, width, he...]
  transfers between devices with their start and end apart: 99 -> 4, of which waited for: 44 -> 3; matrix products, arithmetic and copies ran while one was open for 2% -> 0% of each run, Pallas kernels for 0% -> 0%
where the time goes in v1:
time: 99.8 us; the launch traced here: 99.5 us
  starting transfers between devices  56.9 us (57%)
  waiting for transfers between devices  24.2 us (24%)
  Pallas kernels  15.1 us (15%)
  local copies, waits for them, and re-layouts  2.55 us (3%)
    ppermute x1, starting transfers between devices, local(): lax.ppermute(mirror, ('gx', 'gy'), [(i * gy + top, (gx - 1 - i) * gy + to...  47.8 us
    ppermute x1, waiting for transfers between devices, local(): from_right = lax.ppermute(packed, 'gx', [(b, a) for a, b in up])  15.4 us
    pallas_call x1, Pallas kernels, local(): pl.pallas_call(solve_kernel, out_shape=jax.ShapeDtypeStruct((2, width, he...  12.5 us
    ppermute x1, waiting for transfers between devices, local(): from_left = lax.ppermute(packed, 'gx', up)  7.35 us
    ppermute x1, starting transfers between devices, local(): from_right = lax.ppermute(packed, 'gx', [(b, a) for a, b in up])  5.2 us
    pallas_call x1, Pallas kernels, local(): pl.pallas_call(prepare_kernel, out_shape=(jax.ShapeDtypeStruct((main + ou...  2.56 us
    unnamed x5, local copies, waits for them, and re-layouts  2.55 us
  transfers between devices with their start and end apart: 4, of which 3 were waited for; matrix products, arithmetic and copies ran while one was open for 0% of the time, Pallas kernels for 0%

profile of v1, /device:TPU:65, one launch (start us, length us, event | category | flops | bytes accessed | tf_op | source)
XLA Modules:
  0.0 99.5 jit_solution(7104963544116793238)
XLA Ops:
  0.0 1.4 %copy.7.ice_ref = s32[32,24]{1,0:T(8,128)} copy(s32[32,24]{0,1:T(8,128)} %param.11) | data formatting | bytes 6144 | tf_op args[5]
  1.4 2.6 %shard_map.64 = (f32[1672,128]{1,0:T(8,128)}, f32[136,128]{1,0:T(8,128)}, f32[136,128]{1,0:T(8,128)}, f32[136,128]{1,0:T(8,128)}) custom-call(s32[32,24]{1,0:T(8,128)} %copy.7.ice_ref, f32[2,32,1536]{2,1,0:T(8,128)} %forcing_ref.1, f32[32,1536]{1,0:T(8,128)} %visc_ref.1, f32[32,1536]{1,0:T(8,128)} %mass_ref.1, s32[32,1536]{1,0:T(8,128)} %land_ref.1, ...), custom_call_target="tpu_custom_call" | custom-call | tf_op jit(solution)/shard_map/pallas_call | solution.py:309
  3.9 47.8 %collective-permute-start = (f32[136,128]{1,0:T(8,128)}, f32[136,128]{1,0:T(8,128)S(1)}, u32[]{:S(2)}, u32[]{:S(2)}) collective-permute-start(f32[136,128]{1,0:T(8,128)} %get-tuple-element.10), channel_id=1, source_target_pairs={{1,255},{3,253},{5,251},{7,249},{9,247},{11,245},{13,243},{15,241}... | collective-permute-start | bytes 208904 | tf_op jit(solution)/shard_map/ppermute | solution.py:323
  51.8 2.0 %collective-permute-start.1 = (f32[136,128]{1,0:T(8,128)}, f32[136,128]{1,0:T(8,128)S(1)}, u32[]{:S(2)}, u32[]{:S(2)}) collective-permute-start(f32[136,128]{1,0:T(8,128)} %get-tuple-element.11), channel_id=1, source_target_pairs={{0,1},{1,0},{2,3},{3,2},{4,5},{5,4},{6,7},{7,6},{8,9},{9,8},{10,11... | collective-permute-start | bytes 208904 | tf_op jit(solution)/shard_map/ppermute | solution.py:322
  53.7 0.0 collective-permute-done
  53.7 1.4 %collective-permute-done.1 = f32[136,128]{1,0:T(8,128)S(1)} collective-permute-done((f32[136,128]{1,0:T(8,128)}, f32[136,128]{1,0:T(8,128)S(1)}, u32[]{:S(2)}, u32[]{:S(2)}) %collective-permute-start.1) | collective-permute-done | bytes 69664 | tf_op jit(solution)/shard_map/ppermute | solution.py:322
  55.2 0.0 copy-start.1
  55.2 0.6 select_dynamic-update-slice_fusion.own_ref
  55.8 5.2 %collective-permute-start.3 = (f32[1672,128]{1,0:T(8,128)}, f32[1672,128]{1,0:T(8,128)S(1)}, u32[]{:S(2)}, u32[]{:S(2)}) collective-permute-start(f32[1672,128]{1,0:T(8,128)} %select_dynamic-update-slice_fusion.own_ref), channel_id=1, source_target_pairs={{2,0},{4,2},{6,4},{8,6},{10,8},{12,10},{14,12},{16,14},{18,16},{20... | collective-permute-start | bytes 2568200 | tf_op jit(solution)/shard_map/ppermute | solution.py:331
  61.0 2.0 %collective-permute-start.2 = (f32[1672,128]{1,0:T(8,128)}, f32[1672,128]{1,0:T(8,128)S(1)}, u32[]{:S(2)}, u32[]{:S(2)}) collective-permute-start(f32[1672,128]{1,0:T(8,128)} %select_dynamic-update-slice_fusion.own_ref), channel_id=1, source_target_pairs={{0,2},{2,4},{4,6},{6,8},{8,10},{10,12},{12,14},{14,16},{16,18},{18... | collective-permute-start | bytes 2568200 | tf_op jit(solution)/shard_map/ppermute | solution.py:330
  63.0 15.4 %collective-permute-done.3.right_ref = f32[1672,128]{1,0:T(8,128)S(1)} collective-permute-done((f32[1672,128]{1,0:T(8,128)}, f32[1672,128]{1,0:T(8,128)S(1)}, u32[]{:S(2)}, u32[]{:S(2)}) %collective-permute-start.3) | collective-permute-done | bytes 856096 | tf_op jit(solution)/shard_map/ppermute | solution.py:331
  78.4 7.3 %collective-permute-done.2.left_ref = f32[1672,128]{1,0:T(8,128)S(1)} collective-permute-done((f32[1672,128]{1,0:T(8,128)}, f32[1672,128]{1,0:T(8,128)S(1)}, u32[]{:S(2)}, u32[]{:S(2)}) %collective-permute-start.2) | collective-permute-done | bytes 856096 | tf_op jit(solution)/shard_map/ppermute | solution.py:330
  85.7 0.0 copy-done.1
  85.7 0.0 copy-start
  85.7 1.2 %copy-done = f32[1672,128]{1,0:T(8,128)S(1)} copy-done((f32[1672,128]{1,0:T(8,128)S(1)}, f32[1672,128]{1,0:T(8,128)}, u32[]{:S(2)}) %copy-start) | copy-done | bytes 856088
  86.9 12.5 %shard_map.65 = f32[2,32,1536]{2,1,0:T(8,128)} custom-call(f32[1672,128]{1,0:T(8,128)S(1)} %copy-done, f32[1672,128]{1,0:T(8,128)S(1)} %collective-permute-done.2.left_ref, f32[1672,128]{1,0:T(8,128)S(1)} %collective-permute-done.3.right_ref, f32[12,128]{1,0:T(8,128)S(1)} %bitcast.2), custom_call_target="tpu_custom_call" | custom-call | tf_op jit(solution)/shard_map/pallas_call | solution.py:337
  (1 shorter events, 0.0 us)
Async XLA Ops:
  3.9 49.8 %collective-permute-start = (f32[136,128]{1,0:T(8,128)}, f32[136,128]{1,0:T(8,128)S(1)}, u32[]{:S(2)}, u32[]{:S(2)}) collective-permute-start(f32[136,128]{1,0:T(8,128)} %get-tuple-element.10), channel_id=1, source_target_pairs={{1,255},{3,253},{5,251},{7,249},{9,247},{11,245},{13,243},{15,241}... | collective-permute-start | bytes 208904 | tf_op jit(solution)/shard_map/ppermute | solution.py:323
  51.8 3.4 %collective-permute-start.1 = (f32[136,128]{1,0:T(8,128)}, f32[136,128]{1,0:T(8,128)S(1)}, u32[]{:S(2)}, u32[]{:S(2)}) collective-permute-start(f32[136,128]{1,0:T(8,128)} %get-tuple-element.11), channel_id=1, source_target_pairs={{0,1},{1,0},{2,3},{3,2},{4,5},{5,4},{6,7},{7,6},{8,9},{9,8},{10,11... | collective-permute-start | bytes 208904 | tf_op jit(solution)/shard_map/ppermute | solution.py:322
  55.2 30.6 %copy-start.1 = (f32[1536]{0:T(1024)S(1)}, f32[1536]{0:T(1024)}, u32[]{:S(2)}) copy-start(f32[1536]{0:T(1024)} %param.9) | copy-start | bytes 18436
  55.8 22.6 %collective-permute-start.3 = (f32[1672,128]{1,0:T(8,128)}, f32[1672,128]{1,0:T(8,128)S(1)}, u32[]{:S(2)}, u32[]{:S(2)}) collective-permute-start(f32[1672,128]{1,0:T(8,128)} %select_dynamic-update-slice_fusion.own_ref), channel_id=1, source_target_pairs={{2,0},{4,2},{6,4},{8,6},{10,8},{12,10},{14,12},{16,14},{18,16},{20... | collective-permute-start | bytes 2568200 | tf_op jit(solution)/shard_map/ppermute | solution.py:331
  61.0 24.7 %collective-permute-start.2 = (f32[1672,128]{1,0:T(8,128)}, f32[1672,128]{1,0:T(8,128)S(1)}, u32[]{:S(2)}, u32[]{:S(2)}) collective-permute-start(f32[1672,128]{1,0:T(8,128)} %select_dynamic-update-slice_fusion.own_ref), channel_id=1, source_target_pairs={{0,2},{2,4},{4,6},{6,8},{8,10},{10,12},{12,14},{14,16},{16,18},{18... | collective-permute-start | bytes 2568200 | tf_op jit(solution)/shard_map/ppermute | solution.py:330
  85.7 1.2 %copy-start = (f32[1672,128]{1,0:T(8,128)S(1)}, f32[1672,128]{1,0:T(8,128)}, u32[]{:S(2)}) copy-start(f32[1672,128]{1,0:T(8,128)} %select_dynamic-update-slice_fusion.own_ref) | copy-start | bytes 2568196

commit v2 on v0

v2 whole, which is shorter than its diff:
```python
import functools

import jax
import jax.numpy as jnp
from jax import lax
from jax.experimental import pallas as pl
from jax.experimental.pallas import tpu as pltpu
from jax.sharding import PartitionSpec as P

TILE = 128
LEVELS = 4
LANES = 128
SEGS = 4
HALF = LANES // 2
GROUP = 8

relax_weight = 0.8
land_mass = 4.0
f32 = jnp.float32
exact = lax.Precision.HIGHEST


FINE = 6
SPLIT = 2


def iota(shape, axis):
    return lax.broadcasted_iota(jnp.int32, shape, axis)


def prepare_kernel(
    ice_ref, forcing_ref, visc_ref, mass_ref, land_ref, cor_ref,
    packed_ref, lowest_ref, highest_ref, edge_ref, mirror_ref, wall_ref,
):
    width = visc_ref.shape[0]
    tiles = visc_ref.shape[1] // LANES
    tps = tiles // SEGS
    tile_x = lax.axis_index("gx") * width // TILE
    tile_y = lax.axis_index("gy") * tiles
    lane = iota((8, LANES), 1)
    for i in range(width // 8):
        rows = slice(8 * i, 8 * i + 8)
        ends = []
        for t in range(tiles):
            s, k = divmod(t, tps)
            cols = slice(t * LANES, (t + 1) * LANES)
            ice = ice_ref[tile_y + t, tile_x].astype(f32)
            land = land_ref[rows, cols].astype(f32)
            ocean = 1.0 - land
            values = (
                visc_ref[rows, cols] * ice * ocean,
                mass_ref[rows, cols] * ocean + land_mass * land,
                forcing_ref[0, rows, cols] * ocean,
                forcing_ref[1, rows, cols] * ocean,
            )
            for a, value in enumerate(values):
                tile = 8 * i * 2 * tps + (a // 2) * tps + k
                start = tile * 8 + (a % 2) * SEGS + s
                packed_ref[pl.ds(start, 8, stride=2 * tps * 8), :] = value
            if t in (0, tiles - 1):
                ends.append(values)
        for a in range(4):
            start = 8 * i * 4 + a
            edge_ref[pl.ds(start, 8, stride=4), :] = jnp.where(lane < HALF, ends[0][a], ends[1][a])
            if a == 0:
                wall = jnp.broadcast_to(ends[0][0][:, :1], (8, LANES))
            else:
                wall = jnp.full((8, LANES), 1.0 if a == 1 else 0.0, f32)
            wall_ref[pl.ds(start, 8, stride=4), :] = wall
    side = FINE * 2 * tps * 8
    lowest_ref[...] = packed_ref[0:side, :]
    highest_ref[...] = packed_ref[width * 2 * tps * 8 - side : width * 2 * tps * 8, :]
    main = 4 * width
    first, last = cor_ref[0:1, :], cor_ref[tiles - 1 : tiles, :]
    edge_ref[main : main + 8, :] = jnp.broadcast_to(
        jnp.where(lane[:1] < HALF, first, last), (8, LANES)
    )
    wall_ref[main : main + 8, :] = jnp.zeros((8, LANES), f32)
    flip = (iota((LANES, LANES), 0) + iota((LANES, LANES), 1) == LANES - 1).astype(f32)
    row, col = iota((main, main), 0), iota((main, main), 1)
    sign = jnp.where(row & 2 == 0, 1.0, -1.0)
    turn = jnp.where((row & 3 == col & 3) & ((row >> 2) + (col >> 2) == width - 1), sign, 0.0)
    turned = jnp.dot(turn, edge_ref[0:main, :], precision=exact, preferred_element_type=f32)
    mirror_ref[0:main, :] = jnp.dot(turned, flip, precision=exact, preferred_element_type=f32)
    mirror_ref[main : main + 8, :] = jnp.dot(
        edge_ref[main : main + 8, :], flip, precision=exact, preferred_element_type=f32
    )


def edge_kernel(swap_ref, folded_ref, wall_ref, lowest_ref, highest_ref, ext_ref, low_ref, high_ref):
    is_top = lax.axis_index("gy") == lax.axis_size("gy") - 1
    north = iota(swap_ref.shape, 1) < HALF
    swap = swap_ref[...]
    beyond = jnp.where(
        north, jnp.where(is_top, folded_ref[...], swap), jnp.where(is_top, swap, wall_ref[...])
    )
    ext_ref[...] = beyond
    side = lowest_ref.shape[0]
    main = swap_ref.shape[0] - 8
    low_ref[0:side, :] = lowest_ref[...]
    low_ref[side : side + 4 * FINE, :] = ext_ref[0 : 4 * FINE, :]
    high_ref[0:side, :] = highest_ref[...]
    high_ref[side : side + 4 * FINE, :] = ext_ref[main - 4 * FINE : main, :]


class Shifts:
    def __init__(self, tps):
        self.tps = tps
        self.span = (tps + 1) * LANES
        self.shape = (8, self.span)
        self.lane = iota(self.shape, 1)
        lane = iota((8, LANES), 1)
        row = iota((8, LANES), 0) & (SEGS - 1)
        self.first_half = lane < HALF
        self.low = iota((8, LANES), 0) < SEGS
        self.outer = ((row == SEGS - 1) & (lane < HALF)) | ((row == 0) & (lane >= HALF))
        bottom = lax.axis_index("gy") == 0
        wall = (iota(self.shape, 0) & (SEGS - 1) == 0) & (self.lane >= tps * LANES + HALF) & bottom
        self.weight = jnp.where(wall, 0.0, relax_weight)

    def roll(self, value, shift):
        return pltpu.roll(value, shift % self.span, 1)

    def odd(self, step):
        return self.lane & step != 0

    def pair(self, value, step):
        return value + jnp.where(self.odd(step), self.roll(value, step), self.roll(value, -step))

    def with_halo(self, parts, outside):
        inside = jnp.where(self.first_half, pltpu.roll(parts[0], 7, 0), pltpu.roll(parts[-1], 1, 0))
        return parts + [jnp.where(self.outer, outside, inside)]

    def rotations(self, cor_ref, line):
        parts = [cor_ref[pl.ds(k, SEGS, stride=self.tps), :] for k in range(self.tps)]
        parts = [jnp.concatenate([part, -part], 0) for part in parts]
        line = jnp.broadcast_to(line, (8, LANES))
        rotation = jnp.concatenate(self.with_halo(parts, jnp.where(self.low, line, -line)), 1)
        result = []
        for level in range(LEVELS):
            result.append(rotation)
            rotation = 0.5 * self.pair(rotation, 1 << level)
        return result

    def around(self, now, x, field, east, rotation, step):
        north = now["north"][x]
        west_nb, w, east_nb = field
        return (
            east[1] * east_nb
            + east[0] * west_nb
            + north * self.roll(w, -step)
            + self.roll(north * w, step)
            + rotation * other(w)
        )

    def coefficients(self, now, first, group, step):
        east = [now["east"][first + j - 1] for j in range(group + 1)]
        for j in range(group):
            x = first + j
            north = now["north"][x]
            diag = now["mass"][x] + east[j + 1] + east[j] + north + self.roll(north, step)
            scale = self.weight / diag
            now["scale"][x] = scale
            now["field"][x] = scale * now["right"][x]

    def coarse_east(self, now, fine, target, step):
        target[...] = 0.25 * self.pair(now["east"][fine + 1], step)

    def coarse_sums(self, now, coarse, fine, place, step):
        north = now["north"][fine] + now["north"][fine + 1]
        coarse["north"][place] = 0.25 * jnp.where(self.odd(step), north, self.roll(north, -step))
        coarse["mass"][place] = 0.25 * self.pair(now["mass"][fine] + now["mass"][fine + 1], step)

    def restrict(self, now, coarse, fine, place, group, rotation, step):
        field = [now["field"][fine + j - 1] for j in range(2 * group + 2)]
        east = [now["east"][fine + j - 1] for j in range(2 * group + 1)]
        rest = [
            (1.0 - relax_weight) * now["right"][fine + j]
            + self.around(now, fine + j, field[j : j + 3], east[j : j + 2], rotation, step)
            for j in range(2 * group)
        ]
        for j in range(group):
            coarse["right"][place + j] = 0.25 * self.pair(rest[2 * j] + rest[2 * j + 1], step)

    def sweep(self, now, first, group, value, rotation, step, put):
        field = [value(first + j - 1) for j in range(group + 2)]
        east = [now["east"][first + j - 1] for j in range(group + 1)]
        for j in range(group):
            x = first + j
            near = now["right"][x] + self.around(
                now, x, field[j : j + 3], east[j : j + 2], rotation, step
            )
            put(x, (1.0 - relax_weight) * field[j + 1] + now["scale"][x] * near)


def other(value):
    return pltpu.roll(value, SEGS, 0)


def loop(start, count, body, group=GROUP):
    whole, rest = divmod(count, group)
    if whole == 1:
        body(start, group)
    elif whole:
        lax.fori_loop(0, whole, lambda g, c: (body(start + g * group, group), c)[1], 0)
    if rest:
        body(start + whole * group, rest)


FIRST = ("north", "east", "scale", "right", "field")
COARSE = ("right", "east", "north", "mass")


def first_kernel(own_ref, ext_ref, left_ref, right_ref, cor_ref, *refs):
    width = (ext_ref.shape[0] - 8) // 4
    tps = cor_ref.shape[0] // SEGS
    move = Shifts(tps)
    levels = [dict(zip(FIRST, refs[5 * n : 5 * n + 5])) for n in range(SPLIT)]
    sent_ref, rot_ref = refs[5 * SPLIT : 5 * SPLIT + 2]
    rest = list(refs[5 * SPLIT + 2 :])
    visc = rest.pop(0)
    for level in levels:
        level["mass"] = rest.pop(0)
    bottom = dict(zip(COARSE, rest))
    levels.append(bottom)
    main = ext_ref.shape[0] - 8
    rotations = move.rotations(cor_ref, ext_ref[main : main + 1, :])
    for level in range(LEVELS):
        rot_ref[level] = rotations[level]
    top = levels[0]

    def unpack(ref, base, ext, index, x):
        rows = [jnp.broadcast_to(ext[4 * index + a : 4 * index + a + 1], (8, LANES)) for a in range(4)]
        both = move.with_halo(
            [ref[pl.ds(base + 8 * k, 8), :] for k in range(tps)], jnp.where(move.low, rows[0], rows[1])
        )
        turned = [other(part) for part in both]
        value = jnp.concatenate([jnp.where(move.low, a, b) for a, b in zip(both, turned)], 1)
        visc[x] = value
        top["mass"][x] = jnp.concatenate([jnp.where(move.low, b, a) for a, b in zip(both, turned)], 1)
        top["right"][x] = jnp.concatenate(
            move.with_halo(
                [ref[pl.ds(base + 8 * (tps + k), 8), :] for k in range(tps)],
                jnp.where(move.low, rows[2], rows[3]),
            ),
            1,
        )
        top["north"][x] = 0.5 * (value + move.roll(value, -1))

    each = 2 * tps * 8
    for ref, start in ((left_ref, 0), (right_ref, FINE + width)):
        for j in range(0, FINE, 2):
            ext = ref[FINE * each + 4 * j : FINE * each + 4 * j + 8, :]
            for index in range(2):
                unpack(ref, (j + index) * each, ext, index, start + j + index)

    def own(first, group):
        for j in range(0, group, 2):
            x = first + j
            ext = ext_ref[pl.ds(pl.multiple_of(4 * x, 8), 8), :]
            for index in range(2):
                unpack(own_ref, pl.multiple_of((x + index) * each, 8), ext, index, FINE + x + index)

    loop(0, width, own)
    columns = 2 * FINE + width

    def faces(first, group):
        value = [visc[first + j] for j in range(group + 1)]
        for j in range(group):
            top["east"][first + j] = 0.5 * (value[j] + value[j + 1])

    loop(0, columns - 1, faces, 11)
    loop(1, columns - 2, lambda x, n: move.coefficients(top, x, n, 1), 7)
    half = columns // 2
    level1 = levels[1]

    def east1(first, group):
        for j in range(group):
            level1["east"][first + j] = 0.25 * move.pair(top["east"][2 * (first + j) + 1], 1)

    def sums1(first, group):
        for j in range(group):
            move.coarse_sums(top, level1, 2 * (first + j), first + j, 1)

    loop(0, half - 1, east1, 7)
    loop(0, half, sums1, 11)
    loop(1, half - 2, lambda x, n: move.restrict(top, level1, 2 * x, x, n, rotations[0], 1), 5)
    loop(1, half - 2, lambda x, n: move.coefficients(level1, x, n, 2), 10)
    count = width >> SPLIT
    skip = FINE // 2
    for k in range(count):
        bottom["east"][k] = 0.25 * move.pair(level1["east"][skip + 2 * k + 1], 2)
        move.coarse_sums(level1, bottom, skip + 2 * k, k, 2)
    move.restrict(level1, bottom, skip, 0, count, rotations[1], 2)
    bit0, bit1 = move.odd(1), move.odd(2)
    for k in range(count):
        parts = [bottom[name][k] for name in COARSE]
        sent_ref[k] = jnp.where(
            bit1, jnp.where(bit0, parts[3], parts[2]), jnp.where(bit0, parts[1], parts[0])
        )


SECOND = ("right", "east", "north", "mass", "scale", "field")


def second_kernel(own_ref, left_ref, right_ref, rot_ref, *refs):
    out_refs = 5 * SPLIT
    levels = [dict(zip(FIRST, refs[5 * n : 5 * n + 5])) for n in range(SPLIT)]
    out_ref = refs[out_refs]
    rest = list(refs[out_refs + 1 :])
    flat = rest.pop(0)
    for _ in range(SPLIT, LEVELS):
        levels.append(dict(zip(SECOND, rest[:6])))
        rest = rest[6:]
    done = rest
    width = out_ref.shape[1]
    tps = out_ref.shape[2] // LANES // SEGS
    tiles = tps * SEGS
    move = Shifts(tps)
    rotations = [rot_ref[level] for level in range(LEVELS)]
    count = width >> SPLIT
    now = levels[SPLIT]
    bit0, bit1 = move.odd(1), move.odd(2)
    for start, ref in ((0, left_ref), (count, own_ref), (2 * count, right_ref)):
        for j in range(count):
            value = ref[j]
            evens = jnp.where(bit0, move.roll(value, 1), value)
            odds = jnp.where(bit0, value, move.roll(value, -1))
            for name, part, upper in zip(COARSE, (evens, odds, evens, odds), (0, 0, 1, 1)):
                if upper:
                    now[name][start + j] = jnp.where(bit1, part, move.roll(part, -2))
                else:
                    now[name][start + j] = jnp.where(bit1, move.roll(part, 2), part)
    total = 3 * count
    move.coefficients(now, 1, total - 2, 1 << SPLIT)
    for level in range(SPLIT, LEVELS - 1):
        now, coarse = levels[level], levels[level + 1]
        step = 1 << level
        half = total // 2
        for k in range(half - 1):
            coarse["east"][k] = 0.25 * move.pair(now["east"][2 * k + 1], step)
        for k in range(1, half - 1):
            move.coarse_sums(now, coarse, 2 * k, k, step)
        move.restrict(now, coarse, 2, 1, half - 2, rotations[level], step)
        total = half
        move.coefficients(coarse, 1, total - 2, 2 * step)

    def keep(target):
        def put(x, value):
            target[x] = value

        return put

    level = LEVELS - 1
    last, solved = levels[level], done.pop(0)
    own = width >> level
    move.sweep(
        last, own - 2, own + 4, lambda x: last["field"][x], rotations[level], 1 << level, keep(solved)
    )
    move.sweep(
        last, own - 1, own + 2, lambda x: solved[x], rotations[level], 1 << level, keep(last["field"])
    )
    solved, before = last["field"], own
    for level in reversed(range(LEVELS - 1)):
        now = levels[level]
        own = width >> level
        here = own if level >= SPLIT else FINE >> level
        lead = 2 * before - here if level >= SPLIT - 1 else 0

        def value(x, now=now, solved=solved, lead=lead):
            return now["field"][x] + solved[lax.div(x + lead, 2)]

        if level:
            target = done.pop(0)
            loop(
                here - 1,
                own + 2,
                lambda x, n, now=now, value=value, level=level, target=target: move.sweep(
                    now, x, n, value, rotations[level], 1 << level, keep(target)
                ),
                10,
            )
            solved, before = target, here
        else:

            def put(x, result, here=here):
                for k in range(tps):
                    row = pl.multiple_of(((x - here) * tps + k) * 8, 8)
                    flat[pl.ds(row, 8), :] = result[:, k * LANES : (k + 1) * LANES]

            loop(
                here,
                own,
                lambda x, n, now=now, value=value: move.sweep(now, x, n, value, rotations[0], 1, put),
            )

    for c in range(2):
        for i in range(width // 8):
            for t in range(tiles):
                s, k = divmod(t, tps)
                row = (8 * i * tps + k) * 8 + c * SEGS + s
                out_ref[c, 8 * i : 8 * i + 8, t * LANES : (t + 1) * LANES] = flat[
                    pl.ds(row, 8, stride=tps * 8), :
                ]


def local(forcing, viscosity, mass, coriolis, land, ice_tiles):
    width, height = viscosity.shape
    tiles = height // LANES
    tps = tiles // SEGS
    each = 2 * tps * 8
    outside = 4 * width + 8
    gx, gy = lax.axis_size("gx"), lax.axis_size("gy")
    lines = coriolis.reshape(tiles, LANES)
    vmem = pl.BlockSpec(memory_space=pltpu.VMEM)

    def here(*shape):
        return pltpu.VMEM(shape, f32)

    def call(kernel, outs, args, scratch=(), first=None):
        return pl.pallas_call(
            kernel,
            out_shape=outs,
            in_specs=[first or vmem] + [vmem] * (len(args) - 1),
            out_specs=jax.tree.map(lambda _: vmem, outs),
            scratch_shapes=scratch,
            compiler_params=pltpu.CompilerParams(vmem_limit_bytes=24 * 1024 * 1024),
        )(*args)

    packed, lowest, highest, edge, mirror, wall = call(
        prepare_kernel,
        (
            here(width * each, LANES),
            here(FINE * each, LANES),
            here(FINE * each, LANES),
            here(outside, LANES),
            here(outside, LANES),
            here(outside, LANES),
        ),
        (ice_tiles.T, forcing, viscosity, mass, land, lines),
        first=pl.BlockSpec(memory_space=pltpu.SMEM),
    )
    top = gy - 1
    swap = lax.ppermute(edge, "gy", [(i, gy - 1 - i) for i in range(gy)])
    folded = lax.ppermute(
        mirror, ("gx", "gy"), [(i * gy + top, (gx - 1 - i) * gy + top) for i in range(gx)]
    )
    ext, low, high = call(
        edge_kernel,
        (here(outside, LANES),) + (here(FINE * (each + 4), LANES),) * 2,
        (swap, folded, wall, lowest, highest),
    )
    up = [(i, (i + 1) % gx) for i in range(gx)]
    down = [(b, a) for a, b in up]
    from_left = lax.ppermute(high, "gx", up)
    from_right = lax.ppermute(low, "gx", down)

    span = (tps + 1) * LANES
    columns = [(2 * FINE + width) >> level for level in range(SPLIT)]
    columns += [3 * width >> level for level in range(SPLIT, LEVELS)]
    count = width >> SPLIT

    def lines_of(number):
        return here(number, 8, span)

    state = call(
        first_kernel,
        tuple(lines_of(columns[level]) for level in range(SPLIT) for _ in FIRST)
        + (lines_of(count), lines_of(LEVELS)),
        (packed, ext, from_left, from_right, lines),
        scratch=[lines_of(columns[0])]
        + [lines_of(columns[level]) for level in range(SPLIT)]
        + [lines_of(count)] * len(COARSE),
    )
    *kept, sent, rotation = state
    from_left = lax.ppermute(sent, "gx", up)
    from_right = lax.ppermute(sent, "gx", down)
    return call(
        second_kernel,
        jax.ShapeDtypeStruct((2, width, height), f32),
        (sent, from_left, from_right, rotation, *kept),
        scratch=[pltpu.VMEM((width * tps * 8, LANES), f32)]
        + [lines_of(columns[level]) for level in range(SPLIT, LEVELS) for _ in SECOND]
        + [lines_of(columns[level]) for level in reversed(range(1, LEVELS))],
    )


def solution(mesh):
    return jax.shard_map(
        local,
        mesh=mesh,
        in_specs=(
            P(None, ("groups", "gx"), "gy"),
            P(("groups", "gx"), "gy"),
            P(("groups", "gx"), "gy"),
            P("gy"),
            P("gx", "gy"),
            P("groups", None),
        ),
        out_specs=P(None, ("groups", "gx"), "gy"),
        check_vma=False,
    )
```

time: 678 us -> 94.8 us (0.14)
  starting transfers between devices: 413 us -> 68.1 us
  waiting for transfers between devices: 178 us -> 11 us
  local copies, waits for them, and re-layouts: 67.3 us -> 5.18 us
  Pallas kernels: 0 us -> 9.91 us
  other arithmetic: 8.82 us -> 0 us
    ppermute x99 -> x6, starting transfers between devices: 413 us -> 68.1 us  [the longest x1 43.4 us: local(): swap = lax.ppermute(edge, 'gy', [(i, gy - 1 - i) for i in range(gy)])]
    ppermute x99 -> x6, waiting for transfers between devices: 178 us -> 11 us  [the longest x1 7.09 us: local(): from_left = lax.ppermute(sent, 'gx', up)]
    slice x88 -> x0, local copies, waits for them, and re-layouts: 62.1 us -> none  [the longest x6 7.68 us: pair_mean(): values[..., 1::2, 1::2]]
    pallas_call x0 -> x4, Pallas kernels: none -> 9.91 us  [call(): pl.pallas_call(kernel, out_shape=outs, in_specs=[first or vmem] + [vmem]...]
  transfers between devices with their start and end apart: 99 -> 6, of which waited for: 44 -> 4; matrix products, arithmetic and copies ran while one was open for 2% -> 0% of each run, Pallas kernels for 0% -> 0%
where the time goes in v2:
time: 94.8 us; the launch traced here: 94.3 us
  starting transfers between devices  68.1 us (72%)
  waiting for transfers between devices  11 us (12%)
  Pallas kernels  9.91 us (10%)
  local copies, waits for them, and re-layouts  5.18 us (5%)
    ppermute x1, starting transfers between devices, local(): swap = lax.ppermute(edge, 'gy', [(i, gy - 1 - i) for i in range(gy)])  43.4 us
    pallas_call x4, Pallas kernels, call(): pl.pallas_call(kernel, out_shape=outs, in_specs=[first or vmem] + [vmem]...  9.91 us
    ppermute x1, starting transfers between devices, local(): from_right = lax.ppermute(sent, 'gx', down)  7.16 us
    ppermute x1, waiting for transfers between devices, local(): from_left = lax.ppermute(sent, 'gx', up)  7.09 us
    ppermute x1, starting transfers between devices, local(): lax.ppermute(mirror, ('gx', 'gy'), [(i * gy + top, (gx - 1 - i) * gy + to...  7 us
    unnamed x14, local copies, waits for them, and re-layouts  5.18 us
    ppermute x1, starting transfers between devices, local(): from_right = lax.ppermute(low, 'gx', down)  4.8 us
    ppermute x1, starting transfers between devices, local(): from_left = lax.ppermute(high, 'gx', up)  3.87 us
  transfers between devices with their start and end apart: 6, of which 4 were waited for; matrix products, arithmetic and copies ran while one was open for 0% of the time, Pallas kernels for 0%

profile of v2, /device:TPU:65, one launch (start us, length us, event | category | flops | bytes accessed | tf_op | source)
XLA Modules:
  0.0 94.3 jit_solution(3086020426361411685)
XLA Ops:
  0.0 0.0 copy-start
  0.0 1.0 %copy-done = f32[2,32,1536]{2,1,0:T(8,128)S(1)} copy-done((f32[2,32,1536]{2,1,0:T(8,128)S(1)}, f32[2,32,1536]{2,1,0:T(8,128)}, u32[]{:S(2)}) %copy-start) | copy-done | bytes 393240
  1.0 0.0 copy-start.1
  1.0 0.9 copy-done.1
  1.9 0.0 copy-start.2
  1.9 0.9 copy-done.2
  2.9 0.0 copy-start.3
  2.9 0.9 copy-done.3
  3.8 0.0 copy-start.4
  3.8 0.7 copy-done.4
  4.5 0.0 copy-start.6
  4.5 0.7 copy-done.6
  5.2 1.4 %shard_map.64 = (f32[1536,128]{1,0:T(8,128)S(1)}, f32[288,128]{1,0:T(8,128)S(1)}, f32[288,128]{1,0:T(8,128)S(1)}, f32[136,128]{1,0:T(8,128)S(1)}, f32[136,128]{1,0:T(8,128)S(1)}, /*index=5*/f32[136,128]{1,0:T(8,128)S(1)}) custom-call(s32[24,32]{1,0:T(8,128)S(1)} %bitcast.4, f32[2,32,1536]{2,1,0:T(8,128)S(1)} %copy-done, f32[32,1536]{1,0:T(8,128)S(1)} %copy-done.1, ...), custom_call_target="tpu_custom_call" | custom-call | tf_op jit(solution)/shard_map/pallas_call | solution.py:421
  6.6 43.4 %collective-permute-start = (f32[136,128]{1,0:T(8,128)S(1)}, f32[136,128]{1,0:T(8,128)S(1)}, u32[]{:S(2)}, u32[]{:S(2)}) collective-permute-start(f32[136,128]{1,0:T(8,128)S(1)} %get-tuple-element.27), channel_id=1, source_target_pairs={{0,1},{1,0},{2,3},{3,2},{4,5},{5,4},{6,7},{7,6},{8,9},{9,8},{10,11... | collective-permute-start | bytes 208904 | tf_op jit(solution)/shard_map/ppermute | solution.py:444
  50.0 7.0 %collective-permute-start.1 = (f32[136,128]{1,0:T(8,128)S(1)}, f32[136,128]{1,0:T(8,128)S(1)}, u32[]{:S(2)}, u32[]{:S(2)}) collective-permute-start(f32[136,128]{1,0:T(8,128)S(1)} %get-tuple-element.28), channel_id=1, source_target_pairs={{1,255},{3,253},{5,251},{7,249},{9,247},{11,245},{13,243},{15,241}... | collective-permute-start | bytes 208904 | tf_op jit(solution)/shard_map/ppermute | solution.py:445
  57.0 0.0 collective-permute-done.swap_ref
  57.0 1.7 %collective-permute-done.1.folded_ref = f32[136,128]{1,0:T(8,128)S(1)} collective-permute-done((f32[136,128]{1,0:T(8,128)S(1)}, f32[136,128]{1,0:T(8,128)S(1)}, u32[]{:S(2)}, u32[]{:S(2)}) %collective-permute-start.1) | collective-permute-done | bytes 69664 | tf_op jit(solution)/shard_map/ppermute | solution.py:445
  58.7 0.0 copy-start.5
  58.7 3.9 %collective-permute-start.2 = (f32[312,128]{1,0:T(8,128)S(1)}, f32[312,128]{1,0:T(8,128)S(1)}, u32[]{:S(2)}, u32[]{:S(2)}) collective-permute-start(f32[312,128]{1,0:T(8,128)S(1)} %get-tuple-element.33), channel_id=1, source_target_pairs={{0,2},{2,4},{4,6},{6,8},{8,10},{10,12},{12,14},{14,16},{16,18},{18... | collective-permute-start | bytes 479240 | tf_op jit(solution)/shard_map/ppermute | solution.py:455
  62.6 4.8 %collective-permute-start.3 = (f32[312,128]{1,0:T(8,128)S(1)}, f32[312,128]{1,0:T(8,128)S(1)}, u32[]{:S(2)}, u32[]{:S(2)}) collective-permute-start(f32[312,128]{1,0:T(8,128)S(1)} %get-tuple-element.34), channel_id=1, source_target_pairs={{2,0},{4,2},{6,4},{8,6},{10,8},{12,10},{14,12},{16,14},{18,16},{20... | collective-permute-start | bytes 479240 | tf_op jit(solution)/shard_map/ppermute | solution.py:456
  67.4 0.7 collective-permute-done.2.left_ref
  68.1 1.5 %collective-permute-done.3.right_ref = f32[312,128]{1,0:T(8,128)S(1)} collective-permute-done((f32[312,128]{1,0:T(8,128)S(1)}, f32[312,128]{1,0:T(8,128)S(1)}, u32[]{:S(2)}, u32[]{:S(2)}) %collective-permute-start.3) | collective-permute-done | bytes 159776 | tf_op jit(solution)/shard_map/ppermute | solution.py:456
  69.6 0.0 copy-done.5
  69.6 4.0 %shard_map.66 = (f32[44,8,512]{2,1,0:T(8,128)S(1)}, f32[44,8,512]{2,1,0:T(8,128)S(1)}, f32[44,8,512]{2,1,0:T(8,128)S(1)}, f32[44,8,512]{2,1,0:T(8,128)S(1)}, f32...) custom-call(f32[1536,128]{1,0:T(8,128)S(1)} %get-tuple-element.26.ow, ...), custom_call_target="tpu_custom_call" | custom-call | tf_op jit(solution)/shard_map/pallas_call | solution.py:421
  73.6 7.2 %collective-permute-start.5 = (f32[8,8,512]{2,1,0:T(8,128)S(1)}, f32[8,8,512]{2,1,0:T(8,128)S(1)}, u32[]{:S(2)}, u32[]{:S(2)}) collective-permute-start(f32[8,8,512]{2,1,0:T(8,128)S(1)} %get-tuple-element.35.own_ref), channel_id=1, source_target_pairs={{2,0},{4,2},{6,4},{8,6},{10,8},{12,10},{14,12},{16,14},{18,16},{20... | collective-permute-start | bytes 393224 | tf_op jit(solution)/shard_map/ppermute | solution.py:477
  80.8 2.0 %collective-permute-start.4 = (f32[8,8,512]{2,1,0:T(8,128)S(1)}, f32[8,8,512]{2,1,0:T(8,128)S(1)}, u32[]{:S(2)}, u32[]{:S(2)}) collective-permute-start(f32[8,8,512]{2,1,0:T(8,128)S(1)} %get-tuple-element.35.own_ref), channel_id=1, source_target_pairs={{0,2},{2,4},{4,6},{6,8},{8,10},{10,12},{12,14},{14,16},{16,18},{18... | collective-permute-start | bytes 393224 | tf_op jit(solution)/shard_map/ppermute | solution.py:476
  82.7 0.0 collective-permute-done.5.right_ref
  82.7 7.1 %collective-permute-done.4.left_ref = f32[8,8,512]{2,1,0:T(8,128)S(1)} collective-permute-done((f32[8,8,512]{2,1,0:T(8,128)S(1)}, f32[8,8,512]{2,1,0:T(8,128)S(1)}, u32[]{:S(2)}, u32[]{:S(2)}) %collective-permute-start.4) | collective-permute-done | bytes 131104 | tf_op jit(solution)/shard_map/ppermute | solution.py:476
  89.8 4.5 %shard_map.67 = f32[2,32,1536]{2,1,0:T(8,128)} custom-call(f32[8,8,512]{2,1,0:T(8,128)S(1)} %get-tuple-element.35.own_ref, f32[8,8,512]{2,1,0:T(8,128)S(1)} %collective-permute-done.4.left_ref, f32[8,8,512]{2,1,0:T(8,128)S(1)} %collective-permute-done.5.right_ref, f32[4,8,512]{2,1,0:T(8,128)S(1)} %get-tuple-element.36.rot_ref, ...), custom_call_target="tpu_custom_call" | custom-call | tf_op jit(solution)/shard_map/pallas_call | solution.py:421
  (1 shorter events, 0.0 us)
Async XLA Ops:
  0.0 1.0 %copy-start = (f32[2,32,1536]{2,1,0:T(8,128)S(1)}, f32[2,32,1536]{2,1,0:T(8,128)}, u32[]{:S(2)}) copy-start(f32[2,32,1536]{2,1,0:T(8,128)} %forcing_ref.1) | copy-start | bytes 1179652
  1.0 0.9 copy-start.1
  1.9 0.9 copy-start.2
  2.9 0.9 copy-start.3
  3.8 0.7 copy-start.4
  4.5 0.7 copy-start.6
  6.6 50.4 %collective-permute-start = (f32[136,128]{1,0:T(8,128)S(1)}, f32[136,128]{1,0:T(8,128)S(1)}, u32[]{:S(2)}, u32[]{:S(2)}) collective-permute-start(f32[136,128]{1,0:T(8,128)S(1)} %get-tuple-element.27), channel_id=1, source_target_pairs={{0,1},{1,0},{2,3},{3,2},{4,5},{5,4},{6,7},{7,6},{8,9},{9,8},{10,11... | collective-permute-start | bytes 208904 | tf_op jit(solution)/shard_map/ppermute | solution.py:444
  50.0 8.7 %collective-permute-start.1 = (f32[136,128]{1,0:T(8,128)S(1)}, f32[136,128]{1,0:T(8,128)S(1)}, u32[]{:S(2)}, u32[]{:S(2)}) collective-permute-start(f32[136,128]{1,0:T(8,128)S(1)} %get-tuple-element.28), channel_id=1, source_target_pairs={{1,255},{3,253},{5,251},{7,249},{9,247},{11,245},{13,243},{15,241}... | collective-permute-start | bytes 208904 | tf_op jit(solution)/shard_map/ppermute | solution.py:445
  58.7 10.9 %copy-start.5 = (f32[1536]{0:T(1024)S(1)}, f32[1536]{0:T(1024)}, u32[]{:S(2)}) copy-start(f32[1536]{0:T(1024)} %param.9) | copy-start | bytes 18436
  58.7 9.4 %collective-permute-start.2 = (f32[312,128]{1,0:T(8,128)S(1)}, f32[312,128]{1,0:T(8,128)S(1)}, u32[]{:S(2)}, u32[]{:S(2)}) collective-permute-start(f32[312,128]{1,0:T(8,128)S(1)} %get-tuple-element.33), channel_id=1, source_target_pairs={{0,2},{2,4},{4,6},{6,8},{8,10},{10,12},{12,14},{14,16},{16,18},{18... | collective-permute-start | bytes 479240 | tf_op jit(solution)/shard_map/ppermute | solution.py:455
  62.6 7.0 %collective-permute-start.3 = (f32[312,128]{1,0:T(8,128)S(1)}, f32[312,128]{1,0:T(8,128)S(1)}, u32[]{:S(2)}, u32[]{:S(2)}) collective-permute-start(f32[312,128]{1,0:T(8,128)S(1)} %get-tuple-element.34), channel_id=1, source_target_pairs={{2,0},{4,2},{6,4},{8,6},{10,8},{12,10},{14,12},{16,14},{18,16},{20... | collective-permute-start | bytes 479240 | tf_op jit(solution)/shard_map/ppermute | solution.py:456
  73.6 9.1 %collective-permute-start.5 = (f32[8,8,512]{2,1,0:T(8,128)S(1)}, f32[8,8,512]{2,1,0:T(8,128)S(1)}, u32[]{:S(2)}, u32[]{:S(2)}) collective-permute-start(f32[8,8,512]{2,1,0:T(8,128)S(1)} %get-tuple-element.35.own_ref), channel_id=1, source_target_pairs={{2,0},{4,2},{6,4},{8,6},{10,8},{12,10},{14,12},{16,14},{18,16},{20... | collective-permute-start | bytes 393224 | tf_op jit(solution)/shard_map/ppermute | solution.py:477
  80.8 9.1 %collective-permute-start.4 = (f32[8,8,512]{2,1,0:T(8,128)S(1)}, f32[8,8,512]{2,1,0:T(8,128)S(1)}, u32[]{:S(2)}, u32[]{:S(2)}) collective-permute-start(f32[8,8,512]{2,1,0:T(8,128)S(1)} %get-tuple-element.35.own_ref), channel_id=1, source_target_pairs={{0,2},{2,4},{4,6},{6,8},{8,10},{10,12},{12,14},{14,16},{16,18},{18... | collective-permute-start | bytes 393224 | tf_op jit(solution)/shard_map/ppermute | solution.py:476

commit v3 on v2

--- a/solution.py
+++ b/solution.py
@@ -1,5 +1,3 @@
-import functools
-
 import jax
 import jax.numpy as jnp
 from jax import lax
@@ -7,6 +5,7 @@
 from jax.experimental.pallas import tpu as pltpu
 from jax.sharding import PartitionSpec as P
 
+
 TILE = 128
 LEVELS = 4
 LANES = 128
@@ -28,16 +27,26 @@
     return lax.broadcasted_iota(jnp.int32, shape, axis)
 
 
-def prepare_kernel(
-    ice_ref, forcing_ref, visc_ref, mass_ref, land_ref, cor_ref,
-    packed_ref, lowest_ref, highest_ref, edge_ref, mirror_ref, wall_ref,
-):
+def is_even():
+    return lax.axis_index("gx") & 1 == 0
+
+
+def prepare_kernel(*refs):
+    sources, outs = refs[:6], refs[6:12]
+    held, sems = refs[12:18], refs[18]
+    copies = [pltpu.make_async_copy(a, b, sems.at[n]) for n, (a, b) in enumerate(zip(sources, held))]
+    for copy in copies:
+        copy.start()
+    ice_ref, forcing_ref, visc_ref, mass_ref, land_ref, cor_ref = held
+    packed_ref, lowest_ref, highest_ref, edge_ref, mirror_ref, wall_ref = outs
     width = visc_ref.shape[0]
     tiles = visc_ref.shape[1] // LANES
     tps = tiles // SEGS
     tile_x = lax.axis_index("gx") * width // TILE
     tile_y = lax.axis_index("gy") * tiles
     lane = iota((8, LANES), 1)
+    for copy in copies:
+        copy.wait()
     for i in range(width // 8):
         rows = slice(8 * i, 8 * i + 8)
         ends = []
@@ -87,7 +96,7 @@
     )
 
 
-def edge_kernel(swap_ref, folded_ref, wall_ref, lowest_ref, highest_ref, ext_ref, low_ref, high_ref):
+def edge_kernel(swap_ref, folded_ref, wall_ref, lowest_ref, highest_ref, ext_ref, odd_ref, even_ref):
     is_top = lax.axis_index("gy") == lax.axis_size("gy") - 1
     north = iota(swap_ref.shape, 1) < HALF
     swap = swap_ref[...]
@@ -97,10 +106,18 @@
     ext_ref[...] = beyond
     side = lowest_ref.shape[0]
     main = swap_ref.shape[0] - 8
-    low_ref[0:side, :] = lowest_ref[...]
-    low_ref[side : side + 4 * FINE, :] = ext_ref[0 : 4 * FINE, :]
-    high_ref[0:side, :] = highest_ref[...]
-    high_ref[side : side + 4 * FINE, :] = ext_ref[main - 4 * FINE : main, :]
+    even = is_even()
+    parts = (
+        (slice(0, side), lowest_ref[...], highest_ref[...]),
+        (
+            slice(side, side + 4 * FINE),
+            ext_ref[0 : 4 * FINE, :],
+            ext_ref[main - 4 * FINE : main, :],
+        ),
+    )
+    for rows, low, high in parts:
+        odd_ref[rows, :] = jnp.where(even, low, high)
+        even_ref[rows, :] = jnp.where(even, high, low)
 
 
 class Shifts:
@@ -211,7 +228,7 @@
 COARSE = ("right", "east", "north", "mass")
 
 
-def first_kernel(own_ref, ext_ref, left_ref, right_ref, cor_ref, *refs):
+def first_kernel(own_ref, ext_ref, odd_ref, even_ref, cor_ref, *refs):
     width = (ext_ref.shape[0] - 8) // 4
     tps = cor_ref.shape[0] // SEGS
     move = Shifts(tps)
@@ -229,10 +246,18 @@
         rot_ref[level] = rotations[level]
     top = levels[0]
 
-    def unpack(ref, base, ext, index, x):
+    even = is_even()
+
+    def from_left(rows):
+        return jnp.where(even, odd_ref[rows, :], even_ref[rows, :])
+
+    def from_right(rows):
+        return jnp.where(even, even_ref[rows, :], odd_ref[rows, :])
+
+    def unpack(load, base, ext, index, x):
         rows = [jnp.broadcast_to(ext[4 * index + a : 4 * index + a + 1], (8, LANES)) for a in range(4)]
         both = move.with_halo(
-            [ref[pl.ds(base + 8 * k, 8), :] for k in range(tps)], jnp.where(move.low, rows[0], rows[1])
+            [load(pl.ds(base + 8 * k, 8)) for k in range(tps)], jnp.where(move.low, rows[0], rows[1])
         )
         turned = [other(part) for part in both]
         value = jnp.concatenate([jnp.where(move.low, a, b) for a, b in zip(both, turned)], 1)
@@ -240,7 +265,7 @@
         top["mass"][x] = jnp.concatenate([jnp.where(move.low, b, a) for a, b in zip(both, turned)], 1)
         top["right"][x] = jnp.concatenate(
             move.with_halo(
-                [ref[pl.ds(base + 8 * (tps + k), 8), :] for k in range(tps)],
+                [load(pl.ds(base + 8 * (tps + k), 8)) for k in range(tps)],
                 jnp.where(move.low, rows[2], rows[3]),
             ),
             1,
@@ -248,18 +273,24 @@
         top["north"][x] = 0.5 * (value + move.roll(value, -1))
 
     each = 2 * tps * 8
-    for ref, start in ((left_ref, 0), (right_ref, FINE + width)):
+    for load, start in ((from_left, 0), (from_right, FINE + width)):
         for j in range(0, FINE, 2):
-            ext = ref[FINE * each + 4 * j : FINE * each + 4 * j + 8, :]
+            ext = load(pl.ds(FINE * each + 4 * j, 8))
             for index in range(2):
-                unpack(ref, (j + index) * each, ext, index, start + j + index)
+                unpack(load, (j + index) * each, ext, index, start + j + index)
 
     def own(first, group):
         for j in range(0, group, 2):
             x = first + j
             ext = ext_ref[pl.ds(pl.multiple_of(4 * x, 8), 8), :]
             for index in range(2):
-                unpack(own_ref, pl.multiple_of((x + index) * each, 8), ext, index, FINE + x + index)
+                unpack(
+                    lambda rows: own_ref[rows, :],
+                    pl.multiple_of((x + index) * each, 8),
+                    ext,
+                    index,
+                    FINE + x + index,
+                )
 
     loop(0, width, own)
     columns = 2 * FINE + width
@@ -303,7 +334,7 @@
 SECOND = ("right", "east", "north", "mass", "scale", "field")
 
 
-def second_kernel(own_ref, left_ref, right_ref, rot_ref, *refs):
+def second_kernel(own_ref, odd_ref, even_ref, rot_ref, *refs):
     out_refs = 5 * SPLIT
     levels = [dict(zip(FIRST, refs[5 * n : 5 * n + 5])) for n in range(SPLIT)]
     out_ref = refs[out_refs]
@@ -321,9 +352,16 @@
     count = width >> SPLIT
     now = levels[SPLIT]
     bit0, bit1 = move.odd(1), move.odd(2)
-    for start, ref in ((0, left_ref), (count, own_ref), (2 * count, right_ref)):
+    even = is_even()
+    loads = (
+        lambda j: jnp.where(even, odd_ref[j], even_ref[j]),
+        lambda j: own_ref[j],
+        lambda j: jnp.where(even, even_ref[j], odd_ref[j]),
+    )
+    for third, load in enumerate(loads):
+        start = third * count
         for j in range(count):
-            value = ref[j]
+            value = load(j)
             evens = jnp.where(bit0, move.roll(value, 1), value)
             odds = jnp.where(bit0, value, move.roll(value, -1))
             for name, part, upper in zip(COARSE, (evens, odds, evens, odds), (0, 0, 1, 1)):
@@ -417,16 +455,17 @@
     def here(*shape):
         return pltpu.VMEM(shape, f32)
 
-    def call(kernel, outs, args, scratch=(), first=None):
+    def call(kernel, outs, args, scratch=(), space=pltpu.VMEM):
         return pl.pallas_call(
             kernel,
             out_shape=outs,
-            in_specs=[first or vmem] + [vmem] * (len(args) - 1),
+            in_specs=[pl.BlockSpec(memory_space=space)] * len(args),
             out_specs=jax.tree.map(lambda _: vmem, outs),
             scratch_shapes=scratch,
             compiler_params=pltpu.CompilerParams(vmem_limit_bytes=24 * 1024 * 1024),
-        )(*args)
-
+        )(*(pltpu.with_memory_space_constraint(arg, space) for arg in args))
+
+    sources = (ice_tiles.T, forcing, viscosity, mass, land, lines)
     packed, lowest, highest, edge, mirror, wall = call(
         prepare_kernel,
         (
@@ -437,23 +476,26 @@
             here(outside, LANES),
             here(outside, LANES),
         ),
-        (ice_tiles.T, forcing, viscosity, mass, land, lines),
-        first=pl.BlockSpec(memory_space=pltpu.SMEM),
+        sources,
+        scratch=[pltpu.SMEM(sources[0].shape, sources[0].dtype)]
+        + [pltpu.VMEM(source.shape, source.dtype) for source in sources[1:]]
+        + [pltpu.SemaphoreType.DMA((len(sources),))],
+        space=pltpu.HBM,
     )
     top = gy - 1
-    swap = lax.ppermute(edge, "gy", [(i, gy - 1 - i) for i in range(gy)])
     folded = lax.ppermute(
         mirror, ("gx", "gy"), [(i * gy + top, (gx - 1 - i) * gy + top) for i in range(gx)]
     )
-    ext, low, high = call(
+    swap = lax.ppermute(edge, "gy", [(i, gy - 1 - i) for i in range(gy)])
+    ext, odd, even = call(
         edge_kernel,
         (here(outside, LANES),) + (here(FINE * (each + 4), LANES),) * 2,
         (swap, folded, wall, lowest, highest),
     )
-    up = [(i, (i + 1) % gx) for i in range(gx)]
-    down = [(b, a) for a, b in up]
-    from_left = lax.ppermute(high, "gx", up)
-    from_right = lax.ppermute(low, "gx", down)
+    odd_pairs = [(i, (i + (1 if i % 2 else gx - 1)) % gx) for i in range(gx)]
+    even_pairs = [(i, i ^ 1) for i in range(gx)]
+    by_odd = lax.ppermute(odd, "gx", odd_pairs)
+    by_even = lax.ppermute(even, "gx", even_pairs)
 
     span = (tps + 1) * LANES
     columns = [(2 * FINE + width) >> level for level in range(SPLIT)]
@@ -467,18 +509,18 @@
         first_kernel,
         tuple(lines_of(columns[level]) for level in range(SPLIT) for _ in FIRST)
         + (lines_of(count), lines_of(LEVELS)),
-        (packed, ext, from_left, from_right, lines),
+        (packed, ext, by_odd, by_even, lines),
         scratch=[lines_of(columns[0])]
         + [lines_of(columns[level]) for level in range(SPLIT)]
         + [lines_of(count)] * len(COARSE),
     )
     *kept, sent, rotation = state
-    from_left = lax.ppermute(sent, "gx", up)
-    from_right = lax.ppermute(sent, "gx", down)
+    by_odd = lax.ppermute(sent, "gx", odd_pairs)
+    by_even = lax.ppermute(sent, "gx", even_pairs)
     return call(
         second_kernel,
         jax.ShapeDtypeStruct((2, width, height), f32),
-        (sent, from_left, from_right, rotation, *kept),
+        (sent, by_odd, by_even, rotation, *kept),
         scratch=[pltpu.VMEM((width * tps * 8, LANES), f32)]
         + [lines_of(columns[level]) for level in range(SPLIT, LEVELS) for _ in SECOND]
         + [lines_of(columns[level]) for level in reversed(range(1, LEVELS))],

time: 94.8 us -> 86.7 us (0.915)
  local copies, waits for them, and re-layouts: 5.18 us -> 0.01 us
  waiting for transfers between devices: 11 us -> 8.96 us
  starting transfers between devices: 68.1 us -> 66.8 us
    unnamed x14 -> x2, local copies, waits for them, and re-layouts: 5.18 us -> 0.01 us
    ppermute x4, waiting for transfers between devices: 9.29 us -> 7.27 us  [the longest x1 3.39 us: local(): by_even = lax.ppermute(even, 'gx', even_pairs)]
    ppermute x4, starting transfers between devices: 17.8 us -> 16.5 us  [the longest x1 6.7 us: local(): by_odd = lax.ppermute(odd, 'gx', odd_pairs)]
where the time goes in v3:
time: 86.7 us; the launch traced here: 86.3 us
  starting transfers between devices  66.8 us (77%)
  Pallas kernels  10.5 us (12%)
  waiting for transfers between devices  8.96 us (10%)
    ppermute x1, starting transfers between devices, local(): swap = lax.ppermute(edge, 'gy', [(i, gy - 1 - i) for i in range(gy)])  43.4 us
    pallas_call x4, Pallas kernels, call(): pl.pallas_call(kernel, out_shape=outs, in_specs=[pl.BlockSpec(memory_spac...  10.5 us
    ppermute x1, starting transfers between devices, local(): lax.ppermute(mirror, ('gx', 'gy'), [(i * gy + top, (gx - 1 - i) * gy + to...  7 us
    ppermute x1, starting transfers between devices, local(): by_odd = lax.ppermute(odd, 'gx', odd_pairs)  6.7 us
    ppermute x1, starting transfers between devices, local(): by_odd = lax.ppermute(sent, 'gx', odd_pairs)  5.87 us
    ppermute x1, waiting for transfers between devices, local(): by_even = lax.ppermute(even, 'gx', even_pairs)  3.39 us
    ppermute x1, waiting for transfers between devices, local(): by_odd = lax.ppermute(sent, 'gx', odd_pairs)  3.18 us
    ppermute x1, starting transfers between devices, local(): by_even = lax.ppermute(even, 'gx', even_pairs)  1.95 us
  transfers between devices with their start and end apart: 6, of which 4 were waited for; matrix products, arithmetic and copies ran while one was open for 0% of the time, Pallas kernels for 0%

profile of v3, /device:TPU:65, one launch (start us, length us, event | category | flops | bytes accessed | tf_op | source)
XLA Modules:
  0.0 86.3 jit_solution(17446269530501286994)
XLA Ops:
  0.0 1.9 %shard_map.64 = (f32[1536,128]{1,0:T(8,128)S(1)}, f32[288,128]{1,0:T(8,128)S(1)}, f32[288,128]{1,0:T(8,128)S(1)}, f32[136,128]{1,0:T(8,128)S(1)}, f32[136,128]{1,0:T(8,128)S(1)}, /*index=5*/f32[136,128]{1,0:T(8,128)S(1)}) custom-call(s32[24,32]{1,0:T(8,128)} %bitcast.4, f32[2,32,1536]{2,1,0:T(8,128)} %refs_1_.1, f32[32,1536]{1,0:T(8,128)} %refs_2_.1, ...), custom_call_target="tpu_custom_call" | custom-call | tf_op jit(solution)/shard_map/pallas_call | solution.py:459
  1.9 43.4 %collective-permute-start = (f32[136,128]{1,0:T(8,128)S(1)}, f32[136,128]{1,0:T(8,128)S(1)}, u32[]{:S(2)}, u32[]{:S(2)}) collective-permute-start(f32[136,128]{1,0:T(8,128)S(1)} %get-tuple-element.27), channel_id=1, source_target_pairs={{0,1},{1,0},{2,3},{3,2},{4,5},{5,4},{6,7},{7,6},{8,9},{9,8},{10,11... | collective-permute-start | bytes 208904 | tf_op jit(solution)/shard_map/ppermute | solution.py:489
  45.3 7.0 %collective-permute-start.1 = (f32[136,128]{1,0:T(8,128)S(1)}, f32[136,128]{1,0:T(8,128)S(1)}, u32[]{:S(2)}, u32[]{:S(2)}) collective-permute-start(f32[136,128]{1,0:T(8,128)S(1)} %get-tuple-element.28), channel_id=1, source_target_pairs={{1,255},{3,253},{5,251},{7,249},{9,247},{11,245},{13,243},{15,241}... | collective-permute-start | bytes 208904 | tf_op jit(solution)/shard_map/ppermute | solution.py:486
  52.3 0.0 collective-permute-done.swap_ref
  52.3 1.7 %collective-permute-done.1.folded_ref = f32[136,128]{1,0:T(8,128)S(1)} collective-permute-done((f32[136,128]{1,0:T(8,128)S(1)}, f32[136,128]{1,0:T(8,128)S(1)}, u32[]{:S(2)}, u32[]{:S(2)}) %collective-permute-start.1) | collective-permute-done | bytes 69664 | tf_op jit(solution)/shard_map/ppermute | solution.py:486
  54.0 0.0 copy-start
  54.0 0.1 shard_map.65
  54.1 6.7 %collective-permute-start.2 = (f32[312,128]{1,0:T(8,128)S(1)}, f32[312,128]{1,0:T(8,128)S(1)}, u32[]{:S(2)}, u32[]{:S(2)}) collective-permute-start(f32[312,128]{1,0:T(8,128)S(1)} %get-tuple-element.33), channel_id=1, source_target_pairs={{0,254},{2,4},{4,2},{6,8},{8,6},{10,12},{12,10},{14,16},{16,14},{1... | collective-permute-start | bytes 479240 | tf_op jit(solution)/shard_map/ppermute | solution.py:497
  60.8 2.0 %collective-permute-start.3 = (f32[312,128]{1,0:T(8,128)S(1)}, f32[312,128]{1,0:T(8,128)S(1)}, u32[]{:S(2)}, u32[]{:S(2)}) collective-permute-start(f32[312,128]{1,0:T(8,128)S(1)} %get-tuple-element.34), channel_id=1, source_target_pairs={{0,2},{2,0},{4,6},{6,4},{8,10},{10,8},{12,14},{14,12},{16,18},{18,... | collective-permute-start | bytes 479240 | tf_op jit(solution)/shard_map/ppermute | solution.py:498
  62.7 0.7 collective-permute-done.2.odd_ref
  63.4 3.4 %collective-permute-done.3.even_ref = f32[312,128]{1,0:T(8,128)S(1)} collective-permute-done((f32[312,128]{1,0:T(8,128)S(1)}, f32[312,128]{1,0:T(8,128)S(1)}, u32[]{:S(2)}, u32[]{:S(2)}) %collective-permute-start.3) | collective-permute-done | bytes 159776 | tf_op jit(solution)/shard_map/ppermute | solution.py:498
  66.8 0.0 copy-done
  66.8 4.0 %shard_map.66 = (f32[44,8,512]{2,1,0:T(8,128)S(1)}, f32[44,8,512]{2,1,0:T(8,128)S(1)}, f32[44,8,512]{2,1,0:T(8,128)S(1)}, f32[44,8,512]{2,1,0:T(8,128)S(1)}, f32...) custom-call(f32[1536,128]{1,0:T(8,128)S(1)} %get-tuple-element.26.ow, ...), custom_call_target="tpu_custom_call" | custom-call | tf_op jit(solution)/shard_map/pallas_call | solution.py:459
  70.8 2.0 %collective-permute-start.5 = (f32[8,8,512]{2,1,0:T(8,128)S(1)}, f32[8,8,512]{2,1,0:T(8,128)S(1)}, u32[]{:S(2)}, u32[]{:S(2)}) collective-permute-start(f32[8,8,512]{2,1,0:T(8,128)S(1)} %get-tuple-element.35.own_ref), channel_id=1, source_target_pairs={{0,2},{2,0},{4,6},{6,4},{8,10},{10,8},{12,14},{14,12},{16,18},{18,... | collective-permute-start | bytes 393224 | tf_op jit(solution)/shard_map/ppermute | solution.py:519
  72.8 5.9 %collective-permute-start.4 = (f32[8,8,512]{2,1,0:T(8,128)S(1)}, f32[8,8,512]{2,1,0:T(8,128)S(1)}, u32[]{:S(2)}, u32[]{:S(2)}) collective-permute-start(f32[8,8,512]{2,1,0:T(8,128)S(1)} %get-tuple-element.35.own_ref), channel_id=1, source_target_pairs={{0,254},{2,4},{4,2},{6,8},{8,6},{10,12},{12,10},{14,16},{16,14},{1... | collective-permute-start | bytes 393224 | tf_op jit(solution)/shard_map/ppermute | solution.py:518
  78.7 0.0 collective-permute-done.5.even_ref
  78.7 3.2 %collective-permute-done.4.odd_ref = f32[8,8,512]{2,1,0:T(8,128)S(1)} collective-permute-done((f32[8,8,512]{2,1,0:T(8,128)S(1)}, f32[8,8,512]{2,1,0:T(8,128)S(1)}, u32[]{:S(2)}, u32[]{:S(2)}) %collective-permute-start.4) | collective-permute-done | bytes 131104 | tf_op jit(solution)/shard_map/ppermute | solution.py:518
  81.9 4.5 %shard_map.67 = f32[2,32,1536]{2,1,0:T(8,128)} custom-call(f32[8,8,512]{2,1,0:T(8,128)S(1)} %get-tuple-element.35.own_ref, f32[8,8,512]{2,1,0:T(8,128)S(1)} %collective-permute-done.4.odd_ref, f32[8,8,512]{2,1,0:T(8,128)S(1)} %collective-permute-done.5.even_ref, f32[4,8,512]{2,1,0:T(8,128)S(1)} %get-tuple-element.36.rot_ref, ...), custom_call_target="tpu_custom_call" | custom-call | tf_op jit(solution)/shard_map/pallas_call | solution.py:459
Async XLA Ops:
  1.9 50.4 %collective-permute-start = (f32[136,128]{1,0:T(8,128)S(1)}, f32[136,128]{1,0:T(8,128)S(1)}, u32[]{:S(2)}, u32[]{:S(2)}) collective-permute-start(f32[136,128]{1,0:T(8,128)S(1)} %get-tuple-element.27), channel_id=1, source_target_pairs={{0,1},{1,0},{2,3},{3,2},{4,5},{5,4},{6,7},{7,6},{8,9},{9,8},{10,11... | collective-permute-start | bytes 208904 | tf_op jit(solution)/shard_map/ppermute | solution.py:489
  45.3 8.7 %collective-permute-start.1 = (f32[136,128]{1,0:T(8,128)S(1)}, f32[136,128]{1,0:T(8,128)S(1)}, u32[]{:S(2)}, u32[]{:S(2)}) collective-permute-start(f32[136,128]{1,0:T(8,128)S(1)} %get-tuple-element.28), channel_id=1, source_target_pairs={{1,255},{3,253},{5,251},{7,249},{9,247},{11,245},{13,243},{15,241}... | collective-permute-start | bytes 208904 | tf_op jit(solution)/shard_map/ppermute | solution.py:486
  54.0 12.8 %copy-start = (f32[1536]{0:T(1024)S(1)}, f32[1536]{0:T(1024)}, u32[]{:S(2)}) copy-start(f32[1536]{0:T(1024)} %param.9) | copy-start | bytes 18436
  54.1 9.4 %collective-permute-start.2 = (f32[312,128]{1,0:T(8,128)S(1)}, f32[312,128]{1,0:T(8,128)S(1)}, u32[]{:S(2)}, u32[]{:S(2)}) collective-permute-start(f32[312,128]{1,0:T(8,128)S(1)} %get-tuple-element.33), channel_id=1, source_target_pairs={{0,254},{2,4},{4,2},{6,8},{8,6},{10,12},{12,10},{14,16},{16,14},{1... | collective-permute-start | bytes 479240 | tf_op jit(solution)/shard_map/ppermute | solution.py:497
  60.8 6.0 %collective-permute-start.3 = (f32[312,128]{1,0:T(8,128)S(1)}, f32[312,128]{1,0:T(8,128)S(1)}, u32[]{:S(2)}, u32[]{:S(2)}) collective-permute-start(f32[312,128]{1,0:T(8,128)S(1)} %get-tuple-element.34), channel_id=1, source_target_pairs={{0,2},{2,0},{4,6},{6,4},{8,10},{10,8},{12,14},{14,12},{16,18},{18,... | collective-permute-start | bytes 479240 | tf_op jit(solution)/shard_map/ppermute | solution.py:498
  70.8 7.8 %collective-permute-start.5 = (f32[8,8,512]{2,1,0:T(8,128)S(1)}, f32[8,8,512]{2,1,0:T(8,128)S(1)}, u32[]{:S(2)}, u32[]{:S(2)}) collective-permute-start(f32[8,8,512]{2,1,0:T(8,128)S(1)} %get-tuple-element.35.own_ref), channel_id=1, source_target_pairs={{0,2},{2,0},{4,6},{6,4},{8,10},{10,8},{12,14},{14,12},{16,18},{18,... | collective-permute-start | bytes 393224 | tf_op jit(solution)/shard_map/ppermute | solution.py:519
  72.8 9.1 %collective-permute-start.4 = (f32[8,8,512]{2,1,0:T(8,128)S(1)}, f32[8,8,512]{2,1,0:T(8,128)S(1)}, u32[]{:S(2)}, u32[]{:S(2)}) collective-permute-start(f32[8,8,512]{2,1,0:T(8,128)S(1)} %get-tuple-element.35.own_ref), channel_id=1, source_target_pairs={{0,254},{2,4},{4,2},{6,8},{8,6},{10,12},{12,10},{14,16},{16,14},{1... | collective-permute-start | bytes 393224 | tf_op jit(solution)/shard_map/ppermute | solution.py:518

commit v4 on v3

v4 whole, which is shorter than its diff:
```python
import jax
import jax.numpy as jnp
from jax import lax
from jax.experimental import pallas as pl
from jax.experimental.pallas import tpu as pltpu
from jax.sharding import PartitionSpec as P


TILE = 128
LEVELS = 4
LANES = 128
SEGS = 4
HALF = LANES // 2
GROUP = 8

relax_weight = 0.8
land_mass = 4.0
f32 = jnp.float32
exact = lax.Precision.HIGHEST


FINE = 6
SPLIT = 2


def iota(shape, axis):
    return lax.broadcasted_iota(jnp.int32, shape, axis)


def is_even():
    return lax.axis_index("gx") & 1 == 0


def masked(ice, visc, mass, land, forcing):
    land = land.astype(f32)
    ocean = 1.0 - land
    return (
        visc * ice * ocean,
        mass * ocean + land_mass * land,
        forcing[0] * ocean,
        forcing[1] * ocean,
    )


def fetch(sources, held, sems):
    copies = [pltpu.make_async_copy(a, b, sems.at[n]) for n, (a, b) in enumerate(zip(sources, held))]
    for copy in copies:
        copy.start()
    return copies


def ends_kernel(
    ice_hbm, forcing_hbm, visc_hbm, mass_hbm, land_hbm, cor_hbm, edge_ref, mirror_ref, wall_ref,
    ice_ref, cor_ref, forcing_ref, visc_ref, mass_ref, land_ref, sems,
):
    width = visc_hbm.shape[0]
    tiles = visc_hbm.shape[1] // LANES
    sources, held = [ice_hbm, cor_hbm], [ice_ref, cor_ref]
    for n, t in enumerate((0, tiles - 1)):
        cols = pl.ds(t * LANES, LANES)
        sources += [forcing_hbm.at[:, :, cols]] + [a.at[:, cols] for a in (visc_hbm, mass_hbm, land_hbm)]
        held += [a.at[n] for a in (forcing_ref, visc_ref, mass_ref, land_ref)]
    copies = fetch(sources, held, sems)
    tile_x = lax.axis_index("gx") * width // TILE
    tile_y = lax.axis_index("gy") * tiles
    lane = iota((8, LANES), 1)
    main = 4 * width
    flip = (iota((LANES, LANES), 0) + iota((LANES, LANES), 1) == LANES - 1).astype(f32)
    row, col = iota((main, main), 0), iota((main, main), 1)
    sign = jnp.where(row & 2 == 0, 1.0, -1.0)
    turn = jnp.where((row & 3 == col & 3) & ((row >> 2) + (col >> 2) == width - 1), sign, 0.0)
    wall_ref[main : main + 8, :] = jnp.zeros((8, LANES), f32)
    for copy in copies:
        copy.wait()
    for i in range(width // 8):
        rows = slice(8 * i, 8 * i + 8)
        ends = [
            masked(
                ice_ref[tile_y + t, tile_x].astype(f32),
                visc_ref[n, rows, :],
                mass_ref[n, rows, :],
                land_ref[n, rows, :],
                [forcing_ref[n, c, rows, :] for c in range(2)],
            )
            for n, t in enumerate((0, tiles - 1))
        ]
        for a in range(4):
            start = 8 * i * 4 + a
            edge_ref[pl.ds(start, 8, stride=4), :] = jnp.where(lane < HALF, ends[0][a], ends[1][a])
            if a == 0:
                wall = jnp.broadcast_to(ends[0][0][:, :1], (8, LANES))
            else:
                wall = jnp.full((8, LANES), 1.0 if a == 1 else 0.0, f32)
            wall_ref[pl.ds(start, 8, stride=4), :] = wall
    first, last = cor_ref[0:1, :], cor_ref[tiles - 1 : tiles, :]
    edge_ref[main : main + 8, :] = jnp.broadcast_to(
        jnp.where(lane[:1] < HALF, first, last), (8, LANES)
    )
    turned = jnp.dot(turn, edge_ref[0:main, :], precision=exact, preferred_element_type=f32)
    mirror_ref[0:main, :] = jnp.dot(turned, flip, precision=exact, preferred_element_type=f32)
    mirror_ref[main : main + 8, :] = jnp.dot(
        edge_ref[main : main + 8, :], flip, precision=exact, preferred_element_type=f32
    )


def pack_kernel(
    ice_hbm, forcing_hbm, visc_hbm, mass_hbm, land_hbm, packed_ref, lowest_ref, highest_ref,
    ice_ref, forcing_ref, visc_ref, mass_ref, land_ref, sems,
):
    copies = fetch(
        (ice_hbm, forcing_hbm, visc_hbm, mass_hbm, land_hbm),
        (ice_ref, forcing_ref, visc_ref, mass_ref, land_ref),
        sems,
    )
    width = visc_ref.shape[0]
    tiles = visc_ref.shape[1] // LANES
    tps = tiles // SEGS
    tile_x = lax.axis_index("gx") * width // TILE
    tile_y = lax.axis_index("gy") * tiles
    for copy in copies:
        copy.wait()
    for i in range(width // 8):
        rows = slice(8 * i, 8 * i + 8)
        for t in range(tiles):
            s, k = divmod(t, tps)
            cols = slice(t * LANES, (t + 1) * LANES)
            values = masked(
                ice_ref[tile_y + t, tile_x].astype(f32),
                visc_ref[rows, cols],
                mass_ref[rows, cols],
                land_ref[rows, cols],
                [forcing_ref[c, rows, cols] for c in range(2)],
            )
            for a, value in enumerate(values):
                tile = 8 * i * 2 * tps + (a // 2) * tps + k
                start = tile * 8 + (a % 2) * SEGS + s
                packed_ref[pl.ds(start, 8, stride=2 * tps * 8), :] = value
    side = FINE * 2 * tps * 8
    lowest_ref[...] = packed_ref[0:side, :]
    highest_ref[...] = packed_ref[width * 2 * tps * 8 - side : width * 2 * tps * 8, :]


def edge_kernel(swap_ref, folded_ref, wall_ref, lowest_ref, highest_ref, ext_ref, odd_ref, even_ref):
    is_top = lax.axis_index("gy") == lax.axis_size("gy") - 1
    north = iota(swap_ref.shape, 1) < HALF
    swap = swap_ref[...]
    beyond = jnp.where(
        north, jnp.where(is_top, folded_ref[...], swap), jnp.where(is_top, swap, wall_ref[...])
    )
    ext_ref[...] = beyond
    side = lowest_ref.shape[0]
    main = swap_ref.shape[0] - 8
    even = is_even()
    parts = (
        (slice(0, side), lowest_ref[...], highest_ref[...]),
        (
            slice(side, side + 4 * FINE),
            ext_ref[0 : 4 * FINE, :],
            ext_ref[main - 4 * FINE : main, :],
        ),
    )
    for rows, low, high in parts:
        odd_ref[rows, :] = jnp.where(even, low, high)
        even_ref[rows, :] = jnp.where(even, high, low)


class Shifts:
    def __init__(self, tps):
        self.tps = tps
        self.span = (tps + 1) * LANES
        self.shape = (8, self.span)
        self.lane = iota(self.shape, 1)
        lane = iota((8, LANES), 1)
        row = iota((8, LANES), 0) & (SEGS - 1)
        self.first_half = lane < HALF
        self.low = iota((8, LANES), 0) < SEGS
        self.outer = ((row == SEGS - 1) & (lane < HALF)) | ((row == 0) & (lane >= HALF))
        bottom = lax.axis_index("gy") == 0
        wall = (iota(self.shape, 0) & (SEGS - 1) == 0) & (self.lane >= tps * LANES + HALF) & bottom
        self.weight = jnp.where(wall, 0.0, relax_weight)

    def roll(self, value, shift):
        return pltpu.roll(value, shift % self.span, 1)

    def odd(self, step):
        return self.lane & step != 0

    def pair(self, value, step):
        return value + jnp.where(self.odd(step), self.roll(value, step), self.roll(value, -step))

    def with_halo(self, parts, outside):
        inside = jnp.where(self.first_half, pltpu.roll(parts[0], 7, 0), pltpu.roll(parts[-1], 1, 0))
        return parts + [jnp.where(self.outer, outside, inside)]

    def rotations(self, cor_ref, line):
        parts = [cor_ref[pl.ds(k, SEGS, stride=self.tps), :] for k in range(self.tps)]
        parts = [jnp.concatenate([part, -part], 0) for part in parts]
        line = jnp.broadcast_to(line, (8, LANES))
        rotation = jnp.concatenate(self.with_halo(parts, jnp.where(self.low, line, -line)), 1)
        result = []
        for level in range(LEVELS):
            result.append(rotation)
            rotation = 0.5 * self.pair(rotation, 1 << level)
        return result

    def around(self, now, x, field, east, rotation, step):
        north = now["north"][x]
        west_nb, w, east_nb = field
        return (
            east[1] * east_nb
            + east[0] * west_nb
            + north * self.roll(w, -step)
            + self.roll(north * w, step)
            + rotation * other(w)
        )

    def coefficients(self, now, first, group, step):
        east = [now["east"][first + j - 1] for j in range(group + 1)]
        for j in range(group):
            x = first + j
            north = now["north"][x]
            diag = now["mass"][x] + east[j + 1] + east[j] + north + self.roll(north, step)
            scale = self.weight / diag
            now["scale"][x] = scale
            now["field"][x] = scale * now["right"][x]

    def coarse_east(self, now, fine, target, step):
        target[...] = 0.25 * self.pair(now["east"][fine + 1], step)

    def coarse_sums(self, now, coarse, fine, place, step):
        north = now["north"][fine] + now["north"][fine + 1]
        coarse["north"][place] = 0.25 * jnp.where(self.odd(step), north, self.roll(north, -step))
        coarse["mass"][place] = 0.25 * self.pair(now["mass"][fine] + now["mass"][fine + 1], step)

    def restrict(self, now, coarse, fine, place, group, rotation, step):
        field = [now["field"][fine + j - 1] for j in range(2 * group + 2)]
        east = [now["east"][fine + j - 1] for j in range(2 * group + 1)]
        rest = [
            (1.0 - relax_weight) * now["right"][fine + j]
            + self.around(now, fine + j, field[j : j + 3], east[j : j + 2], rotation, step)
            for j in range(2 * group)
        ]
        for j in range(group):
            coarse["right"][place + j] = 0.25 * self.pair(rest[2 * j] + rest[2 * j + 1], step)

    def sweep(self, now, first, group, value, rotation, step, put):
        field = [value(first + j - 1) for j in range(group + 2)]
        east = [now["east"][first + j - 1] for j in range(group + 1)]
        for j in range(group):
            x = first + j
            near = now["right"][x] + self.around(
                now, x, field[j : j + 3], east[j : j + 2], rotation, step
            )
            put(x, (1.0 - relax_weight) * field[j + 1] + now["scale"][x] * near)


def other(value):
    return pltpu.roll(value, SEGS, 0)


def loop(start, count, body, group=GROUP):
    whole, rest = divmod(count, group)
    if whole == 1:
        body(start, group)
    elif whole:
        lax.fori_loop(0, whole, lambda g, c: (body(start + g * group, group), c)[1], 0)
    if rest:
        body(start + whole * group, rest)


FIRST = ("north", "east", "scale", "right", "field")
STATE = FIRST + ("mass",)
COARSE = ("right", "east", "north", "mass")
AHEAD = ("done", "same", "side", "up", "down", "turn")


def faces(visc, east, first, group):
    value = [visc[first + j] for j in range(group + 1)]
    for j in range(group):
        east[first + j] = 0.5 * (value[j] + value[j + 1])


def unpack(move, visc, top, load, base, ext, index, x):
    tps = move.tps
    rows = [jnp.broadcast_to(ext[4 * index + a : 4 * index + a + 1], (8, LANES)) for a in range(4)]
    both = move.with_halo(
        [load(pl.ds(base + 8 * k, 8)) for k in range(tps)], jnp.where(move.low, rows[0], rows[1])
    )
    turned = [other(part) for part in both]
    value = jnp.concatenate([jnp.where(move.low, a, b) for a, b in zip(both, turned)], 1)
    visc[x] = value
    top["mass"][x] = jnp.concatenate([jnp.where(move.low, b, a) for a, b in zip(both, turned)], 1)
    top["right"][x] = jnp.concatenate(
        move.with_halo(
            [load(pl.ds(base + 8 * (tps + k), 8)) for k in range(tps)],
            jnp.where(move.low, rows[2], rows[3]),
        ),
        1,
    )
    top["north"][x] = 0.5 * (value + move.roll(value, -1))


def coarsen(move, now, coarse, first, group, skip, step, with_east=True, with_sums=True):
    for j in range(group):
        x = 2 * (first + j) + skip
        if with_east:
            coarse["east"][first + j] = 0.25 * move.pair(now["east"][x + 1], step)
        if with_sums:
            move.coarse_sums(now, coarse, x, first + j, step)


def send(move, bottom, sent_ref, columns):
    bit0, bit1 = move.odd(1), move.odd(2)
    for k in columns:
        parts = [bottom[name][k] for name in COARSE]
        sent_ref[k] = jnp.where(
            bit1, jnp.where(bit0, parts[3], parts[2]), jnp.where(bit0, parts[1], parts[0])
        )


def grouped(refs):
    levels = [dict(zip(STATE, refs[6 * n : 6 * n + 6])) for n in range(SPLIT)]
    return levels, refs[6 * SPLIT], refs[6 * SPLIT + 1]


def own_kernel(own_ref, ext_ref, cor_ref, *refs):
    width = (ext_ref.shape[0] - 8) // 4
    tps = cor_ref.shape[0] // SEGS
    move = Shifts(tps)
    (top, level1), visc, sent_ref = grouped(refs)
    rot_ref = refs[6 * SPLIT + 2]
    bottom = dict(zip(COARSE, refs[6 * SPLIT + 3 :]))
    main = ext_ref.shape[0] - 8
    rotations = move.rotations(cor_ref, ext_ref[main : main + 1, :])
    for level in range(LEVELS):
        rot_ref[level] = rotations[level]
    each = 2 * tps * 8

    def own(first, group):
        for j in range(0, group, 2):
            x = first + j
            ext = ext_ref[pl.ds(pl.multiple_of(4 * x, 8), 8), :]
            for index in range(2):
                base = pl.multiple_of((x + index) * each, 8)
                unpack(
                    move, visc, top, lambda rows: own_ref[rows, :], base, ext, index, FINE + x + index
                )

    loop(0, width, own)
    loop(FINE, width - 1, lambda x, n: faces(visc, top["east"], x, n), 16)
    loop(FINE + 1, width - 2, lambda x, n: move.coefficients(top, x, n, 1), 10)
    skip, half, count = FINE // 2, width // 2, width >> SPLIT
    loop(skip, half - 1, lambda x, n: coarsen(move, top, level1, x, n, 0, 1), 15)
    coarsen(move, top, level1, skip + half - 1, 1, 0, 1, with_east=False)
    loop(
        skip + 1, half - 2, lambda x, n: move.restrict(top, level1, 2 * x, x, n, rotations[0], 1), 7
    )
    move.coefficients(level1, skip + 1, half - 2, 2)
    coarsen(move, level1, bottom, 1, count - 2, skip, 2)
    move.restrict(level1, bottom, skip + 2, 1, count - 2, rotations[1], 2)
    send(move, bottom, sent_ref, range(1, count - 1))


def sides_kernel(odd_ref, even_ref, rot_ref, *refs):
    (top, level1), visc, sent_ref = grouped(refs[6 * SPLIT + 2 : 12 * SPLIT + 4])
    bottom = dict(zip(COARSE, refs[12 * SPLIT + 4 :]))
    columns, _, span = visc.shape
    width = columns - 2 * FINE
    tps = span // LANES - 1
    move = Shifts(tps)
    each = 2 * tps * 8
    even = is_even()
    skip, half, count = FINE // 2, columns // 2, width >> SPLIT

    def from_left(rows):
        return jnp.where(even, odd_ref[rows, :], even_ref[rows, :])

    def from_right(rows):
        return jnp.where(even, even_ref[rows, :], odd_ref[rows, :])

    for load, start in ((from_left, 0), (from_right, FINE + width)):
        for j in range(0, FINE, 2):
            ext = load(pl.ds(FINE * each + 4 * j, 8))
            for index in range(2):
                unpack(move, visc, top, load, (j + index) * each, ext, index, start + j + index)
    for start in (0, columns - 1 - FINE):
        faces(visc, top["east"], start, FINE)
    for start in (1, columns - 1 - FINE):
        move.coefficients(top, start, FINE, 1)
    for start in (0, half - 1 - skip):
        coarsen(move, top, level1, start, skip, 0, 1, with_sums=False)
    for start in (1, half - skip):
        coarsen(move, top, level1, start, skip - 1, 0, 1, with_east=False)
    for start in (1, half - 1 - skip):
        move.restrict(top, level1, 2 * start, start, skip, rot_ref[0], 1)
        move.coefficients(level1, start, skip, 2)
    for k in (0, count - 1):
        coarsen(move, level1, bottom, k, 1, skip, 2)
        move.restrict(level1, bottom, skip + 2 * k, k, 1, rot_ref[1], 2)
    send(move, bottom, sent_ref, (0, count - 1))


def ahead_kernel(rot_ref, *refs):
    levels = [dict(zip(FIRST, refs[5 * n : 5 * n + 5])) for n in range(SPLIT)]
    outs = refs[5 * SPLIT :]
    move = Shifts(rot_ref.shape[2] // LANES - 1)
    for level, now in enumerate(levels):
        step = 1 << level
        ahead = dict(zip(AHEAD, outs[6 * level : 6 * level + 6]))
        start = FINE if level == 0 else (FINE >> level) - 1
        count = ahead["done"].shape[0]
        rotation = rot_ref[level]

        def body(first, group, now=now, ahead=ahead, step=step, start=start, level=level, rotation=rotation):
            x0 = first + start
            field = [now["field"][x0 + j - 1] for j in range(group + 2)]
            east = [now["east"][x0 + j - 1] for j in range(group + 1)]
            for j in range(group):
                x, place = x0 + j, first + j
                scale = now["scale"][x]
                north = now["north"][x]
                near = now["right"][x] + move.around(
                    now, x, field[j : j + 3], east[j : j + 2], rotation, step
                )
                ahead["done"][place] = (1.0 - relax_weight) * field[j + 1] + scale * near
                inner, outer = east[j + 1], east[j]
                if (j + level) % 2:
                    inner, outer = outer, inner
                ahead["same"][place] = (1.0 - relax_weight) + scale * inner
                ahead["side"][place] = scale * outer
                ahead["up"][place] = scale * north
                ahead["down"][place] = scale * move.roll(north, step)
                ahead["turn"][place] = scale * rotation

        loop(0, count, body, 8 if level == 0 else 6)


SECOND = ("right", "east", "north", "mass", "scale", "field")


def second_kernel(own_ref, odd_ref, even_ref, rot_ref, *refs):
    aheads = [dict(zip(AHEAD, refs[6 * n : 6 * n + 6])) for n in range(SPLIT)]
    out_hbm = refs[6 * SPLIT]
    rest = list(refs[6 * SPLIT + 1 :])
    flat, out_ref, sems = rest[:3]
    rest = rest[3:]
    levels = [None] * SPLIT
    for _ in range(SPLIT, LEVELS):
        levels.append(dict(zip(SECOND, rest[:6])))
        rest = rest[6:]
    done = rest
    width = out_ref.shape[1]
    tps = out_ref.shape[2] // LANES // SEGS
    tiles = tps * SEGS
    move = Shifts(tps)
    rotations = [rot_ref[level] for level in range(LEVELS)]
    count = width >> SPLIT
    now = levels[SPLIT]
    bit0, bit1 = move.odd(1), move.odd(2)
    even = is_even()
    loads = (
        lambda j: jnp.where(even, odd_ref[j], even_ref[j]),
        lambda j: own_ref[j],
        lambda j: jnp.where(even, even_ref[j], odd_ref[j]),
    )
    for third, load in enumerate(loads):
        start = third * count
        for j in range(count):
            value = load(j)
            evens = jnp.where(bit0, move.roll(value, 1), value)
            odds = jnp.where(bit0, value, move.roll(value, -1))
            for name, part, upper in zip(COARSE, (evens, odds, evens, odds), (0, 0, 1, 1)):
                if upper:
                    now[name][start + j] = jnp.where(bit1, part, move.roll(part, -2))
                else:
                    now[name][start + j] = jnp.where(bit1, move.roll(part, 2), part)
    total = 3 * count
    move.coefficients(now, 1, total - 2, 1 << SPLIT)
    for level in range(SPLIT, LEVELS - 1):
        now, coarse = levels[level], levels[level + 1]
        step = 1 << level
        half = total // 2
        for k in range(half - 1):
            coarse["east"][k] = 0.25 * move.pair(now["east"][2 * k + 1], step)
        for k in range(1, half - 1):
            move.coarse_sums(now, coarse, 2 * k, k, step)
        move.restrict(now, coarse, 2, 1, half - 2, rotations[level], step)
        total = half
        move.coefficients(coarse, 1, total - 2, 2 * step)

    def keep(target):
        def put(x, value):
            target[x] = value

        return put

    level = LEVELS - 1
    last, solved = levels[level], done.pop(0)
    own = width >> level
    move.sweep(
        last, own - 2, own + 4, lambda x: last["field"][x], rotations[level], 1 << level, keep(solved)
    )
    move.sweep(
        last, own - 1, own + 2, lambda x: solved[x], rotations[level], 1 << level, keep(last["field"])
    )
    solved, before = last["field"], own
    for level in reversed(range(SPLIT, LEVELS - 1)):
        now = levels[level]
        own = width >> level

        def value(x, now=now, solved=solved):
            return now["field"][x] + solved[lax.div(x, 2)]

        target = done.pop(0)
        move.sweep(now, own - 1, own + 2, value, rotations[level], 1 << level, keep(target))
        solved, before = target, own

    def correct(ahead, solved, first, count, place, step, put):
        for j in range(count):
            middle = solved[first + j]
            moved = (move.roll(middle, -step), move.roll(middle, step), other(middle))
            for child in range(2):
                x = place + 2 * j + child
                if isinstance(x, int) and not 0 <= x < ahead["done"].shape[0]:
                    continue
                result = (
                    ahead["done"][x]
                    + ahead["same"][x] * middle
                    + ahead["side"][x] * solved[first + j + 2 * child - 1]
                    + ahead["up"][x] * moved[0]
                    + ahead["down"][x] * moved[1]
                    + ahead["turn"][x] * moved[2]
                )
                put(x, result)

    target = done.pop(0)
    correct(aheads[1], solved, before - 1, (width >> SPLIT) + 2, -1, 2, keep(target))

    def put(x, result):
        for k in range(tps):
            row = pl.multiple_of((x * tps + k) * 8, 8)
            flat[pl.ds(row, 8), :] = result[:, k * LANES : (k + 1) * LANES]

    copies = []
    for i in range(width // 8):
        correct(aheads[0], target, 4 * i + 1, 4, 8 * i, 1, put)
        rows = pl.ds(8 * i, 8)
        for c in range(2):
            for t in range(tiles):
                s, k = divmod(t, tps)
                row = (8 * i * tps + k) * 8 + c * SEGS + s
                out_ref[c, rows, t * LANES : (t + 1) * LANES] = flat[pl.ds(row, 8, stride=tps * 8), :]
        copies.append(pltpu.make_async_copy(out_ref.at[:, rows, :], out_hbm.at[:, rows, :], sems.at[i]))
        copies[-1].start()
    for copy in copies:
        copy.wait()


def local(forcing, viscosity, mass, coriolis, land, ice_tiles):
    width, height = viscosity.shape
    tiles = height // LANES
    tps = tiles // SEGS
    each = 2 * tps * 8
    outside = 4 * width + 8
    gx, gy = lax.axis_size("gx"), lax.axis_size("gy")
    lines = coriolis.reshape(tiles, LANES)

    def here(*shape):
        return pltpu.VMEM(shape, f32)

    def call(kernel, outs, args, scratch=(), space=pltpu.VMEM, out_space=pltpu.VMEM, aliases={}):
        return pl.pallas_call(
            kernel,
            out_shape=outs,
            in_specs=[pl.BlockSpec(memory_space=space)] * len(args),
            out_specs=jax.tree.map(lambda _: pl.BlockSpec(memory_space=out_space), outs),
            scratch_shapes=scratch,
            input_output_aliases=aliases,
            compiler_params=pltpu.CompilerParams(vmem_limit_bytes=24 * 1024 * 1024),
        )(*(pltpu.with_memory_space_constraint(arg, space) for arg in args))

    sources = (ice_tiles.T, forcing, viscosity, mass, land, lines)
    ice_space = pltpu.SMEM(sources[0].shape, sources[0].dtype)
    edge, mirror, wall = call(
        ends_kernel,
        (here(outside, LANES),) * 3,
        sources,
        scratch=[ice_space, pltpu.VMEM(lines.shape, f32), pltpu.VMEM((2, 2, width, LANES), f32)]
        + [pltpu.VMEM((2, width, LANES), source.dtype) for source in sources[2:5]]
        + [pltpu.SemaphoreType.DMA((10,))],
        space=pltpu.HBM,
    )
    top = gy - 1
    folded = lax.ppermute(
        mirror, ("gx", "gy"), [(i * gy + top, (gx - 1 - i) * gy + top) for i in range(gx)]
    )
    swap = lax.ppermute(edge, "gy", [(i, gy - 1 - i) for i in range(gy)])
    packed, lowest, highest = call(
        pack_kernel,
        (here(width * each, LANES), here(FINE * each, LANES), here(FINE * each, LANES)),
        sources[:5],
        scratch=[ice_space]
        + [pltpu.VMEM(source.shape, source.dtype) for source in sources[1:5]]
        + [pltpu.SemaphoreType.DMA((5,))],
        space=pltpu.HBM,
    )
    ext, odd, even = call(
        edge_kernel,
        (here(outside, LANES),) + (here(FINE * (each + 4), LANES),) * 2,
        (swap, folded, wall, lowest, highest),
    )
    odd_pairs = [(i, (i + (1 if i % 2 else gx - 1)) % gx) for i in range(gx)]
    even_pairs = [(i, i ^ 1) for i in range(gx)]
    by_odd = lax.ppermute(odd, "gx", odd_pairs)
    by_even = lax.ppermute(even, "gx", even_pairs)

    span = (tps + 1) * LANES
    columns = [(2 * FINE + width) >> level for level in range(SPLIT)]
    columns += [3 * width >> level for level in range(SPLIT, LEVELS)]
    count = width >> SPLIT

    def lines_of(number):
        return here(number, 8, span)

    kept = tuple(lines_of(columns[level]) for level in range(SPLIT) for _ in STATE)
    kept += (lines_of(columns[0]), lines_of(count))
    coarse = [lines_of(count)] * len(COARSE)
    *state, rotation = call(
        own_kernel, kept + (lines_of(LEVELS),), (packed, ext, lines), scratch=coarse
    )
    state = call(
        sides_kernel,
        kept,
        (by_odd, by_even, rotation, *state),
        scratch=coarse,
        aliases={3 + n: n for n in range(len(kept))},
    )
    sent = state[-1]
    by_odd = lax.ppermute(sent, "gx", odd_pairs)
    by_even = lax.ppermute(sent, "gx", even_pairs)
    ahead = call(
        ahead_kernel,
        (lines_of(width),) * len(AHEAD) + (lines_of(width // 2 + 2),) * len(AHEAD),
        (rotation, *(state[len(STATE) * level + n] for level in range(SPLIT) for n in range(len(FIRST)))),
    )
    return call(
        second_kernel,
        jax.ShapeDtypeStruct((2, width, height), f32),
        (sent, by_odd, by_even, rotation, *ahead),
        scratch=[
            pltpu.VMEM((width * tps * 8, LANES), f32),
            pltpu.VMEM((2, width, height), f32),
            pltpu.SemaphoreType.DMA((width // 8,)),
        ]
        + [lines_of(columns[level]) for level in range(SPLIT, LEVELS) for _ in SECOND]
        + [lines_of(columns[level]) for level in reversed(range(SPLIT, LEVELS))]
        + [lines_of(width // 2 + 2)],
        out_space=pltpu.HBM,
    )


def solution(mesh):
    return jax.shard_map(
        local,
        mesh=mesh,
        in_specs=(
            P(None, ("groups", "gx"), "gy"),
            P(("groups", "gx"), "gy"),
            P(("groups", "gx"), "gy"),
            P("gy"),
            P("gx", "gy"),
            P("groups", None),
        ),
        out_specs=P(None, ("groups", "gx"), "gy"),
        check_vma=False,
    )
```

time: 86.7 us -> 82.7 us (0.954)
  waiting for transfers between devices: 8.96 us -> 2.84 us
  starting transfers between devices: 66.8 us -> 68.1 us
    ppermute x1, waiting for transfers between devices: 3.18 us -> 1.15 us  [local(): by_odd = lax.ppermute(sent, 'gx', odd_pairs)]
    ppermute x1, waiting for transfers between devices: 3.39 us -> 1.53 us  [local(): by_even = lax.ppermute(even, 'gx', even_pairs)]
    ppermute x1, waiting for transfers between devices: 1.68 us -> 0.15 us  [local(): lax.ppermute(mirror, ('gx', 'gy'), [(i * gy + top, (gx - 1 - i) * gy + to...]
    ppermute x1, starting transfers between devices: 5.87 us -> 7.08 us  [local(): by_odd = lax.ppermute(sent, 'gx', odd_pairs)]
    pallas_call x4 -> x7, Pallas kernels: 10.5 us -> 11.3 us  [call(): pl.pallas_call(kernel, out_shape=outs, in_specs=[pl.BlockSpec(memory_spac...]
  transfers between devices with their start and end apart: 6 -> 6, of which waited for: 4 -> 3; matrix products, arithmetic and copies ran while one was open for 0% -> 0% of each run, Pallas kernels for 0% -> 6%
where the time goes in v4:
time: 82.7 us; the launch traced here: 82.3 us
  starting transfers between devices  68.1 us (82%)
  Pallas kernels  11.3 us (14%)
  waiting for transfers between devices  2.84 us (3%)
    ppermute x1, starting transfers between devices, local(): swap = lax.ppermute(edge, 'gy', [(i, gy - 1 - i) for i in range(gy)])  43.4 us
    pallas_call x7, Pallas kernels, call(): pl.pallas_call(kernel, out_shape=outs, in_specs=[pl.BlockSpec(memory_spac...  11.3 us
    ppermute x1, starting transfers between devices, local(): by_odd = lax.ppermute(sent, 'gx', odd_pairs)  7.08 us
    ppermute x1, starting transfers between devices, local(): lax.ppermute(mirror, ('gx', 'gy'), [(i * gy + top, (gx - 1 - i) * gy + to...  7 us
    ppermute x1, starting transfers between devices, local(): by_odd = lax.ppermute(odd, 'gx', odd_pairs)  6.71 us
    ppermute x1, starting transfers between devices, local(): by_even = lax.ppermute(sent, 'gx', even_pairs)  1.95 us
    ppermute x1, starting transfers between devices, local(): by_even = lax.ppermute(even, 'gx', even_pairs)  1.95 us
  transfers between devices with their start and end apart: 6, of which 3 were waited for; matrix products, arithmetic and copies ran while one was open for 0% of the time, Pallas kernels for 6%

profile of v4, /device:TPU:65, one launch (start us, length us, event | category | flops | bytes accessed | tf_op | source)
XLA Modules:
  0.0 82.3 jit_solution(2070221182590343226)
XLA Ops:
  0.0 1.4 %shard_map.64 = (f32[136,128]{1,0:T(8,128)S(1)}, f32[136,128]{1,0:T(8,128)S(1)}, f32[136,128]{1,0:T(8,128)S(1)}) custom-call(s32[24,32]{1,0:T(8,128)} %bitcast.4, f32[2,32,1536]{2,1,0:T(8,128)} %forcing_hbm.3, f32[32,1536]{1,0:T(8,128)} %visc_hbm.3, f32[32,1536]{1,0:T(8,128)} %mass_hbm.3, s32[32,1536]{1,0:T(8,128)} %land_hbm.3, f32[12,128]{1,0:T(8,128)} %bitcast.2), custom_call_target="tpu_custom_call" | custom-call | tf_op jit(solution)/shard_map/pallas_call | solution.py:572
  1.4 43.4 %collective-permute-start = (f32[136,128]{1,0:T(8,128)S(1)}, f32[136,128]{1,0:T(8,128)S(1)}, u32[]{:S(2)}, u32[]{:S(2)}) collective-permute-start(f32[136,128]{1,0:T(8,128)S(1)} %get-tuple-element.52), channel_id=1, source_target_pairs={{0,1},{1,0},{2,3},{3,2},{4,5},{5,4},{6,7},{7,6},{8,9},{9,8},{10,11... | collective-permute-start | bytes 208904 | tf_op jit(solution)/shard_map/ppermute | solution.py:597
  44.8 7.0 %collective-permute-start.1 = (f32[136,128]{1,0:T(8,128)S(1)}, f32[136,128]{1,0:T(8,128)S(1)}, u32[]{:S(2)}, u32[]{:S(2)}) collective-permute-start(f32[136,128]{1,0:T(8,128)S(1)} %get-tuple-element.53), channel_id=1, source_target_pairs={{1,255},{3,253},{5,251},{7,249},{9,247},{11,245},{13,243},{15,241}... | collective-permute-start | bytes 208904 | tf_op jit(solution)/shard_map/ppermute | solution.py:594
  51.8 1.5 %shard_map.65 = (f32[1536,128]{1,0:T(8,128)S(1)}, f32[288,128]{1,0:T(8,128)S(1)}, f32[288,128]{1,0:T(8,128)S(1)}) custom-call(s32[24,32]{1,0:T(8,128)} %bitcast.5, f32[2,32,1536]{2,1,0:T(8,128)} %forcing_hbm.3, f32[32,1536]{1,0:T(8,128)} %visc_hbm.3, f32[32,1536]{1,0:T(8,128)} %mass_hbm.3, s32[32,1536]{1,0:T(8,128)} %land_hbm.3), custom_call_target="tpu_custom_call" | custom-call | tf_op jit(solution)/shard_map/pallas_call | solution.py:572
  53.3 0.0 collective-permute-done.swap_ref
  53.3 0.2 collective-permute-done.1.folded_ref
  53.5 0.0 copy-start
  53.5 0.1 shard_map.66
  53.5 6.7 %collective-permute-start.2 = (f32[312,128]{1,0:T(8,128)S(1)}, f32[312,128]{1,0:T(8,128)S(1)}, u32[]{:S(2)}, u32[]{:S(2)}) collective-permute-start(f32[312,128]{1,0:T(8,128)S(1)} %get-tuple-element.57), channel_id=1, source_target_pairs={{0,254},{2,4},{4,2},{6,8},{8,6},{10,12},{12,10},{14,16},{16,14},{1... | collective-permute-start | bytes 479240 | tf_op jit(solution)/shard_map/ppermute | solution.py:614
  60.3 2.0 %collective-permute-start.3 = (f32[312,128]{1,0:T(8,128)S(1)}, f32[312,128]{1,0:T(8,128)S(1)}, u32[]{:S(2)}, u32[]{:S(2)}) collective-permute-start(f32[312,128]{1,0:T(8,128)S(1)} %get-tuple-element.58), channel_id=1, source_target_pairs={{0,2},{2,0},{4,6},{6,4},{8,10},{10,8},{12,14},{14,12},{16,18},{18,... | collective-permute-start | bytes 479240 | tf_op jit(solution)/shard_map/ppermute | solution.py:615
  62.2 0.0 copy-done
  62.2 2.5 %shard_map.67 = (f32[44,8,512]{2,1,0:T(8,128)S(1)}, f32[44,8,512]{2,1,0:T(8,128)S(1)}, f32[44,8,512]{2,1,0:T(8,128)S(1)}, f32[44,8,512]{2,1,0:T(8,128)S(1)}, f32...) custom-call(f32[1536,128]{1,0:T(8,128)S(1)} %get-tuple-element.59.ow, ...), custom_call_target="tpu_custom_call" | custom-call | tf_op jit(solution)/shard_map/pallas_call | solution.py:572
  64.8 0.0 collective-permute-done.2.odd_ref
  64.8 1.5 %collective-permute-done.3.even_ref = f32[312,128]{1,0:T(8,128)S(1)} collective-permute-done((f32[312,128]{1,0:T(8,128)S(1)}, f32[312,128]{1,0:T(8,128)S(1)}, u32[]{:S(2)}, u32[]{:S(2)}) %collective-permute-start.3) | collective-permute-done | bytes 159776 | tf_op jit(solution)/shard_map/ppermute | solution.py:615
  66.3 0.8 shard_map.68
  67.1 2.0 %collective-permute-start.5 = (f32[8,8,512]{2,1,0:T(8,128)S(1)}, f32[8,8,512]{2,1,0:T(8,128)S(1)}, u32[]{:S(2)}, u32[]{:S(2)}) collective-permute-start(f32[8,8,512]{2,1,0:T(8,128)S(1)} %get-tuple-element.76.own_ref), channel_id=1, source_target_pairs={{0,2},{2,0},{4,6},{6,4},{8,10},{10,8},{12,14},{14,12},{16,18},{18,... | collective-permute-start | bytes 393224 | tf_op jit(solution)/shard_map/ppermute | solution.py:640
  69.1 7.1 %collective-permute-start.4 = (f32[8,8,512]{2,1,0:T(8,128)S(1)}, f32[8,8,512]{2,1,0:T(8,128)S(1)}, u32[]{:S(2)}, u32[]{:S(2)}) collective-permute-start(f32[8,8,512]{2,1,0:T(8,128)S(1)} %get-tuple-element.76.own_ref), channel_id=1, source_target_pairs={{0,254},{2,4},{4,2},{6,8},{8,6},{10,12},{12,10},{14,16},{16,14},{1... | collective-permute-start | bytes 393224 | tf_op jit(solution)/shard_map/ppermute | solution.py:639
  76.1 1.2 %shard_map.69 = (f32[32,8,512]{2,1,0:T(8,128)S(1)}, f32[32,8,512]{2,1,0:T(8,128)S(1)}, f32[32,8,512]{2,1,0:T(8,128)S(1)}, f32[32,8,512]{2,1,0:T(8,128)S(1)}, f32...) custom-call(f32[4,8,512]{2,1,0:T(8,128)S(1)} %get-tuple-element.61.r, ...), custom_call_target="tpu_custom_call" | custom-call | tf_op jit(solution)/shard_map/pallas_call | solution.py:572
  77.3 0.0 collective-permute-done.5.even_ref
  77.3 1.1 %collective-permute-done.4.odd_ref = f32[8,8,512]{2,1,0:T(8,128)S(1)} collective-permute-done((f32[8,8,512]{2,1,0:T(8,128)S(1)}, f32[8,8,512]{2,1,0:T(8,128)S(1)}, u32[]{:S(2)}, u32[]{:S(2)}) %collective-permute-start.4) | collective-permute-done | bytes 131104 | tf_op jit(solution)/shard_map/ppermute | solution.py:639
  78.5 3.8 %shard_map.70 = f32[2,32,1536]{2,1,0:T(8,128)} custom-call(f32[8,8,512]{2,1,0:T(8,128)S(1)} %get-tuple-element.76.own_ref, f32[8,8,512]{2,1,0:T(8,128)S(1)} %collective-permute-done.4.odd_ref, f32[8,8,512]{2,1,0:T(8,128)S(1)} %collective-permute-done.5.even_ref, f32[4,8,512]{2,1,0:T(8,128)S(1)} %get-tuple-element.61.rot_ref, ...), custom_call_target="tpu_custom_call" | custom-call | tf_op jit(solution)/shard_map/pallas_call | solution.py:572
Async XLA Ops:
  1.4 51.9 %collective-permute-start = (f32[136,128]{1,0:T(8,128)S(1)}, f32[136,128]{1,0:T(8,128)S(1)}, u32[]{:S(2)}, u32[]{:S(2)}) collective-permute-start(f32[136,128]{1,0:T(8,128)S(1)} %get-tuple-element.52), channel_id=1, source_target_pairs={{0,1},{1,0},{2,3},{3,2},{4,5},{5,4},{6,7},{7,6},{8,9},{9,8},{10,11... | collective-permute-start | bytes 208904 | tf_op jit(solution)/shard_map/ppermute | solution.py:597
  44.8 8.7 %collective-permute-start.1 = (f32[136,128]{1,0:T(8,128)S(1)}, f32[136,128]{1,0:T(8,128)S(1)}, u32[]{:S(2)}, u32[]{:S(2)}) collective-permute-start(f32[136,128]{1,0:T(8,128)S(1)} %get-tuple-element.53), channel_id=1, source_target_pairs={{1,255},{3,253},{5,251},{7,249},{9,247},{11,245},{13,243},{15,241}... | collective-permute-start | bytes 208904 | tf_op jit(solution)/shard_map/ppermute | solution.py:594
  53.5 8.7 %copy-start = (f32[1536]{0:T(1024)S(1)}, f32[1536]{0:T(1024)}, u32[]{:S(2)}) copy-start(f32[1536]{0:T(1024)} %param.9) | copy-start | bytes 18436
  53.5 11.2 %collective-permute-start.2 = (f32[312,128]{1,0:T(8,128)S(1)}, f32[312,128]{1,0:T(8,128)S(1)}, u32[]{:S(2)}, u32[]{:S(2)}) collective-permute-start(f32[312,128]{1,0:T(8,128)S(1)} %get-tuple-element.57), channel_id=1, source_target_pairs={{0,254},{2,4},{4,2},{6,8},{8,6},{10,12},{12,10},{14,16},{16,14},{1... | collective-permute-start | bytes 479240 | tf_op jit(solution)/shard_map/ppermute | solution.py:614
  60.3 6.0 %collective-permute-start.3 = (f32[312,128]{1,0:T(8,128)S(1)}, f32[312,128]{1,0:T(8,128)S(1)}, u32[]{:S(2)}, u32[]{:S(2)}) collective-permute-start(f32[312,128]{1,0:T(8,128)S(1)} %get-tuple-element.58), channel_id=1, source_target_pairs={{0,2},{2,0},{4,6},{6,4},{8,10},{10,8},{12,14},{14,12},{16,18},{18,... | collective-permute-start | bytes 479240 | tf_op jit(solution)/shard_map/ppermute | solution.py:615
  67.1 10.2 %collective-permute-start.5 = (f32[8,8,512]{2,1,0:T(8,128)S(1)}, f32[8,8,512]{2,1,0:T(8,128)S(1)}, u32[]{:S(2)}, u32[]{:S(2)}) collective-permute-start(f32[8,8,512]{2,1,0:T(8,128)S(1)} %get-tuple-element.76.own_ref), channel_id=1, source_target_pairs={{0,2},{2,0},{4,6},{6,4},{8,10},{10,8},{12,14},{14,12},{16,18},{18,... | collective-permute-start | bytes 393224 | tf_op jit(solution)/shard_map/ppermute | solution.py:640
  69.1 9.4 %collective-permute-start.4 = (f32[8,8,512]{2,1,0:T(8,128)S(1)}, f32[8,8,512]{2,1,0:T(8,128)S(1)}, u32[]{:S(2)}, u32[]{:S(2)}) collective-permute-start(f32[8,8,512]{2,1,0:T(8,128)S(1)} %get-tuple-element.76.own_ref), channel_id=1, source_target_pairs={{0,254},{2,4},{4,2},{6,8},{8,6},{10,12},{12,10},{14,16},{16,14},{1... | collective-permute-start | bytes 393224 | tf_op jit(solution)/shard_map/ppermute | solution.py:639

commit v5 on v4

--- a/solution.py
+++ b/solution.py
@@ -19,7 +19,7 @@
 exact = lax.Precision.HIGHEST
 
 
-FINE = 6
+FINE = 8
 SPLIT = 2
 
 
@@ -104,7 +104,7 @@
 
 
 def pack_kernel(
-    ice_hbm, forcing_hbm, visc_hbm, mass_hbm, land_hbm, packed_ref, lowest_ref, highest_ref,
+    ice_hbm, forcing_hbm, visc_hbm, mass_hbm, land_hbm, packed_ref,
     ice_ref, forcing_ref, visc_ref, mass_ref, land_ref, sems,
 ):
     copies = fetch(
@@ -135,33 +135,6 @@
                 tile = 8 * i * 2 * tps + (a // 2) * tps + k
                 start = tile * 8 + (a % 2) * SEGS + s
                 packed_ref[pl.ds(start, 8, stride=2 * tps * 8), :] = value
-    side = FINE * 2 * tps * 8
-    lowest_ref[...] = packed_ref[0:side, :]
-    highest_ref[...] = packed_ref[width * 2 * tps * 8 - side : width * 2 * tps * 8, :]
-
-
-def edge_kernel(swap_ref, folded_ref, wall_ref, lowest_ref, highest_ref, ext_ref, odd_ref, even_ref):
-    is_top = lax.axis_index("gy") == lax.axis_size("gy") - 1
-    north = iota(swap_ref.shape, 1) < HALF
-    swap = swap_ref[...]
-    beyond = jnp.where(
-        north, jnp.where(is_top, folded_ref[...], swap), jnp.where(is_top, swap, wall_ref[...])
-    )
-    ext_ref[...] = beyond
-    side = lowest_ref.shape[0]
-    main = swap_ref.shape[0] - 8
-    even = is_even()
-    parts = (
-        (slice(0, side), lowest_ref[...], highest_ref[...]),
-        (
-            slice(side, side + 4 * FINE),
-            ext_ref[0 : 4 * FINE, :],
-            ext_ref[main - 4 * FINE : main, :],
-        ),
-    )
-    for rows, low, high in parts:
-        odd_ref[rows, :] = jnp.where(even, low, high)
-        even_ref[rows, :] = jnp.where(even, high, low)
 
 
 class Shifts:
@@ -309,32 +282,66 @@
             move.coarse_sums(now, coarse, x, first + j, step)
 
 
-def send(move, bottom, sent_ref, columns):
+def put_packed(move, bottom, column, first, put):
     bit0, bit1 = move.odd(1), move.odd(2)
-    for k in columns:
-        parts = [bottom[name][k] for name in COARSE]
-        sent_ref[k] = jnp.where(
-            bit1, jnp.where(bit0, parts[3], parts[2]), jnp.where(bit0, parts[1], parts[0])
-        )
+    names = ("east", "north", "mass")
+    east, north, mass = (bottom[name][column] for name in names)
+    right = jnp.zeros(move.shape, f32) if first else bottom["right"][column]
+    value = jnp.where(bit1, jnp.where(bit0, mass, north), jnp.where(bit0, east, right))
+    for k in range(move.tps + 1):
+        put(k, value[:, k * LANES : (k + 1) * LANES])
+
+
+def from_packed(move, value):
+    bit0, bit1 = move.odd(1), move.odd(2)
+    evens = jnp.where(bit0, move.roll(value, 1), value)
+    odds = jnp.where(bit0, value, move.roll(value, -1))
+    for name, part, upper in zip(COARSE, (evens, odds, evens, odds), (0, 0, 1, 1)):
+        if upper:
+            yield name, jnp.where(bit1, part, move.roll(part, -2))
+        else:
+            yield name, jnp.where(bit1, move.roll(part, 2), part)
 
 
 def grouped(refs):
     levels = [dict(zip(STATE, refs[6 * n : 6 * n + 6])) for n in range(SPLIT)]
-    return levels, refs[6 * SPLIT], refs[6 * SPLIT + 1]
-
-
-def own_kernel(own_ref, ext_ref, cor_ref, *refs):
-    width = (ext_ref.shape[0] - 8) // 4
+    levels.append(dict(zip(COARSE, refs[6 * SPLIT : 6 * SPLIT + 4])))
+    return levels, refs[6 * SPLIT + 4]
+
+
+KEPT = 6 * SPLIT + 5
+
+
+def own_kernel(own_ref, swap_ref, folded_ref, wall_ref, cor_ref, *refs):
     tps = cor_ref.shape[0] // SEGS
     move = Shifts(tps)
-    (top, level1), visc, sent_ref = grouped(refs)
-    rot_ref = refs[6 * SPLIT + 2]
-    bottom = dict(zip(COARSE, refs[6 * SPLIT + 3 :]))
-    main = ext_ref.shape[0] - 8
+    (top, level1, bottom), visc = grouped(refs)
+    rot_ref, odd_ref, even_ref, ext_ref = refs[KEPT:]
+    main = swap_ref.shape[0] - 8
+    width = main // 4
+    is_top = lax.axis_index("gy") == lax.axis_size("gy") - 1
+    north = iota(swap_ref.shape, 1) < HALF
+    swap = swap_ref[...]
+    ext_ref[...] = jnp.where(
+        north, jnp.where(is_top, folded_ref[...], swap), jnp.where(is_top, swap, wall_ref[...])
+    )
+    even = is_even()
+    each = 2 * tps * 8
+    side, total = FINE * each, width * each
+    parts = (
+        (slice(0, side), own_ref[0:side, :], own_ref[total - side : total, :]),
+        (
+            slice(side, side + 4 * FINE),
+            ext_ref[0 : 4 * FINE, :],
+            ext_ref[main - 4 * FINE : main, :],
+        ),
+    )
+    for rows, low, high in parts:
+        odd_ref[rows, :] = jnp.where(even, low, high)
+        even_ref[rows, :] = jnp.where(even, high, low)
     rotations = move.rotations(cor_ref, ext_ref[main : main + 1, :])
     for level in range(LEVELS):
         rot_ref[level] = rotations[level]
-    each = 2 * tps * 8
 
     def own(first, group):
         for j in range(0, group, 2):
@@ -356,21 +363,91 @@
         skip + 1, half - 2, lambda x, n: move.restrict(top, level1, 2 * x, x, n, rotations[0], 1), 7
     )
     move.coefficients(level1, skip + 1, half - 2, 2)
-    coarsen(move, level1, bottom, 1, count - 2, skip, 2)
-    move.restrict(level1, bottom, skip + 2, 1, count - 2, rotations[1], 2)
-    send(move, bottom, sent_ref, range(1, count - 1))
-
-
-def sides_kernel(odd_ref, even_ref, rot_ref, *refs):
-    (top, level1), visc, sent_ref = grouped(refs[6 * SPLIT + 2 : 12 * SPLIT + 4])
-    bottom = dict(zip(COARSE, refs[12 * SPLIT + 4 :]))
-    columns, _, span = visc.shape
-    width = columns - 2 * FINE
-    tps = span // LANES - 1
+    coarsen(move, level1, bottom, count, count - 1, skip - 2 * count, 2)
+    coarsen(move, level1, bottom, 2 * count - 1, 1, skip - 2 * count, 2, with_east=False)
+    move.restrict(level1, bottom, skip + 2, count + 1, count - 2, rotations[1], 2)
+    for column in range(count - 1):
+
+        def put(k, tile, column=column):
+            row = side + 4 * FINE + (column * (tps + 1) + k) * 8
+            odd_ref[row : row + 8, :] = tile
+            even_ref[row : row + 8, :] = tile
+
+        put_packed(move, bottom, count + column, column == 0, put)
+
+
+def ahead_columns(move, now, ahead, rotation, level, place, group, parity=None):
+    step = 1 << level
+    parity = place % 2 if parity is None else parity
+    x0 = place + (FINE >> level) - level
+    field = [now["field"][x0 + j - 1] for j in range(group + 2)]
+    east = [now["east"][x0 + j - 1] for j in range(group + 1)]
+    for j in range(group):
+        x, at = x0 + j, place + j
+        scale = now["scale"][x]
+        north = now["north"][x]
+        near = now["right"][x] + move.around(now, x, field[j : j + 3], east[j : j + 2], rotation, step)
+        ahead["done"][at] = (1.0 - relax_weight) * field[j + 1] + scale * near
+        inner, outer = east[j + 1], east[j]
+        if (parity + j + level) % 2:
+            inner, outer = outer, inner
+        ahead["same"][at] = (1.0 - relax_weight) + scale * inner
+        ahead["side"][at] = scale * outer
+        ahead["up"][at] = scale * north
+        ahead["down"][at] = scale * move.roll(north, step)
+        ahead["turn"][at] = scale * rotation
+
+
+def aheads_of(refs):
+    return [dict(zip(AHEAD, refs[6 * n : 6 * n + 6])) for n in range(SPLIT)]
+
+
+def ahead_kernel(rot_ref, *refs):
+    levels = [dict(zip(FIRST, refs[5 * n : 5 * n + 5])) for n in range(SPLIT)]
+    aheads = aheads_of(refs[5 * SPLIT :])
+    move = Shifts(rot_ref.shape[2] // LANES - 1)
+    width = aheads[0]["done"].shape[0]
+    loop(
+        2,
+        width - 4,
+        lambda x, n: ahead_columns(move, levels[0], aheads[0], rot_ref[0], 0, x, n, parity=0),
+        14,
+    )
+    loop(
+        3,
+        width // 2 - 4,
+        lambda x, n: ahead_columns(move, levels[1], aheads[1], rot_ref[1], 1, x, n, parity=1),
+        6,
+    )
+
+
+SECOND = ("scale", "field")
+THIRD = ("right", "east", "north", "mass", "scale", "field")
+
+
+def second_kernel(odd_ref, even_ref, rot_ref, *refs):
+    out_hbm = refs[KEPT + 12]
+    refs = list(refs[KEPT + 13 :])
+    levels, visc = grouped(refs)
+    aheads = aheads_of(refs[KEPT:])
+    rest = refs[KEPT + 12 :]
+    flat, out_ref, sems = rest[:3]
+    levels[SPLIT].update(zip(SECOND, rest[3:5]))
+    rest = rest[5:]
+    for _ in range(SPLIT + 1, LEVELS):
+        levels.append(dict(zip(THIRD, rest[:6])))
+        rest = rest[6:]
+    done = rest
+    width = out_ref.shape[1]
+    tps = out_ref.shape[2] // LANES // SEGS
+    tiles = tps * SEGS
     move = Shifts(tps)
+    rotations = [rot_ref[level] for level in range(LEVELS)]
     each = 2 * tps * 8
     even = is_even()
+    columns = visc.shape[0]
     skip, half, count = FINE // 2, columns // 2, width >> SPLIT
+    top, level1, now = levels[: SPLIT + 1]
 
     def from_left(rows):
         return jnp.where(even, odd_ref[rows, :], even_ref[rows, :])
@@ -383,6 +460,15 @@
             ext = load(pl.ds(FINE * each + 4 * j, 8))
             for index in range(2):
                 unpack(move, visc, top, load, (j + index) * each, ext, index, start + j + index)
+    for load, start, columns_sent in (
+        (from_left, 0, range(count - 1)),
+        (from_right, 2 * count, range(1, count - 1)),
+    ):
+        for column in columns_sent:
+            row = FINE * (each + 4) + column * (tps + 1) * 8
+            value = jnp.concatenate([load(pl.ds(row + 8 * k, 8)) for k in range(tps + 1)], 1)
+            for name, part in from_packed(move, value):
+                now[name][start + column] = part
     for start in (0, columns - 1 - FINE):
         faces(visc, top["east"], start, FINE)
     for start in (1, columns - 1 - FINE):
@@ -392,88 +478,17 @@
     for start in (1, half - skip):
         coarsen(move, top, level1, start, skip - 1, 0, 1, with_east=False)
     for start in (1, half - 1 - skip):
-        move.restrict(top, level1, 2 * start, start, skip, rot_ref[0], 1)
+        move.restrict(top, level1, 2 * start, start, skip, rotations[0], 1)
         move.coefficients(level1, start, skip, 2)
-    for k in (0, count - 1):
-        coarsen(move, level1, bottom, k, 1, skip, 2)
-        move.restrict(level1, bottom, skip + 2 * k, k, 1, rot_ref[1], 2)
-    send(move, bottom, sent_ref, (0, count - 1))
-
-
-def ahead_kernel(rot_ref, *refs):
-    levels = [dict(zip(FIRST, refs[5 * n : 5 * n + 5])) for n in range(SPLIT)]
-    outs = refs[5 * SPLIT :]
-    move = Shifts(rot_ref.shape[2] // LANES - 1)
-    for level, now in enumerate(levels):
-        step = 1 << level
-        ahead = dict(zip(AHEAD, outs[6 * level : 6 * level + 6]))
-        start = FINE if level == 0 else (FINE >> level) - 1
-        count = ahead["done"].shape[0]
-        rotation = rot_ref[level]
-
-        def body(first, group, now=now, ahead=ahead, step=step, start=start, level=level, rotation=rotation):
-            x0 = first + start
-            field = [now["field"][x0 + j - 1] for j in range(group + 2)]
-            east = [now["east"][x0 + j - 1] for j in range(group + 1)]
-            for j in range(group):
-                x, place = x0 + j, first + j
-                scale = now["scale"][x]
-                north = now["north"][x]
-                near = now["right"][x] + move.around(
-                    now, x, field[j : j + 3], east[j : j + 2], rotation, step
-                )
-                ahead["done"][place] = (1.0 - relax_weight) * field[j + 1] + scale * near
-                inner, outer = east[j + 1], east[j]
-                if (j + level) % 2:
-                    inner, outer = outer, inner
-                ahead["same"][place] = (1.0 - relax_weight) + scale * inner
-                ahead["side"][place] = scale * outer
-                ahead["up"][place] = scale * north
-                ahead["down"][place] = scale * move.roll(north, step)
-                ahead["turn"][place] = scale * rotation
-
-        loop(0, count, body, 8 if level == 0 else 6)
-
-
-SECOND = ("right", "east", "north", "mass", "scale", "field")
-
-
-def second_kernel(own_ref, odd_ref, even_ref, rot_ref, *refs):
-    aheads = [dict(zip(AHEAD, refs[6 * n : 6 * n + 6])) for n in range(SPLIT)]
-    out_hbm = refs[6 * SPLIT]
-    rest = list(refs[6 * SPLIT + 1 :])
-    flat, out_ref, sems = rest[:3]
-    rest = rest[3:]
-    levels = [None] * SPLIT
-    for _ in range(SPLIT, LEVELS):
-        levels.append(dict(zip(SECOND, rest[:6])))
-        rest = rest[6:]
-    done = rest
-    width = out_ref.shape[1]
-    tps = out_ref.shape[2] // LANES // SEGS
-    tiles = tps * SEGS
-    move = Shifts(tps)
-    rotations = [rot_ref[level] for level in range(LEVELS)]
-    count = width >> SPLIT
-    now = levels[SPLIT]
-    bit0, bit1 = move.odd(1), move.odd(2)
-    even = is_even()
-    loads = (
-        lambda j: jnp.where(even, odd_ref[j], even_ref[j]),
-        lambda j: own_ref[j],
-        lambda j: jnp.where(even, even_ref[j], odd_ref[j]),
-    )
-    for third, load in enumerate(loads):
-        start = third * count
-        for j in range(count):
-            value = load(j)
-            evens = jnp.where(bit0, move.roll(value, 1), value)
-            odds = jnp.where(bit0, value, move.roll(value, -1))
-            for name, part, upper in zip(COARSE, (evens, odds, evens, odds), (0, 0, 1, 1)):
-                if upper:
-                    now[name][start + j] = jnp.where(bit1, part, move.roll(part, -2))
-                else:
-                    now[name][start + j] = jnp.where(bit1, move.roll(part, 2), part)
+    for column in (count - 1, 2 * count):
+        coarsen(move, level1, now, column, 1, skip - 2 * count, 2)
+    coarsen(move, level1, now, 2 * count - 1, 1, skip - 2 * count, 2, with_sums=False)
+    for column in (count - 1, 2 * count - 1):
+        move.restrict(level1, now, 2 * column + skip - 2 * count, column, 2, rotations[1], 2)
+    for place in (0, width - 2):
+        ahead_columns(move, top, aheads[0], rotations[0], 0, place, 2)
+    for place in (0, width // 2 - 1):
+        ahead_columns(move, level1, aheads[1], rotations[1], 1, place, 3)
     total = 3 * count
     move.coefficients(now, 1, total - 2, 1 << SPLIT)
     for level in range(SPLIT, LEVELS - 1):
@@ -568,12 +583,16 @@
     def here(*shape):
         return pltpu.VMEM(shape, f32)
 
-    def call(kernel, outs, args, scratch=(), space=pltpu.VMEM, out_space=pltpu.VMEM, aliases={}):
+    def call(kernel, outs, args, scratch=(), space=pltpu.VMEM, out_spaces=None, aliases={}):
         return pl.pallas_call(
             kernel,
             out_shape=outs,
             in_specs=[pl.BlockSpec(memory_space=space)] * len(args),
-            out_specs=jax.tree.map(lambda _: pl.BlockSpec(memory_space=out_space), outs),
+            out_specs=jax.tree.map(
+                lambda _, where: pl.BlockSpec(memory_space=where),
+                outs,
+                out_spaces or jax.tree.map(lambda _: pltpu.VMEM, outs),
+            ),
             scratch_shapes=scratch,
             input_output_aliases=aliases,
             compiler_params=pltpu.CompilerParams(vmem_limit_bytes=24 * 1024 * 1024),
@@ -595,25 +614,17 @@
         mirror, ("gx", "gy"), [(i * gy + top, (gx - 1 - i) * gy + top) for i in range(gx)]
     )
     swap = lax.ppermute(edge, "gy", [(i, gy - 1 - i) for i in range(gy)])
-    packed, lowest, highest = call(
+    packed = call(
         pack_kernel,
-        (here(width * each, LANES), here(FINE * each, LANES), here(FINE * each, LANES)),
+        here(width * each, LANES),
         sources[:5],
         scratch=[ice_space]
         + [pltpu.VMEM(source.shape, source.dtype) for source in sources[1:5]]
         + [pltpu.SemaphoreType.DMA((5,))],
         space=pltpu.HBM,
     )
-    ext, odd, even = call(
-        edge_kernel,
-        (here(outside, LANES),) + (here(FINE * (each + 4), LANES),) * 2,
-        (swap, folded, wall, lowest, highest),
-    )
     odd_pairs = [(i, (i + (1 if i % 2 else gx - 1)) % gx) for i in range(gx)]
     even_pairs = [(i, i ^ 1) for i in range(gx)]
-    by_odd = lax.ppermute(odd, "gx", odd_pairs)
-    by_even = lax.ppermute(even, "gx", even_pairs)
-
     span = (tps + 1) * LANES
     columns = [(2 * FINE + width) >> level for level in range(SPLIT)]
     columns += [3 * width >> level for level in range(SPLIT, LEVELS)]
@@ -623,40 +634,39 @@
         return here(number, 8, span)
 
     kept = tuple(lines_of(columns[level]) for level in range(SPLIT) for _ in STATE)
-    kept += (lines_of(columns[0]), lines_of(count))
-    coarse = [lines_of(count)] * len(COARSE)
-    *state, rotation = call(
-        own_kernel, kept + (lines_of(LEVELS),), (packed, ext, lines), scratch=coarse
-    )
-    state = call(
-        sides_kernel,
-        kept,
-        (by_odd, by_even, rotation, *state),
-        scratch=coarse,
-        aliases={3 + n: n for n in range(len(kept))},
-    )
-    sent = state[-1]
-    by_odd = lax.ppermute(sent, "gx", odd_pairs)
-    by_even = lax.ppermute(sent, "gx", even_pairs)
+    kept += (lines_of(columns[SPLIT]),) * len(COARSE) + (lines_of(columns[0]),)
+    message = here(FINE * (each + 4) + (count - 1) * (tps + 1) * 8, LANES)
+    *state, rotation, odd, even = call(
+        own_kernel,
+        kept + (lines_of(LEVELS), message, message),
+        (packed, swap, folded, wall, lines),
+        scratch=[here(outside, LANES)],
+    )
+    by_odd = lax.ppermute(odd, "gx", odd_pairs)
+    by_even = lax.ppermute(even, "gx", even_pairs)
+    ahead_shapes = (lines_of(width),) * len(AHEAD) + (lines_of(width // 2 + 2),) * len(AHEAD)
     ahead = call(
         ahead_kernel,
-        (lines_of(width),) * len(AHEAD) + (lines_of(width // 2 + 2),) * len(AHEAD),
+        ahead_shapes,
         (rotation, *(state[len(STATE) * level + n] for level in range(SPLIT) for n in range(len(FIRST)))),
     )
+    out = jax.ShapeDtypeStruct((2, width, height), f32)
     return call(
         second_kernel,
-        jax.ShapeDtypeStruct((2, width, height), f32),
-        (sent, by_odd, by_even, rotation, *ahead),
+        (out,) + kept + ahead_shapes,
+        (by_odd, by_even, rotation, *state, *ahead),
         scratch=[
             pltpu.VMEM((width * tps * 8, LANES), f32),
             pltpu.VMEM((2, width, height), f32),
             pltpu.SemaphoreType.DMA((width // 8,)),
         ]
-        + [lines_of(columns[level]) for level in range(SPLIT, LEVELS) for _ in SECOND]
+        + [lines_of(columns[SPLIT]) for _ in SECOND]
+        + [lines_of(columns[level]) for level in range(SPLIT + 1, LEVELS) for _ in THIRD]
         + [lines_of(columns[level]) for level in reversed(range(SPLIT, LEVELS))]
         + [lines_of(width // 2 + 2)],
-        out_space=pltpu.HBM,
-    )
+        out_spaces=(pltpu.HBM,) + (pltpu.VMEM,) * (KEPT + 12),
+        aliases={3 + n: 1 + n for n in range(KEPT + 12)},
+    )[0]
 
 
 def solution(mesh):

time: 82.7 us -> 75.2 us (0.909)
  starting transfers between devices: 68.1 us -> 59 us
  waiting for transfers between devices: 2.84 us -> 5.21 us
    ppermute x2 -> x0, starting transfers between devices: 9.03 us -> none  [the longest x1 7.08 us: local(): by_odd = lax.ppermute(sent, 'gx', odd_pairs)]
    ppermute x1, waiting for transfers between devices: 1.53 us -> 3.39 us  [local(): by_even = lax.ppermute(even, 'gx', even_pairs)]
    ppermute x1, waiting for transfers between devices: 0.01 us -> 1.63 us  [local(): by_odd = lax.ppermute(odd, 'gx', odd_pairs)]
    ppermute x2 -> x0, waiting for transfers between devices: 1.15 us -> none  [the longest x1 1.15 us: local(): by_odd = lax.ppermute(sent, 'gx', odd_pairs)]
    pallas_call x7 -> x5, Pallas kernels: 11.3 us -> 10.6 us  [call(): pl.pallas_call(kernel, out_shape=outs, in_specs=[pl.BlockSpec(memory_spac...]
  transfers between devices with their start and end apart: 6 -> 4, of which waited for: 3 -> 3; matrix products, arithmetic and copies ran while one was open for 0% -> 0% of each run, Pallas kernels for 6% -> 3%
where the time goes in v5:
time: 75.2 us; the launch traced here: 74.9 us
  starting transfers between devices  59 us (78%)
  Pallas kernels  10.6 us (14%)
  waiting for transfers between devices  5.21 us (7%)
    ppermute x1, starting transfers between devices, local(): swap = lax.ppermute(edge, 'gy', [(i, gy - 1 - i) for i in range(gy)])  43.4 us
    pallas_call x5, Pallas kernels, call(): pl.pallas_call(kernel, out_shape=outs, in_specs=[pl.BlockSpec(memory_spac...  10.6 us
    ppermute x1, starting transfers between devices, local(): lax.ppermute(mirror, ('gx', 'gy'), [(i * gy + top, (gx - 1 - i) * gy + to...  6.99 us
    ppermute x1, starting transfers between devices, local(): by_odd = lax.ppermute(odd, 'gx', odd_pairs)  6.71 us
    ppermute x1, waiting for transfers between devices, local(): by_even = lax.ppermute(even, 'gx', even_pairs)  3.39 us
    ppermute x1, starting transfers between devices, local(): by_even = lax.ppermute(even, 'gx', even_pairs)  1.95 us
    ppermute x1, waiting for transfers between devices, local(): by_odd = lax.ppermute(odd, 'gx', odd_pairs)  1.63 us
  transfers between devices with their start and end apart: 4, of which 3 were waited for; matrix products, arithmetic and copies ran while one was open for 0% of the time, Pallas kernels for 3%

profile of v5, /device:TPU:65, one launch (start us, length us, event | category | flops | bytes accessed | tf_op | source)
XLA Modules:
  0.0 74.9 jit_solution(10271545466577251984)
XLA Ops:
  0.0 1.4 %shard_map.65 = (f32[136,128]{1,0:T(8,128)S(1)}, f32[136,128]{1,0:T(8,128)S(1)}, f32[136,128]{1,0:T(8,128)S(1)}) custom-call(s32[24,32]{1,0:T(8,128)} %bitcast.4, f32[2,32,1536]{2,1,0:T(8,128)} %forcing_hbm.3, f32[32,1536]{1,0:T(8,128)} %visc_hbm.3, f32[32,1536]{1,0:T(8,128)} %mass_hbm.3, s32[32,1536]{1,0:T(8,128)} %land_hbm.3, f32[12,128]{1,0:T(8,128)} %bitcast.2), custom_call_target="tpu_custom_call" | custom-call | tf_op jit(solution)/shard_map/pallas_call | solution.py:587
  1.4 43.4 %collective-permute-start = (f32[136,128]{1,0:T(8,128)S(1)}, f32[136,128]{1,0:T(8,128)S(1)}, u32[]{:S(2)}, u32[]{:S(2)}) collective-permute-start(f32[136,128]{1,0:T(8,128)S(1)} %get-tuple-element.41), channel_id=1, source_target_pairs={{0,1},{1,0},{2,3},{3,2},{4,5},{5,4},{6,7},{7,6},{8,9},{9,8},{10,11... | collective-permute-start | bytes 208904 | tf_op jit(solution)/shard_map/ppermute | solution.py:616
  44.8 0.0 copy-start
  44.8 7.0 %collective-permute-start.1 = (f32[136,128]{1,0:T(8,128)S(1)}, f32[136,128]{1,0:T(8,128)S(1)}, u32[]{:S(2)}, u32[]{:S(2)}) collective-permute-start(f32[136,128]{1,0:T(8,128)S(1)} %get-tuple-element.42), channel_id=1, source_target_pairs={{1,255},{3,253},{5,251},{7,249},{9,247},{11,245},{13,243},{15,241}... | collective-permute-start | bytes 208904 | tf_op jit(solution)/shard_map/ppermute | solution.py:613
  51.8 1.5 %shard_map.64.own_ref = f32[1536,128]{1,0:T(8,128)S(1)} custom-call(s32[24,32]{1,0:T(8,128)} %bitcast.5, f32[2,32,1536]{2,1,0:T(8,128)} %forcing_hbm.3, f32[32,1536]{1,0:T(8,128)} %visc_hbm.3, f32[32,1536]{1,0:T(8,128)} %mass_hbm.3, s32[32,1536]{1,0:T(8,128)} %land_hbm.3), custom_call_target="tpu_custom_call" | custom-call | tf_op jit(solution)/shard_map/pallas_call | solution.py:587
  53.3 0.0 collective-permute-done.swap_ref
  53.3 0.2 collective-permute-done.1.folded_ref
  53.5 0.0 copy-done
  53.5 2.6 %shard_map.66 = (f32[48,8,512]{2,1,0:T(8,128)S(1)}, f32[48,8,512]{2,1,0:T(8,128)S(1)}, f32[48,8,512]{2,1,0:T(8,128)S(1)}, f32[48,8,512]{2,1,0:T(8,128)S(1)}, f32...) custom-call(f32[1536,128]{1,0:T(8,128)S(1)} %shard_map.64.own_ref, ...), custom_call_target="tpu_custom_call" | custom-call | tf_op jit(solution)/shard_map/pallas_call | solution.py:587
  56.1 6.7 %collective-permute-start.2 = (f32[640,128]{1,0:T(8,128)S(1)}, f32[640,128]{1,0:T(8,128)S(1)}, u32[]{:S(2)}, u32[]{:S(2)}) collective-permute-start(f32[640,128]{1,0:T(8,128)S(1)} %get-tuple-element.44), channel_id=1, source_target_pairs={{0,254},{2,4},{4,2},{6,8},{8,6},{10,12},{12,10},{14,16},{16,14},{1... | collective-permute-start | bytes 983048 | tf_op jit(solution)/shard_map/ppermute | solution.py:645
  62.8 2.0 %collective-permute-start.3 = (f32[640,128]{1,0:T(8,128)S(1)}, f32[640,128]{1,0:T(8,128)S(1)}, u32[]{:S(2)}, u32[]{:S(2)}) collective-permute-start(f32[640,128]{1,0:T(8,128)S(1)} %get-tuple-element.45), channel_id=1, source_target_pairs={{0,2},{2,0},{4,6},{6,4},{8,10},{10,8},{12,14},{14,12},{16,18},{18,... | collective-permute-start | bytes 983048 | tf_op jit(solution)/shard_map/ppermute | solution.py:646
  64.7 0.9 %shard_map.67 = (f32[32,8,512]{2,1,0:T(8,128)S(1)}, f32[32,8,512]{2,1,0:T(8,128)S(1)}, f32[32,8,512]{2,1,0:T(8,128)S(1)}, f32[32,8,512]{2,1,0:T(8,128)S(1)}, f32...) custom-call(f32[4,8,512]{2,1,0:T(8,128)S(1)} %get-tuple-element.46.r, ...), custom_call_target="tpu_custom_call" | custom-call | tf_op jit(solution)/shard_map/pallas_call | solution.py:587
  65.6 1.6 %collective-permute-done.2.odd_ref = f32[640,128]{1,0:T(8,128)S(1)} collective-permute-done((f32[640,128]{1,0:T(8,128)S(1)}, f32[640,128]{1,0:T(8,128)S(1)}, u32[]{:S(2)}, u32[]{:S(2)}) %collective-permute-start.2) | collective-permute-done | bytes 327712 | tf_op jit(solution)/shard_map/ppermute | solution.py:645
  67.2 3.4 %collective-permute-done.3.even_ref = f32[640,128]{1,0:T(8,128)S(1)} collective-permute-done((f32[640,128]{1,0:T(8,128)S(1)}, f32[640,128]{1,0:T(8,128)S(1)}, u32[]{:S(2)}, u32[]{:S(2)}) %collective-permute-start.3) | collective-permute-done | bytes 327712 | tf_op jit(solution)/shard_map/ppermute | solution.py:646
  70.6 4.3 %shard_map.68 = (f32[2,32,1536]{2,1,0:T(8,128)}, f32[48,8,512]{2,1,0:T(8,128)S(1)}, f32[48,8,512]{2,1,0:T(8,128)S(1)}, f32[48,8,512]{2,1,0:T(8,128)S(1)}, f32[48...) custom-call(f32[640,128]{1,0:T(8,128)S(1)} %collective-permute-done., ...), custom_call_target="tpu_custom_call", output_to_operand_aliasing={{1}: (3, {}), {2}: (4, {}), {3}: (5, {}), {4}: (6, {}), {5}... | custom-call | tf_op jit(solution)/shard_map/pallas_call | solution.py:587
Async XLA Ops:
  1.4 51.9 %collective-permute-start = (f32[136,128]{1,0:T(8,128)S(1)}, f32[136,128]{1,0:T(8,128)S(1)}, u32[]{:S(2)}, u32[]{:S(2)}) collective-permute-start(f32[136,128]{1,0:T(8,128)S(1)} %get-tuple-element.41), channel_id=1, source_target_pairs={{0,1},{1,0},{2,3},{3,2},{4,5},{5,4},{6,7},{7,6},{8,9},{9,8},{10,11... | collective-permute-start | bytes 208904 | tf_op jit(solution)/shard_map/ppermute | solution.py:616
  44.8 8.7 %copy-start = (f32[1536]{0:T(1024)S(1)}, f32[1536]{0:T(1024)}, u32[]{:S(2)}) copy-start(f32[1536]{0:T(1024)} %param.9) | copy-start | bytes 18436
  44.8 8.7 %collective-permute-start.1 = (f32[136,128]{1,0:T(8,128)S(1)}, f32[136,128]{1,0:T(8,128)S(1)}, u32[]{:S(2)}, u32[]{:S(2)}) collective-permute-start(f32[136,128]{1,0:T(8,128)S(1)} %get-tuple-element.42), channel_id=1, source_target_pairs={{1,255},{3,253},{5,251},{7,249},{9,247},{11,245},{13,243},{15,241}... | collective-permute-start | bytes 208904 | tf_op jit(solution)/shard_map/ppermute | solution.py:613
  56.1 11.2 %collective-permute-start.2 = (f32[640,128]{1,0:T(8,128)S(1)}, f32[640,128]{1,0:T(8,128)S(1)}, u32[]{:S(2)}, u32[]{:S(2)}) collective-permute-start(f32[640,128]{1,0:T(8,128)S(1)} %get-tuple-element.44), channel_id=1, source_target_pairs={{0,254},{2,4},{4,2},{6,8},{8,6},{10,12},{12,10},{14,16},{16,14},{1... | collective-permute-start | bytes 983048 | tf_op jit(solution)/shard_map/ppermute | solution.py:645
  62.8 7.8 %collective-permute-start.3 = (f32[640,128]{1,0:T(8,128)S(1)}, f32[640,128]{1,0:T(8,128)S(1)}, u32[]{:S(2)}, u32[]{:S(2)}) collective-permute-start(f32[640,128]{1,0:T(8,128)S(1)} %get-tuple-element.45), channel_id=1, source_target_pairs={{0,2},{2,0},{4,6},{6,4},{8,10},{10,8},{12,14},{14,12},{16,18},{18,... | collective-permute-start | bytes 983048 | tf_op jit(solution)/shard_map/ppermute | solution.py:646

commit v6 on v5

--- a/solution.py
+++ b/solution.py
@@ -19,7 +19,8 @@
 exact = lax.Precision.HIGHEST
 
 
-FINE = 8
+FINE = 4
+LEAD = 4
 SPLIT = 2
 
 
@@ -49,18 +50,13 @@
     return copies
 
 
-def ends_kernel(
-    ice_hbm, forcing_hbm, visc_hbm, mass_hbm, land_hbm, cor_hbm, edge_ref, mirror_ref, wall_ref,
-    ice_ref, cor_ref, forcing_ref, visc_ref, mass_ref, land_ref, sems,
-):
-    width = visc_hbm.shape[0]
-    tiles = visc_hbm.shape[1] // LANES
-    sources, held = [ice_hbm, cor_hbm], [ice_ref, cor_ref]
-    for n, t in enumerate((0, tiles - 1)):
-        cols = pl.ds(t * LANES, LANES)
-        sources += [forcing_hbm.at[:, :, cols]] + [a.at[:, cols] for a in (visc_hbm, mass_hbm, land_hbm)]
-        held += [a.at[n] for a in (forcing_ref, visc_ref, mass_ref, land_ref)]
-    copies = fetch(sources, held, sems)
+def prepare_kernel(*refs):
+    copies = fetch(refs[:6], refs[10:16], refs[16])
+    packed_ref, edge_ref, mirror_ref, wall_ref = refs[6:10]
+    ice_ref, forcing_ref, visc_ref, mass_ref, land_ref, cor_ref = refs[10:16]
+    width = visc_ref.shape[0]
+    tiles = visc_ref.shape[1] // LANES
+    tps = tiles // SEGS
     tile_x = lax.axis_index("gx") * width // TILE
     tile_y = lax.axis_index("gy") * tiles
     lane = iota((8, LANES), 1)
@@ -74,53 +70,7 @@
         copy.wait()
     for i in range(width // 8):
         rows = slice(8 * i, 8 * i + 8)
-        ends = [
-            masked(
-                ice_ref[tile_y + t, tile_x].astype(f32),
-                visc_ref[n, rows, :],
-                mass_ref[n, rows, :],
-                land_ref[n, rows, :],
-                [forcing_ref[n, c, rows, :] for c in range(2)],
-            )
-            for n, t in enumerate((0, tiles - 1))
-        ]
-        for a in range(4):
-            start = 8 * i * 4 + a
-            edge_ref[pl.ds(start, 8, stride=4), :] = jnp.where(lane < HALF, ends[0][a], ends[1][a])
-            if a == 0:
-                wall = jnp.broadcast_to(ends[0][0][:, :1], (8, LANES))
-            else:
-                wall = jnp.full((8, LANES), 1.0 if a == 1 else 0.0, f32)
-            wall_ref[pl.ds(start, 8, stride=4), :] = wall
-    first, last = cor_ref[0:1, :], cor_ref[tiles - 1 : tiles, :]
-    edge_ref[main : main + 8, :] = jnp.broadcast_to(
-        jnp.where(lane[:1] < HALF, first, last), (8, LANES)
-    )
-    turned = jnp.dot(turn, edge_ref[0:main, :], precision=exact, preferred_element_type=f32)
-    mirror_ref[0:main, :] = jnp.dot(turned, flip, precision=exact, preferred_element_type=f32)
-    mirror_ref[main : main + 8, :] = jnp.dot(
-        edge_ref[main : main + 8, :], flip, precision=exact, preferred_element_type=f32
-    )
-
-
-def pack_kernel(
-    ice_hbm, forcing_hbm, visc_hbm, mass_hbm, land_hbm, packed_ref,
-    ice_ref, forcing_ref, visc_ref, mass_ref, land_ref, sems,
-):
-    copies = fetch(
-        (ice_hbm, forcing_hbm, visc_hbm, mass_hbm, land_hbm),
-        (ice_ref, forcing_ref, visc_ref, mass_ref, land_ref),
-        sems,
-    )
-    width = visc_ref.shape[0]
-    tiles = visc_ref.shape[1] // LANES
-    tps = tiles // SEGS
-    tile_x = lax.axis_index("gx") * width // TILE
-    tile_y = lax.axis_index("gy") * tiles
-    for copy in copies:
-        copy.wait()
-    for i in range(width // 8):
-        rows = slice(8 * i, 8 * i + 8)
+        ends = []
         for t in range(tiles):
             s, k = divmod(t, tps)
             cols = slice(t * LANES, (t + 1) * LANES)
@@ -135,6 +85,25 @@
                 tile = 8 * i * 2 * tps + (a // 2) * tps + k
                 start = tile * 8 + (a % 2) * SEGS + s
                 packed_ref[pl.ds(start, 8, stride=2 * tps * 8), :] = value
+            if t in (0, tiles - 1):
+                ends.append(values)
+        for a in range(4):
+            start = 8 * i * 4 + a
+            edge_ref[pl.ds(start, 8, stride=4), :] = jnp.where(lane < HALF, ends[0][a], ends[1][a])
+            if a == 0:
+                wall = jnp.broadcast_to(ends[0][0][:, :1], (8, LANES))
+            else:
+                wall = jnp.full((8, LANES), 1.0 if a == 1 else 0.0, f32)
+            wall_ref[pl.ds(start, 8, stride=4), :] = wall
+    first, last = cor_ref[0:1, :], cor_ref[tiles - 1 : tiles, :]
+    edge_ref[main : main + 8, :] = jnp.broadcast_to(
+        jnp.where(lane[:1] < HALF, first, last), (8, LANES)
+    )
+    turned = jnp.dot(turn, edge_ref[0:main, :], precision=exact, preferred_element_type=f32)
+    mirror_ref[0:main, :] = jnp.dot(turned, flip, precision=exact, preferred_element_type=f32)
+    mirror_ref[main : main + 8, :] = jnp.dot(
+        edge_ref[main : main + 8, :], flip, precision=exact, preferred_element_type=f32
+    )
 
 
 class Shifts:
@@ -143,6 +112,7 @@
         self.span = (tps + 1) * LANES
         self.shape = (8, self.span)
         self.lane = iota(self.shape, 1)
+        self.upper = iota(self.shape, 0) >= SEGS
         lane = iota((8, LANES), 1)
         row = iota((8, LANES), 0) & (SEGS - 1)
         self.first_half = lane < HALF
@@ -282,25 +252,55 @@
             move.coarse_sums(now, coarse, x, first + j, step)
 
 
+def evens_of(move, value):
+    return jnp.where(move.odd(1), move.roll(value, 1), value)
+
+
+def odds_of(move, value):
+    return jnp.where(move.odd(1), value, move.roll(value, -1))
+
+
 def put_packed(move, bottom, column, first, put):
     bit0, bit1 = move.odd(1), move.odd(2)
     names = ("east", "north", "mass")
     east, north, mass = (bottom[name][column] for name in names)
     right = jnp.zeros(move.shape, f32) if first else bottom["right"][column]
-    value = jnp.where(bit1, jnp.where(bit0, mass, north), jnp.where(bit0, east, right))
-    for k in range(move.tps + 1):
-        put(k, value[:, k * LANES : (k + 1) * LANES])
+    put(jnp.where(bit1, jnp.where(bit0, mass, north), jnp.where(bit0, east, right)))
 
 
 def from_packed(move, value):
-    bit0, bit1 = move.odd(1), move.odd(2)
-    evens = jnp.where(bit0, move.roll(value, 1), value)
-    odds = jnp.where(bit0, value, move.roll(value, -1))
+    bit1 = move.odd(2)
+    evens, odds = evens_of(move, value), odds_of(move, value)
     for name, part, upper in zip(COARSE, (evens, odds, evens, odds), (0, 0, 1, 1)):
         if upper:
             yield name, jnp.where(bit1, part, move.roll(part, -2))
         else:
             yield name, jnp.where(bit1, move.roll(part, 2), part)
+
+
+def middle_packed(move, level1, column):
+    bit0 = move.odd(1)
+    values = []
+    for x in (column, column + 1):
+        coefficients = jnp.where(move.upper, level1["north"][x], level1["east"][x])
+        values.append(jnp.where(bit0, coefficients, level1["right"][x]))
+    masses = jnp.where(move.upper, level1["mass"][column + 1], level1["mass"][column])
+    return values + [jnp.where(bit0, level1["east"][column - 1], masses)]
+
+
+def middle_unpacked(move, level1, column, values, west):
+    for x, value in zip((column, column + 1), values):
+        level1["right"][x] = evens_of(move, value)
+        both = odds_of(move, value)
+        turned = other(both)
+        level1["east"][x] = jnp.where(move.upper, turned, both)
+        level1["north"][x] = jnp.where(move.upper, both, turned)
+    both = evens_of(move, values[2])
+    turned = other(both)
+    level1["mass"][column] = jnp.where(move.upper, turned, both)
+    level1["mass"][column + 1] = jnp.where(move.upper, both, turned)
+    if west:
+        level1["east"][column - 1] = odds_of(move, values[2])
 
 
 def grouped(refs):
@@ -356,30 +356,44 @@
     loop(0, width, own)
     loop(FINE, width - 1, lambda x, n: faces(visc, top["east"], x, n), 16)
     loop(FINE + 1, width - 2, lambda x, n: move.coefficients(top, x, n, 1), 10)
-    skip, half, count = FINE // 2, width // 2, width >> SPLIT
-    loop(skip, half - 1, lambda x, n: coarsen(move, top, level1, x, n, 0, 1), 15)
-    coarsen(move, top, level1, skip + half - 1, 1, 0, 1, with_east=False)
+    skip, half, count = FINE - 2 * LEAD, width // 2, width >> SPLIT
+    loop(LEAD, half - 1, lambda x, n: coarsen(move, top, level1, x, n, skip, 1), 15)
+    coarsen(move, top, level1, LEAD + half - 1, 1, skip, 1, with_east=False)
     loop(
-        skip + 1, half - 2, lambda x, n: move.restrict(top, level1, 2 * x, x, n, rotations[0], 1), 7
-    )
-    move.coefficients(level1, skip + 1, half - 2, 2)
-    coarsen(move, level1, bottom, count, count - 1, skip - 2 * count, 2)
-    coarsen(move, level1, bottom, 2 * count - 1, 1, skip - 2 * count, 2, with_east=False)
-    move.restrict(level1, bottom, skip + 2, count + 1, count - 2, rotations[1], 2)
+        LEAD + 1,
+        half - 2,
+        lambda x, n: move.restrict(top, level1, 2 * x + skip, x, n, rotations[0], 1),
+        7,
+    )
+    move.coefficients(level1, LEAD + 1, half - 2, 2)
+    skip = LEAD - 2 * count
+    coarsen(move, level1, bottom, count, count - 1, skip, 2)
+    coarsen(move, level1, bottom, 2 * count - 1, 1, skip, 2, with_east=False)
+    move.restrict(level1, bottom, LEAD + 2, count + 1, count - 2, rotations[1], 2)
+
+    def put(ref, column, value):
+        for k in range(tps + 1):
+            row = side + 4 * FINE + (column * (tps + 1) + k) * 8
+            ref[row : row + 8, :] = value[:, k * LANES : (k + 1) * LANES]
+
+    lows = middle_packed(move, level1, LEAD + 1)
+    highs = middle_packed(move, level1, LEAD + half - 3)
+    for n, (low, high) in enumerate(zip(lows, highs)):
+        put(odd_ref, n, jnp.where(even, low, high))
+        put(even_ref, n, jnp.where(even, high, low))
     for column in range(count - 1):
 
-        def put(k, tile, column=column):
-            row = side + 4 * FINE + (column * (tps + 1) + k) * 8
-            odd_ref[row : row + 8, :] = tile
-            even_ref[row : row + 8, :] = tile
-
-        put_packed(move, bottom, count + column, column == 0, put)
+        def put_both(value, column=column):
+            put(odd_ref, 3 + column, value)
+            put(even_ref, 3 + column, value)
+
+        put_packed(move, bottom, count + column, column == 0, put_both)
 
 
 def ahead_columns(move, now, ahead, rotation, level, place, group, parity=None):
     step = 1 << level
     parity = place % 2 if parity is None else parity
-    x0 = place + (FINE >> level) - level
+    x0 = place + (FINE, LEAD - 1)[level]
     field = [now["field"][x0 + j - 1] for j in range(group + 2)]
     east = [now["east"][x0 + j - 1] for j in range(group + 1)]
     for j in range(group):
@@ -445,8 +459,7 @@
     rotations = [rot_ref[level] for level in range(LEVELS)]
     each = 2 * tps * 8
     even = is_even()
-    columns = visc.shape[0]
-    skip, half, count = FINE // 2, columns // 2, width >> SPLIT
+    columns, count, half = visc.shape[0], width >> SPLIT, width // 2
     top, level1, now = levels[: SPLIT + 1]
 
     def from_left(rows):
@@ -460,31 +473,40 @@
             ext = load(pl.ds(FINE * each + 4 * j, 8))
             for index in range(2):
                 unpack(move, visc, top, load, (j + index) * each, ext, index, start + j + index)
+
+    def received(load, column):
+        row = FINE * (each + 4) + column * (tps + 1) * 8
+        return jnp.concatenate([load(pl.ds(row + 8 * k, 8)) for k in range(tps + 1)], 1)
+
+    middle_unpacked(move, level1, 1, [received(from_left, n) for n in range(3)], True)
+    middle_unpacked(
+        move, level1, LEAD + half + 1, [received(from_right, n) for n in range(3)], False
+    )
     for load, start, columns_sent in (
         (from_left, 0, range(count - 1)),
         (from_right, 2 * count, range(1, count - 1)),
     ):
         for column in columns_sent:
-            row = FINE * (each + 4) + column * (tps + 1) * 8
-            value = jnp.concatenate([load(pl.ds(row + 8 * k, 8)) for k in range(tps + 1)], 1)
-            for name, part in from_packed(move, value):
+            for name, part in from_packed(move, received(load, 3 + column)):
                 now[name][start + column] = part
     for start in (0, columns - 1 - FINE):
         faces(visc, top["east"], start, FINE)
     for start in (1, columns - 1 - FINE):
         move.coefficients(top, start, FINE, 1)
-    for start in (0, half - 1 - skip):
-        coarsen(move, top, level1, start, skip, 0, 1, with_sums=False)
-    for start in (1, half - skip):
-        coarsen(move, top, level1, start, skip - 1, 0, 1, with_east=False)
-    for start in (1, half - 1 - skip):
-        move.restrict(top, level1, 2 * start, start, skip, rotations[0], 1)
-        move.coefficients(level1, start, skip, 2)
+    skip = FINE - 2 * LEAD
+    for column in (LEAD - 1, LEAD + half):
+        coarsen(move, top, level1, column, 1, skip, 1)
+    coarsen(move, top, level1, LEAD + half - 1, 1, skip, 1, with_sums=False)
+    for column in (LEAD - 1, LEAD + half - 1):
+        move.restrict(top, level1, 2 * column + skip, column, 2, rotations[0], 1)
+    for column in (1, LEAD + half - 1):
+        move.coefficients(level1, column, 4, 2)
+    skip = LEAD - 2 * count
     for column in (count - 1, 2 * count):
-        coarsen(move, level1, now, column, 1, skip - 2 * count, 2)
-    coarsen(move, level1, now, 2 * count - 1, 1, skip - 2 * count, 2, with_sums=False)
+        coarsen(move, level1, now, column, 1, skip, 2)
+    coarsen(move, level1, now, 2 * count - 1, 1, skip, 2, with_sums=False)
     for column in (count - 1, 2 * count - 1):
-        move.restrict(level1, now, 2 * column + skip - 2 * count, column, 2, rotations[1], 2)
+        move.restrict(level1, now, 2 * column + skip, column, 2, rotations[1], 2)
     for place in (0, width - 2):
         ahead_columns(move, top, aheads[0], rotations[0], 0, place, 2)
     for place in (0, width // 2 - 1):
@@ -599,14 +621,13 @@
         )(*(pltpu.with_memory_space_constraint(arg, space) for arg in args))
 
     sources = (ice_tiles.T, forcing, viscosity, mass, land, lines)
-    ice_space = pltpu.SMEM(sources[0].shape, sources[0].dtype)
-    edge, mirror, wall = call(
-        ends_kernel,
-        (here(outside, LANES),) * 3,
+    packed, edge, mirror, wall = call(
+        prepare_kernel,
+        (here(width * each, LANES),) + (here(outside, LANES),) * 3,
         sources,
-        scratch=[ice_space, pltpu.VMEM(lines.shape, f32), pltpu.VMEM((2, 2, width, LANES), f32)]
-        + [pltpu.VMEM((2, width, LANES), source.dtype) for source in sources[2:5]]
-        + [pltpu.SemaphoreType.DMA((10,))],
+        scratch=[pltpu.SMEM(sources[0].shape, sources[0].dtype)]
+        + [pltpu.VMEM(source.shape, source.dtype) for source in sources[1:]]
+        + [pltpu.SemaphoreType.DMA((len(sources),))],
         space=pltpu.HBM,
     )
     top = gy - 1
@@ -614,19 +635,10 @@
         mirror, ("gx", "gy"), [(i * gy + top, (gx - 1 - i) * gy + top) for i in range(gx)]
     )
     swap = lax.ppermute(edge, "gy", [(i, gy - 1 - i) for i in range(gy)])
-    packed = call(
-        pack_kernel,
-        here(width * each, LANES),
-        sources[:5],
-        scratch=[ice_space]
-        + [pltpu.VMEM(source.shape, source.dtype) for source in sources[1:5]]
-        + [pltpu.SemaphoreType.DMA((5,))],
-        space=pltpu.HBM,
-    )
     odd_pairs = [(i, (i + (1 if i % 2 else gx - 1)) % gx) for i in range(gx)]
     even_pairs = [(i, i ^ 1) for i in range(gx)]
     span = (tps + 1) * LANES
-    columns = [(2 * FINE + width) >> level for level in range(SPLIT)]
+    columns = [2 * FINE + width, 2 * LEAD + width // 2]
     columns += [3 * width >> level for level in range(SPLIT, LEVELS)]
     count = width >> SPLIT
 
@@ -635,7 +647,7 @@
 
     kept = tuple(lines_of(columns[level]) for level in range(SPLIT) for _ in STATE)
     kept += (lines_of(columns[SPLIT]),) * len(COARSE) + (lines_of(columns[0]),)
-    message = here(FINE * (each + 4) + (count - 1) * (tps + 1) * 8, LANES)
+    message = here(FINE * (each + 4) + (count + 2) * (tps + 1) * 8, LANES)
     *state, rotation, odd, even = call(
         own_kernel,
         kept + (lines_of(LEVELS), message, message),

time: 75.2 us -> 74.8 us (level)
  Pallas kernels: 10.6 us -> 9.44 us
  waiting for transfers between devices: 5.21 us -> 6.1 us
    ppermute x1, waiting for transfers between devices: 0.18 us -> 1.68 us  [local(): lax.ppermute(mirror, ('gx', 'gy'), [(i * gy + top, (gx - 1 - i) * gy + to...]
    pallas_call x5 -> x4, Pallas kernels: 10.6 us -> 9.44 us  [call(): pl.pallas_call(kernel, out_shape=outs, in_specs=[pl.BlockSpec(memory_spac...]
  transfers between devices with their start and end apart: 4 -> 4, of which waited for: 3 -> 3; matrix products, arithmetic and copies ran while one was open for 0% -> 0% of each run, Pallas kernels for 3% -> 1%
where the time goes in v6:
time: 74.8 us; the launch traced here: 74.6 us
  starting transfers between devices  59 us (79%)
  Pallas kernels  9.44 us (13%)
  waiting for transfers between devices  6.1 us (8%)
    ppermute x1, starting transfers between devices, local(): swap = lax.ppermute(edge, 'gy', [(i, gy - 1 - i) for i in range(gy)])  43.4 us
    pallas_call x4, Pallas kernels, call(): pl.pallas_call(kernel, out_shape=outs, in_specs=[pl.BlockSpec(memory_spac...  9.44 us
    ppermute x1, starting transfers between devices, local(): lax.ppermute(mirror, ('gx', 'gy'), [(i * gy + top, (gx - 1 - i) * gy + to...  7 us
    ppermute x1, starting transfers between devices, local(): by_odd = lax.ppermute(odd, 'gx', odd_pairs)  6.7 us
    ppermute x1, waiting for transfers between devices, local(): by_even = lax.ppermute(even, 'gx', even_pairs)  3.39 us
    ppermute x1, starting transfers between devices, local(): by_even = lax.ppermute(even, 'gx', even_pairs)  1.95 us
    ppermute x1, waiting for transfers between devices, local(): lax.ppermute(mirror, ('gx', 'gy'), [(i * gy + top, (gx - 1 - i) * gy + to...  1.68 us
  transfers between devices with their start and end apart: 4, of which 3 were waited for; matrix products, arithmetic and copies ran while one was open for 0% of the time, Pallas kernels for 1%

profile of v6, /device:TPU:65, one launch (start us, length us, event | category | flops | bytes accessed | tf_op | source)
XLA Modules:
  0.0 74.6 jit_solution(11361617669178524457)
XLA Ops:
  0.0 0.0 copy-start
  0.0 1.9 %shard_map.64 = (f32[1536,128]{1,0:T(8,128)S(1)}, f32[136,128]{1,0:T(8,128)S(1)}, f32[136,128]{1,0:T(8,128)S(1)}, f32[136,128]{1,0:T(8,128)S(1)}) custom-call(s32[24,32]{1,0:T(8,128)} %bitcast.4, f32[2,32,1536]{2,1,0:T(8,128)} %refs_1_.1, f32[32,1536]{1,0:T(8,128)} %refs_2_.1, f32[32,1536]{1,0:T(8,128)} %refs_3_.1, s32[32,1536]{1,0:T(8,128)} %refs_4_.1, ...), custom_call_target="tpu_custom_call" | custom-call | tf_op jit(solution)/shard_map/pallas_call | solution.py:609
  2.0 43.4 %collective-permute-start = (f32[136,128]{1,0:T(8,128)S(1)}, f32[136,128]{1,0:T(8,128)S(1)}, u32[]{:S(2)}, u32[]{:S(2)}) collective-permute-start(f32[136,128]{1,0:T(8,128)S(1)} %get-tuple-element.43), channel_id=1, source_target_pairs={{0,1},{1,0},{2,3},{3,2},{4,5},{5,4},{6,7},{7,6},{8,9},{9,8},{10,11... | collective-permute-start | bytes 208904 | tf_op jit(solution)/shard_map/ppermute | solution.py:637
  45.3 7.0 %collective-permute-start.1 = (f32[136,128]{1,0:T(8,128)S(1)}, f32[136,128]{1,0:T(8,128)S(1)}, u32[]{:S(2)}, u32[]{:S(2)}) collective-permute-start(f32[136,128]{1,0:T(8,128)S(1)} %get-tuple-element.44), channel_id=1, source_target_pairs={{1,255},{3,253},{5,251},{7,249},{9,247},{11,245},{13,243},{15,241}... | collective-permute-start | bytes 208904 | tf_op jit(solution)/shard_map/ppermute | solution.py:634
  52.3 0.0 collective-permute-done.swap_ref
  52.3 1.7 %collective-permute-done.1.folded_ref = f32[136,128]{1,0:T(8,128)S(1)} collective-permute-done((f32[136,128]{1,0:T(8,128)S(1)}, f32[136,128]{1,0:T(8,128)S(1)}, u32[]{:S(2)}, u32[]{:S(2)}) %collective-permute-start.1) | collective-permute-done | bytes 69664 | tf_op jit(solution)/shard_map/ppermute | solution.py:634
  54.0 0.0 copy-done
  54.0 2.6 %shard_map.65 = (f32[40,8,512]{2,1,0:T(8,128)S(1)}, f32[40,8,512]{2,1,0:T(8,128)S(1)}, f32[40,8,512]{2,1,0:T(8,128)S(1)}, f32[40,8,512]{2,1,0:T(8,128)S(1)}, f32...) custom-call(f32[1536,128]{1,0:T(8,128)S(1)} %get-tuple-element.42.ow, ...), custom_call_target="tpu_custom_call" | custom-call | tf_op jit(solution)/shard_map/pallas_call | solution.py:609
  56.6 6.7 %collective-permute-start.2 = (f32[528,128]{1,0:T(8,128)S(1)}, f32[528,128]{1,0:T(8,128)S(1)}, u32[]{:S(2)}, u32[]{:S(2)}) collective-permute-start(f32[528,128]{1,0:T(8,128)S(1)} %get-tuple-element.46), channel_id=1, source_target_pairs={{0,254},{2,4},{4,2},{6,8},{8,6},{10,12},{12,10},{14,16},{16,14},{1... | collective-permute-start | bytes 811016 | tf_op jit(solution)/shard_map/ppermute | solution.py:657
  63.3 2.0 %collective-permute-start.3 = (f32[528,128]{1,0:T(8,128)S(1)}, f32[528,128]{1,0:T(8,128)S(1)}, u32[]{:S(2)}, u32[]{:S(2)}) collective-permute-start(f32[528,128]{1,0:T(8,128)S(1)} %get-tuple-element.47), channel_id=1, source_target_pairs={{0,2},{2,0},{4,6},{6,4},{8,10},{10,8},{12,14},{14,12},{16,18},{18,... | collective-permute-start | bytes 811016 | tf_op jit(solution)/shard_map/ppermute | solution.py:658
  65.3 0.9 %shard_map.66 = (f32[32,8,512]{2,1,0:T(8,128)S(1)}, f32[32,8,512]{2,1,0:T(8,128)S(1)}, f32[32,8,512]{2,1,0:T(8,128)S(1)}, f32[32,8,512]{2,1,0:T(8,128)S(1)}, f32...) custom-call(f32[4,8,512]{2,1,0:T(8,128)S(1)} %get-tuple-element.48.r, ...), custom_call_target="tpu_custom_call" | custom-call | tf_op jit(solution)/shard_map/pallas_call | solution.py:609
  66.1 1.0 %collective-permute-done.2.odd_ref = f32[528,128]{1,0:T(8,128)S(1)} collective-permute-done((f32[528,128]{1,0:T(8,128)S(1)}, f32[528,128]{1,0:T(8,128)S(1)}, u32[]{:S(2)}, u32[]{:S(2)}) %collective-permute-start.2) | collective-permute-done | bytes 270368 | tf_op jit(solution)/shard_map/ppermute | solution.py:657
  67.2 3.4 %collective-permute-done.3.even_ref = f32[528,128]{1,0:T(8,128)S(1)} collective-permute-done((f32[528,128]{1,0:T(8,128)S(1)}, f32[528,128]{1,0:T(8,128)S(1)}, u32[]{:S(2)}, u32[]{:S(2)}) %collective-permute-start.3) | collective-permute-done | bytes 270368 | tf_op jit(solution)/shard_map/ppermute | solution.py:658
  70.6 4.1 %shard_map.67 = (f32[2,32,1536]{2,1,0:T(8,128)}, f32[40,8,512]{2,1,0:T(8,128)S(1)}, f32[40,8,512]{2,1,0:T(8,128)S(1)}, f32[40,8,512]{2,1,0:T(8,128)S(1)}, f32[40...) custom-call(f32[528,128]{1,0:T(8,128)S(1)} %collective-permute-done., ...), custom_call_target="tpu_custom_call", output_to_operand_aliasing={{1}: (3, {}), {2}: (4, {}), {3}: (5, {}), {4}: (6, {}), {5}... | custom-call | tf_op jit(solution)/shard_map/pallas_call | solution.py:609
Async XLA Ops:
  0.0 54.0 %copy-start = (f32[1536]{0:T(1024)S(1)}, f32[1536]{0:T(1024)}, u32[]{:S(2)}) copy-start(f32[1536]{0:T(1024)} %param.9) | copy-start | bytes 18436
  2.0 50.4 %collective-permute-start = (f32[136,128]{1,0:T(8,128)S(1)}, f32[136,128]{1,0:T(8,128)S(1)}, u32[]{:S(2)}, u32[]{:S(2)}) collective-permute-start(f32[136,128]{1,0:T(8,128)S(1)} %get-tuple-element.43), channel_id=1, source_target_pairs={{0,1},{1,0},{2,3},{3,2},{4,5},{5,4},{6,7},{7,6},{8,9},{9,8},{10,11... | collective-permute-start | bytes 208904 | tf_op jit(solution)/shard_map/ppermute | solution.py:637
  45.3 8.7 %collective-permute-start.1 = (f32[136,128]{1,0:T(8,128)S(1)}, f32[136,128]{1,0:T(8,128)S(1)}, u32[]{:S(2)}, u32[]{:S(2)}) collective-permute-start(f32[136,128]{1,0:T(8,128)S(1)} %get-tuple-element.44), channel_id=1, source_target_pairs={{1,255},{3,253},{5,251},{7,249},{9,247},{11,245},{13,243},{15,241}... | collective-permute-start | bytes 208904 | tf_op jit(solution)/shard_map/ppermute | solution.py:634
  56.6 10.6 %collective-permute-start.2 = (f32[528,128]{1,0:T(8,128)S(1)}, f32[528,128]{1,0:T(8,128)S(1)}, u32[]{:S(2)}, u32[]{:S(2)}) collective-permute-start(f32[528,128]{1,0:T(8,128)S(1)} %get-tuple-element.46), channel_id=1, source_target_pairs={{0,254},{2,4},{4,2},{6,8},{8,6},{10,12},{12,10},{14,16},{16,14},{1... | collective-permute-start | bytes 811016 | tf_op jit(solution)/shard_map/ppermute | solution.py:657
  63.3 7.2 %collective-permute-start.3 = (f32[528,128]{1,0:T(8,128)S(1)}, f32[528,128]{1,0:T(8,128)S(1)}, u32[]{:S(2)}, u32[]{:S(2)}) collective-permute-start(f32[528,128]{1,0:T(8,128)S(1)} %get-tuple-element.47), channel_id=1, source_target_pairs={{0,2},{2,0},{4,6},{6,4},{8,10},{10,8},{12,14},{14,12},{16,18},{18,... | collective-permute-start | bytes 811016 | tf_op jit(solution)/shard_map/ppermute | solution.py:658

commit v7 on v6

--- a/solution.py
+++ b/solution.py
@@ -51,12 +51,13 @@
 
 
 def prepare_kernel(*refs):
-    copies = fetch(refs[:6], refs[10:16], refs[16])
-    packed_ref, edge_ref, mirror_ref, wall_ref = refs[6:10]
-    ice_ref, forcing_ref, visc_ref, mass_ref, land_ref, cor_ref = refs[10:16]
+    held = (refs[15],) + refs[9:14]
+    copies = fetch(refs[:6], held, refs[16])
+    edge_ref, mirror_ref, wall_ref, ice_ref = refs[6:9] + refs[14:15]
+    forcing_ref, visc_ref, mass_ref, land_ref, cor_ref = refs[9:14]
+    ice_place = refs[15]
     width = visc_ref.shape[0]
     tiles = visc_ref.shape[1] // LANES
-    tps = tiles // SEGS
     tile_x = lax.axis_index("gx") * width // TILE
     tile_y = lax.axis_index("gy") * tiles
     lane = iota((8, LANES), 1)
@@ -68,25 +69,22 @@
     wall_ref[main : main + 8, :] = jnp.zeros((8, LANES), f32)
     for copy in copies:
         copy.wait()
+    for t in range(tiles):
+        ice_ref[8 * t : 8 * t + 8, :] = jnp.full((8, LANES), ice_place[tile_y + t, tile_x].astype(f32), f32)
     for i in range(width // 8):
         rows = slice(8 * i, 8 * i + 8)
         ends = []
-        for t in range(tiles):
-            s, k = divmod(t, tps)
+        for t in (0, tiles - 1):
             cols = slice(t * LANES, (t + 1) * LANES)
-            values = masked(
-                ice_ref[tile_y + t, tile_x].astype(f32),
-                visc_ref[rows, cols],
-                mass_ref[rows, cols],
-                land_ref[rows, cols],
-                [forcing_ref[c, rows, cols] for c in range(2)],
+            ends.append(
+                masked(
+                    ice_place[tile_y + t, tile_x].astype(f32),
+                    visc_ref[rows, cols],
+                    mass_ref[rows, cols],
+                    land_ref[rows, cols],
+                    [forcing_ref[c, rows, cols] for c in range(2)],
+                )
             )
-            for a, value in enumerate(values):
-                tile = 8 * i * 2 * tps + (a // 2) * tps + k
-                start = tile * 8 + (a % 2) * SEGS + s
-                packed_ref[pl.ds(start, 8, stride=2 * tps * 8), :] = value
-            if t in (0, tiles - 1):
-                ends.append(values)
         for a in range(4):
             start = 8 * i * 4 + a
             edge_ref[pl.ds(start, 8, stride=4), :] = jnp.where(lane < HALF, ends[0][a], ends[1][a])
@@ -106,6 +104,28 @@
     )
 
 
+def pack_kernel(forcing_ref, visc_ref, mass_ref, land_ref, ice_ref, packed_ref):
+    width = visc_ref.shape[0]
+    tiles = visc_ref.shape[1] // LANES
+    tps = tiles // SEGS
+    for i in range(width // 8):
+        rows = slice(8 * i, 8 * i + 8)
+        for t in range(tiles):
+            s, k = divmod(t, tps)
+            cols = slice(t * LANES, (t + 1) * LANES)
+            values = masked(
+                ice_ref[8 * t : 8 * t + 8, :],
+                visc_ref[rows, cols],
+                mass_ref[rows, cols],
+                land_ref[rows, cols],
+                [forcing_ref[c, rows, cols] for c in range(2)],
+            )
+            for a, value in enumerate(values):
+                tile = 8 * i * 2 * tps + (a // 2) * tps + k
+                start = tile * 8 + (a % 2) * SEGS + s
+                packed_ref[pl.ds(start, 8, stride=2 * tps * 8), :] = value
+
+
 class Shifts:
     def __init__(self, tps):
         self.tps = tps
@@ -113,7 +133,7 @@
         self.shape = (8, self.span)
         self.lane = iota(self.shape, 1)
         self.upper = iota(self.shape, 0) >= SEGS
-        lane = iota((8, LANES), 1)
+        lane = self.lane1 = iota((8, LANES), 1)
         row = iota((8, LANES), 0) & (SEGS - 1)
         self.first_half = lane < HALF
         self.low = iota((8, LANES), 0) < SEGS
@@ -128,8 +148,12 @@
     def odd(self, step):
         return self.lane & step != 0
 
+    def take(self, value, index):
+        tiles = [value[:, k * LANES : (k + 1) * LANES] for k in range(self.tps + 1)]
+        return jnp.concatenate([jnp.take_along_axis(tile, index, axis=1) for tile in tiles], 1)
+
     def pair(self, value, step):
-        return value + jnp.where(self.odd(step), self.roll(value, step), self.roll(value, -step))
+        return value + self.take(value, self.lane1 ^ step)
 
     def with_halo(self, parts, outside):
         inside = jnp.where(self.first_half, pltpu.roll(parts[0], 7, 0), pltpu.roll(parts[-1], 1, 0))
@@ -172,7 +196,7 @@
 
     def coarse_sums(self, now, coarse, fine, place, step):
         north = now["north"][fine] + now["north"][fine + 1]
-        coarse["north"][place] = 0.25 * jnp.where(self.odd(step), north, self.roll(north, -step))
+        coarse["north"][place] = 0.25 * self.take(north, self.lane1 | step)
         coarse["mass"][place] = 0.25 * self.pair(now["mass"][fine] + now["mass"][fine + 1], step)
 
     def restrict(self, now, coarse, fine, place, group, rotation, step):
@@ -253,11 +277,11 @@
 
 
 def evens_of(move, value):
-    return jnp.where(move.odd(1), move.roll(value, 1), value)
+    return move.take(value, move.lane1 & ~1)
 
 
 def odds_of(move, value):
-    return jnp.where(move.odd(1), value, move.roll(value, -1))
+    return move.take(value, move.lane1 | 1)
 
 
 def put_packed(move, bottom, column, first, put):
@@ -269,13 +293,8 @@
 
 
 def from_packed(move, value):
-    bit1 = move.odd(2)
-    evens, odds = evens_of(move, value), odds_of(move, value)
-    for name, part, upper in zip(COARSE, (evens, odds, evens, odds), (0, 0, 1, 1)):
-        if upper:
-            yield name, jnp.where(bit1, part, move.roll(part, -2))
-        else:
-            yield name, jnp.where(bit1, move.roll(part, 2), part)
+    for n, name in enumerate(COARSE):
+        yield name, move.take(value, (move.lane1 & ~3) | n)
 
 
 def middle_packed(move, level1, column):
@@ -353,9 +372,9 @@
                     move, visc, top, lambda rows: own_ref[rows, :], base, ext, index, FINE + x + index
                 )
 
-    loop(0, width, own)
-    loop(FINE, width - 1, lambda x, n: faces(visc, top["east"], x, n), 16)
-    loop(FINE + 1, width - 2, lambda x, n: move.coefficients(top, x, n, 1), 10)
+    loop(0, width, own, width)
+    loop(FINE, width - 1, lambda x, n: faces(visc, top["east"], x, n), 31)
+    loop(FINE + 1, width - 2, lambda x, n: move.coefficients(top, x, n, 1), width - 2)
     skip, half, count = FINE - 2 * LEAD, width // 2, width >> SPLIT
     loop(LEAD, half - 1, lambda x, n: coarsen(move, top, level1, x, n, skip, 1), 15)
     coarsen(move, top, level1, LEAD + half - 1, 1, skip, 1, with_east=False)
@@ -363,7 +382,7 @@
         LEAD + 1,
         half - 2,
         lambda x, n: move.restrict(top, level1, 2 * x + skip, x, n, rotations[0], 1),
-        7,
+        14,
     )
     move.coefficients(level1, LEAD + 1, half - 2, 2)
     skip = LEAD - 2 * count
@@ -621,13 +640,16 @@
         )(*(pltpu.with_memory_space_constraint(arg, space) for arg in args))
 
     sources = (ice_tiles.T, forcing, viscosity, mass, land, lines)
-    packed, edge, mirror, wall = call(
+    edge, mirror, wall, *fields, lines, ice = call(
         prepare_kernel,
-        (here(width * each, LANES),) + (here(outside, LANES),) * 3,
+        (here(outside, LANES),) * 3
+        + tuple(pltpu.VMEM(source.shape, source.dtype) for source in sources[1:])
+        + (here(8 * tiles, LANES),),
         sources,
-        scratch=[pltpu.SMEM(sources[0].shape, sources[0].dtype)]
-        + [pltpu.VMEM(source.shape, source.dtype) for source in sources[1:]]
-        + [pltpu.SemaphoreType.DMA((len(sources),))],
+        scratch=[
+            pltpu.SMEM(sources[0].shape, sources[0].dtype),
+            pltpu.SemaphoreType.DMA((len(sources),)),
+        ],
         space=pltpu.HBM,
     )
     top = gy - 1
@@ -635,6 +657,7 @@
         mirror, ("gx", "gy"), [(i * gy + top, (gx - 1 - i) * gy + top) for i in range(gx)]
     )
     swap = lax.ppermute(edge, "gy", [(i, gy - 1 - i) for i in range(gy)])
+    packed = call(pack_kernel, here(width * each, LANES), (*fields, ice))
     odd_pairs = [(i, (i + (1 if i % 2 else gx - 1)) % gx) for i in range(gx)]
     even_pairs = [(i, i ^ 1) for i in range(gx)]
     span = (tps + 1) * LANES

time: 74.8 us -> 72.9 us (0.975)
  Pallas kernels: 9.44 us -> 7.69 us
    pallas_call x4 -> x5, Pallas kernels: 9.44 us -> 7.69 us  [call(): pl.pallas_call(kernel, out_shape=outs, in_specs=[pl.BlockSpec(memory_spac...]
  transfers between devices with their start and end apart: 4 -> 4, of which waited for: 3 -> 3; matrix products, arithmetic and copies ran while one was open for 0% -> 0% of each run, Pallas kernels for 1% -> 2%
where the time goes in v7:
time: 72.9 us; the launch traced here: 72.6 us
  starting transfers between devices  59 us (81%)
  Pallas kernels  7.69 us (11%)
  waiting for transfers between devices  5.82 us (8%)
    ppermute x1, starting transfers between devices, local(): swap = lax.ppermute(edge, 'gy', [(i, gy - 1 - i) for i in range(gy)])  43.4 us
    pallas_call x5, Pallas kernels, call(): pl.pallas_call(kernel, out_shape=outs, in_specs=[pl.BlockSpec(memory_spac...  7.69 us
    ppermute x1, starting transfers between devices, local(): lax.ppermute(mirror, ('gx', 'gy'), [(i * gy + top, (gx - 1 - i) * gy + to...  7 us
    ppermute x1, starting transfers between devices, local(): by_odd = lax.ppermute(odd, 'gx', odd_pairs)  6.7 us
    ppermute x1, waiting for transfers between devices, local(): by_even = lax.ppermute(even, 'gx', even_pairs)  3.39 us
    ppermute x1, starting transfers between devices, local(): by_even = lax.ppermute(even, 'gx', even_pairs)  1.95 us
  transfers between devices with their start and end apart: 4, of which 3 were waited for; matrix products, arithmetic and copies ran while one was open for 0% of the time, Pallas kernels for 2%

profile of v7, /device:TPU:65, one launch (start us, length us, event | category | flops | bytes accessed | tf_op | source)
XLA Modules:
  0.0 72.6 jit_solution(11070443537402364180)
XLA Ops:
  0.0 1.7 %shard_map.64 = (f32[136,128]{1,0:T(8,128)S(1)}, f32[136,128]{1,0:T(8,128)S(1)}, f32[136,128]{1,0:T(8,128)S(1)}, f32[2,32,1536]{2,1,0:T(8,128)S(1)}, f32[32,1536...) custom-call(s32[24,32]{1,0:T(8,128)} %bitcast.2, ...), custom_call_target="tpu_custom_call" | custom-call | tf_op jit(solution)/shard_map/pallas_call | solution.py:628
  1.7 43.4 %collective-permute-start = (f32[136,128]{1,0:T(8,128)S(1)}, f32[136,128]{1,0:T(8,128)S(1)}, u32[]{:S(2)}, u32[]{:S(2)}) collective-permute-start(f32[136,128]{1,0:T(8,128)S(1)} %get-tuple-element.52), channel_id=1, source_target_pairs={{0,1},{1,0},{2,3},{3,2},{4,5},{5,4},{6,7},{7,6},{8,9},{9,8},{10,11... | collective-permute-start | bytes 208904 | tf_op jit(solution)/shard_map/ppermute | solution.py:659
  45.1 7.0 %collective-permute-start.1 = (f32[136,128]{1,0:T(8,128)S(1)}, f32[136,128]{1,0:T(8,128)S(1)}, u32[]{:S(2)}, u32[]{:S(2)}) collective-permute-start(f32[136,128]{1,0:T(8,128)S(1)} %get-tuple-element.53), channel_id=1, source_target_pairs={{1,255},{3,253},{5,251},{7,249},{9,247},{11,245},{13,243},{15,241}... | collective-permute-start | bytes 208904 | tf_op jit(solution)/shard_map/ppermute | solution.py:656
  52.1 0.3 shard_map.65.own_ref
  52.4 0.0 collective-permute-done.swap_ref
  52.4 1.4 %collective-permute-done.1.folded_ref = f32[136,128]{1,0:T(8,128)S(1)} collective-permute-done((f32[136,128]{1,0:T(8,128)S(1)}, f32[136,128]{1,0:T(8,128)S(1)}, u32[]{:S(2)}, u32[]{:S(2)}) %collective-permute-start.1) | collective-permute-done | bytes 69664 | tf_op jit(solution)/shard_map/ppermute | solution.py:656
  53.8 1.6 %shard_map.66 = (f32[40,8,512]{2,1,0:T(8,128)S(1)}, f32[40,8,512]{2,1,0:T(8,128)S(1)}, f32[40,8,512]{2,1,0:T(8,128)S(1)}, f32[40,8,512]{2,1,0:T(8,128)S(1)}, f32...) custom-call(f32[1536,128]{1,0:T(8,128)S(1)} %shard_map.65.own_ref, ...), custom_call_target="tpu_custom_call" | custom-call | tf_op jit(solution)/shard_map/pallas_call | solution.py:628
  55.4 6.7 %collective-permute-start.2 = (f32[528,128]{1,0:T(8,128)S(1)}, f32[528,128]{1,0:T(8,128)S(1)}, u32[]{:S(2)}, u32[]{:S(2)}) collective-permute-start(f32[528,128]{1,0:T(8,128)S(1)} %get-tuple-element.56), channel_id=1, source_target_pairs={{0,254},{2,4},{4,2},{6,8},{8,6},{10,12},{12,10},{14,16},{16,14},{1... | collective-permute-start | bytes 811016 | tf_op jit(solution)/shard_map/ppermute | solution.py:680
  62.1 2.0 %collective-permute-start.3 = (f32[528,128]{1,0:T(8,128)S(1)}, f32[528,128]{1,0:T(8,128)S(1)}, u32[]{:S(2)}, u32[]{:S(2)}) collective-permute-start(f32[528,128]{1,0:T(8,128)S(1)} %get-tuple-element.57), channel_id=1, source_target_pairs={{0,2},{2,0},{4,6},{6,4},{8,10},{10,8},{12,14},{14,12},{16,18},{18,... | collective-permute-start | bytes 811016 | tf_op jit(solution)/shard_map/ppermute | solution.py:681
  64.0 0.9 %shard_map.67 = (f32[32,8,512]{2,1,0:T(8,128)S(1)}, f32[32,8,512]{2,1,0:T(8,128)S(1)}, f32[32,8,512]{2,1,0:T(8,128)S(1)}, f32[32,8,512]{2,1,0:T(8,128)S(1)}, f32...) custom-call(f32[4,8,512]{2,1,0:T(8,128)S(1)} %get-tuple-element.58.r, ...), custom_call_target="tpu_custom_call" | custom-call | tf_op jit(solution)/shard_map/pallas_call | solution.py:628
  64.9 1.0 %collective-permute-done.2.odd_ref = f32[528,128]{1,0:T(8,128)S(1)} collective-permute-done((f32[528,128]{1,0:T(8,128)S(1)}, f32[528,128]{1,0:T(8,128)S(1)}, u32[]{:S(2)}, u32[]{:S(2)}) %collective-permute-start.2) | collective-permute-done | bytes 270368 | tf_op jit(solution)/shard_map/ppermute | solution.py:680
  65.9 3.4 %collective-permute-done.3.even_ref = f32[528,128]{1,0:T(8,128)S(1)} collective-permute-done((f32[528,128]{1,0:T(8,128)S(1)}, f32[528,128]{1,0:T(8,128)S(1)}, u32[]{:S(2)}, u32[]{:S(2)}) %collective-permute-start.3) | collective-permute-done | bytes 270368 | tf_op jit(solution)/shard_map/ppermute | solution.py:681
  69.3 3.3 %shard_map.68 = (f32[2,32,1536]{2,1,0:T(8,128)}, f32[40,8,512]{2,1,0:T(8,128)S(1)}, f32[40,8,512]{2,1,0:T(8,128)S(1)}, f32[40,8,512]{2,1,0:T(8,128)S(1)}, f32[40...) custom-call(f32[528,128]{1,0:T(8,128)S(1)} %collective-permute-done., ...), custom_call_target="tpu_custom_call", output_to_operand_aliasing={{1}: (3, {}), {2}: (4, {}), {3}: (5, {}), {4}: (6, {}), {5}... | custom-call | tf_op jit(solution)/shard_map/pallas_call | solution.py:628
Async XLA Ops:
  1.7 50.7 %collective-permute-start = (f32[136,128]{1,0:T(8,128)S(1)}, f32[136,128]{1,0:T(8,128)S(1)}, u32[]{:S(2)}, u32[]{:S(2)}) collective-permute-start(f32[136,128]{1,0:T(8,128)S(1)} %get-tuple-element.52), channel_id=1, source_target_pairs={{0,1},{1,0},{2,3},{3,2},{4,5},{5,4},{6,7},{7,6},{8,9},{9,8},{10,11... | collective-permute-start | bytes 208904 | tf_op jit(solution)/shard_map/ppermute | solution.py:659
  45.1 8.7 %collective-permute-start.1 = (f32[136,128]{1,0:T(8,128)S(1)}, f32[136,128]{1,0:T(8,128)S(1)}, u32[]{:S(2)}, u32[]{:S(2)}) collective-permute-start(f32[136,128]{1,0:T(8,128)S(1)} %get-tuple-element.53), channel_id=1, source_target_pairs={{1,255},{3,253},{5,251},{7,249},{9,247},{11,245},{13,243},{15,241}... | collective-permute-start | bytes 208904 | tf_op jit(solution)/shard_map/ppermute | solution.py:656
  55.4 10.6 %collective-permute-start.2 = (f32[528,128]{1,0:T(8,128)S(1)}, f32[528,128]{1,0:T(8,128)S(1)}, u32[]{:S(2)}, u32[]{:S(2)}) collective-permute-start(f32[528,128]{1,0:T(8,128)S(1)} %get-tuple-element.56), channel_id=1, source_target_pairs={{0,254},{2,4},{4,2},{6,8},{8,6},{10,12},{12,10},{14,16},{16,14},{1... | collective-permute-start | bytes 811016 | tf_op jit(solution)/shard_map/ppermute | solution.py:680
  62.1 7.2 %collective-permute-start.3 = (f32[528,128]{1,0:T(8,128)S(1)}, f32[528,128]{1,0:T(8,128)S(1)}, u32[]{:S(2)}, u32[]{:S(2)}) collective-permute-start(f32[528,128]{1,0:T(8,128)S(1)} %get-tuple-element.57), channel_id=1, source_target_pairs={{0,2},{2,0},{4,6},{6,4},{8,10},{10,8},{12,14},{14,12},{16,18},{18,... | collective-permute-start | bytes 811016 | tf_op jit(solution)/shard_map/ppermute | solution.py:681

commit v8 on v7

--- a/solution.py
+++ b/solution.py
@@ -183,21 +183,26 @@
 
     def coefficients(self, now, first, group, step):
         east = [now["east"][first + j - 1] for j in range(group + 1)]
-        for j in range(group):
+
+        def known(j):
             x = first + j
             north = now["north"][x]
-            diag = now["mass"][x] + east[j + 1] + east[j] + north + self.roll(north, step)
-            scale = self.weight / diag
-            now["scale"][x] = scale
-            now["field"][x] = scale * now["right"][x]
-
-    def coarse_east(self, now, fine, target, step):
-        target[...] = 0.25 * self.pair(now["east"][fine + 1], step)
-
-    def coarse_sums(self, now, coarse, fine, place, step):
-        north = now["north"][fine] + now["north"][fine + 1]
-        coarse["north"][place] = 0.25 * self.take(north, self.lane1 | step)
-        coarse["mass"][place] = 0.25 * self.pair(now["mass"][fine] + now["mass"][fine + 1], step)
+            return north, now["mass"][x] + east[j + 1] + east[j] + north
+
+        for j in range(0, group, 2):
+            north, rest = known(j)
+            if j + 1 < group:
+                north2, rest2 = known(j + 1)
+                north, rest = jnp.where(self.upper, north2, north), jnp.where(self.upper, rest2, rest)
+            scale = self.weight / (rest + self.roll(north, step))
+            scales = (scale,)
+            if j + 1 < group:
+                turned = other(scale)
+                scales = (jnp.where(self.upper, turned, scale), jnp.where(self.upper, scale, turned))
+            for k, scale in enumerate(scales):
+                x = first + j + k
+                now["scale"][x] = scale
+                now["field"][x] = scale * now["right"][x]
 
     def restrict(self, now, coarse, fine, place, group, rotation, step):
         field = [now["field"][fine + j - 1] for j in range(2 * group + 2)]
@@ -268,12 +273,32 @@
 
 
 def coarsen(move, now, coarse, first, group, skip, step, with_east=True, with_sums=True):
+    def norths(j):
+        x = 2 * (first + j) + skip
+        return now["north"][x] + now["north"][x + 1]
+
     for j in range(group):
         x = 2 * (first + j) + skip
-        if with_east:
-            coarse["east"][first + j] = 0.25 * move.pair(now["east"][x + 1], step)
-        if with_sums:
-            move.coarse_sums(now, coarse, x, first + j, step)
+        east = now["east"][x + 1] if with_east else None
+        mass = now["mass"][x] + now["mass"][x + 1] if with_sums else None
+        if with_east and with_sums:
+            both = 0.25 * move.pair(jnp.where(move.upper, mass, east), step)
+            turned = other(both)
+            coarse["east"][first + j] = jnp.where(move.upper, turned, both)
+            coarse["mass"][first + j] = jnp.where(move.upper, both, turned)
+        elif with_east:
+            coarse["east"][first + j] = 0.25 * move.pair(east, step)
+        else:
+            coarse["mass"][first + j] = 0.25 * move.pair(mass, step)
+        if with_sums and j % 2 == 0:
+            if j + 1 < group:
+                both = jnp.where(move.upper, norths(j + 1), norths(j))
+                both = 0.25 * move.take(both, move.lane1 | step)
+                turned = other(both)
+                coarse["north"][first + j] = jnp.where(move.upper, turned, both)
+                coarse["north"][first + j + 1] = jnp.where(move.upper, both, turned)
+            else:
+                coarse["north"][first + j] = 0.25 * move.take(norths(j), move.lane1 | step)
 
 
 def evens_of(move, value):
@@ -284,17 +309,34 @@
     return move.take(value, move.lane1 | 1)
 
 
-def put_packed(move, bottom, column, first, put):
+def coarse_packed(move, bottom, base, count):
     bit0, bit1 = move.odd(1), move.odd(2)
-    names = ("east", "north", "mass")
-    east, north, mass = (bottom[name][column] for name in names)
-    right = jnp.zeros(move.shape, f32) if first else bottom["right"][column]
-    put(jnp.where(bit1, jnp.where(bit0, mass, north), jnp.where(bit0, east, right)))
-
-
-def from_packed(move, value):
-    for n, name in enumerate(COARSE):
-        yield name, move.take(value, (move.lane1 & ~3) | n)
+    values = []
+    for n in range(count // 2):
+        first, second = base + 2 * n, base + min(2 * n + 1, count - 2)
+        east, north, mass = (
+            jnp.where(move.upper, bottom[name][second], bottom[name][first]) for name in COARSE[1:]
+        )
+        right = bottom["right"][base + n + 1]
+        values.append(jnp.where(bit1, jnp.where(bit0, mass, north), jnp.where(bit0, east, right)))
+    rights = [bottom["right"][base + count // 2 + 1 + n] for n in range(2)]
+    return values + [jnp.where(bit0, rights[1], rights[0])]
+
+
+def coarse_unpacked(move, bottom, base, count, load, first_too):
+    for n in range(count // 2):
+        value = load(n)
+        bottom["right"][base + n + 1] = move.take(value, move.lane1 & ~3)
+        for place, name in enumerate(COARSE[1:]):
+            part = move.take(value, (move.lane1 & ~3) | (place + 1))
+            turned = other(part)
+            if n or first_too:
+                bottom[name][base + 2 * n] = jnp.where(move.upper, turned, part)
+            if 2 * n + 1 < count - 1:
+                bottom[name][base + 2 * n + 1] = jnp.where(move.upper, part, turned)
+    value = load(count // 2)
+    bottom["right"][base + count // 2 + 1] = evens_of(move, value)
+    bottom["right"][base + count // 2 + 2] = odds_of(move, value)
 
 
 def middle_packed(move, level1, column):
@@ -400,13 +442,9 @@
     for n, (low, high) in enumerate(zip(lows, highs)):
         put(odd_ref, n, jnp.where(even, low, high))
         put(even_ref, n, jnp.where(even, high, low))
-    for column in range(count - 1):
-
-        def put_both(value, column=column):
-            put(odd_ref, 3 + column, value)
-            put(even_ref, 3 + column, value)
-
-        put_packed(move, bottom, count + column, column == 0, put_both)
+    for n, value in enumerate(coarse_packed(move, bottom, count, count)):
+        put(odd_ref, 3 + n, value)
+        put(even_ref, 3 + n, value)
 
 
 def ahead_columns(move, now, ahead, rotation, level, place, group, parity=None):
@@ -501,13 +539,10 @@
     middle_unpacked(
         move, level1, LEAD + half + 1, [received(from_right, n) for n in range(3)], False
     )
-    for load, start, columns_sent in (
-        (from_left, 0, range(count - 1)),
-        (from_right, 2 * count, range(1, count - 1)),
-    ):
-        for column in columns_sent:
-            for name, part in from_packed(move, received(load, 3 + column)):
-                now[name][start + column] = part
+    for load, start in ((from_left, 0), (from_right, 2 * count)):
+        coarse_unpacked(
+            move, now, start, count, lambda n, load=load: received(load, 3 + n), start == 0
+        )
     for start in (0, columns - 1 - FINE):
         faces(visc, top["east"], start, FINE)
     for start in (1, columns - 1 - FINE):
@@ -536,10 +571,8 @@
         now, coarse = levels[level], levels[level + 1]
         step = 1 << level
         half = total // 2
-        for k in range(half - 1):
-            coarse["east"][k] = 0.25 * move.pair(now["east"][2 * k + 1], step)
-        for k in range(1, half - 1):
-            move.coarse_sums(now, coarse, 2 * k, k, step)
+        coarsen(move, now, coarse, 0, 1, 0, step, with_sums=False)
+        coarsen(move, now, coarse, 1, half - 2, 0, step)
         move.restrict(now, coarse, 2, 1, half - 2, rotations[level], step)
         total = half
         move.coefficients(coarse, 1, total - 2, 2 * step)
@@ -670,7 +703,7 @@
 
     kept = tuple(lines_of(columns[level]) for level in range(SPLIT) for _ in STATE)
     kept += (lines_of(columns[SPLIT]),) * len(COARSE) + (lines_of(columns[0]),)
-    message = here(FINE * (each + 4) + (count + 2) * (tps + 1) * 8, LANES)
+    message = here(FINE * (each + 4) + (count // 2 + 4) * (tps + 1) * 8, LANES)
     *state, rotation, odd, even = call(
         own_kernel,
         kept + (lines_of(LEVELS), message, message),

time: 72.9 us -> 72.1 us (0.989)
  no operation moved by 1% of the time
where the time goes in v8:
time: 72.1 us; the launch traced here: 71.8 us
  starting transfers between devices  59 us (82%)
  Pallas kernels  7.27 us (10%)
  waiting for transfers between devices  5.47 us (8%)
    ppermute x1, starting transfers between devices, local(): swap = lax.ppermute(edge, 'gy', [(i, gy - 1 - i) for i in range(gy)])  43.4 us
    pallas_call x5, Pallas kernels, call(): pl.pallas_call(kernel, out_shape=outs, in_specs=[pl.BlockSpec(memory_spac...  7.27 us
    ppermute x1, starting transfers between devices, local(): lax.ppermute(mirror, ('gx', 'gy'), [(i * gy + top, (gx - 1 - i) * gy + to...  7 us
    ppermute x1, starting transfers between devices, local(): by_odd = lax.ppermute(odd, 'gx', odd_pairs)  6.7 us
    ppermute x1, waiting for transfers between devices, local(): by_even = lax.ppermute(even, 'gx', even_pairs)  3.39 us
    ppermute x1, starting transfers between devices, local(): by_even = lax.ppermute(even, 'gx', even_pairs)  1.95 us
  transfers between devices with their start and end apart: 4, of which 3 were waited for; matrix products, arithmetic and copies ran while one was open for 0% of the time, Pallas kernels for 2%

profile of v8, /device:TPU:65, one launch (start us, length us, event | category | flops | bytes accessed | tf_op | source)
XLA Modules:
  0.0 71.8 jit_solution(3580131095544304833)
XLA Ops:
  0.0 1.7 %shard_map.64 = (f32[136,128]{1,0:T(8,128)S(1)}, f32[136,128]{1,0:T(8,128)S(1)}, f32[136,128]{1,0:T(8,128)S(1)}, f32[2,32,1536]{2,1,0:T(8,128)S(1)}, f32[32,1536...) custom-call(s32[24,32]{1,0:T(8,128)} %bitcast.2, ...), custom_call_target="tpu_custom_call" | custom-call | tf_op jit(solution)/shard_map/pallas_call | solution.py:661
  1.7 43.4 %collective-permute-start = (f32[136,128]{1,0:T(8,128)S(1)}, f32[136,128]{1,0:T(8,128)S(1)}, u32[]{:S(2)}, u32[]{:S(2)}) collective-permute-start(f32[136,128]{1,0:T(8,128)S(1)} %get-tuple-element.52), channel_id=1, source_target_pairs={{0,1},{1,0},{2,3},{3,2},{4,5},{5,4},{6,7},{7,6},{8,9},{9,8},{10,11... | collective-permute-start | bytes 208904 | tf_op jit(solution)/shard_map/ppermute | solution.py:692
  45.1 7.0 %collective-permute-start.1 = (f32[136,128]{1,0:T(8,128)S(1)}, f32[136,128]{1,0:T(8,128)S(1)}, u32[]{:S(2)}, u32[]{:S(2)}) collective-permute-start(f32[136,128]{1,0:T(8,128)S(1)} %get-tuple-element.53), channel_id=1, source_target_pairs={{1,255},{3,253},{5,251},{7,249},{9,247},{11,245},{13,243},{15,241}... | collective-permute-start | bytes 208904 | tf_op jit(solution)/shard_map/ppermute | solution.py:689
  52.1 0.3 shard_map.65.own_ref
  52.4 0.0 collective-permute-done.swap_ref
  52.4 1.4 %collective-permute-done.1.folded_ref = f32[136,128]{1,0:T(8,128)S(1)} collective-permute-done((f32[136,128]{1,0:T(8,128)S(1)}, f32[136,128]{1,0:T(8,128)S(1)}, u32[]{:S(2)}, u32[]{:S(2)}) %collective-permute-start.1) | collective-permute-done | bytes 69664 | tf_op jit(solution)/shard_map/ppermute | solution.py:689
  53.8 1.4 %shard_map.66 = (f32[40,8,512]{2,1,0:T(8,128)S(1)}, f32[40,8,512]{2,1,0:T(8,128)S(1)}, f32[40,8,512]{2,1,0:T(8,128)S(1)}, f32[40,8,512]{2,1,0:T(8,128)S(1)}, f32...) custom-call(f32[1536,128]{1,0:T(8,128)S(1)} %shard_map.65.own_ref, ...), custom_call_target="tpu_custom_call" | custom-call | tf_op jit(solution)/shard_map/pallas_call | solution.py:661
  55.2 6.7 %collective-permute-start.2 = (f32[464,128]{1,0:T(8,128)S(1)}, f32[464,128]{1,0:T(8,128)S(1)}, u32[]{:S(2)}, u32[]{:S(2)}) collective-permute-start(f32[464,128]{1,0:T(8,128)S(1)} %get-tuple-element.56), channel_id=1, source_target_pairs={{0,254},{2,4},{4,2},{6,8},{8,6},{10,12},{12,10},{14,16},{16,14},{1... | collective-permute-start | bytes 712712 | tf_op jit(solution)/shard_map/ppermute | solution.py:713
  61.9 2.0 %collective-permute-start.3 = (f32[464,128]{1,0:T(8,128)S(1)}, f32[464,128]{1,0:T(8,128)S(1)}, u32[]{:S(2)}, u32[]{:S(2)}) collective-permute-start(f32[464,128]{1,0:T(8,128)S(1)} %get-tuple-element.57), channel_id=1, source_target_pairs={{0,2},{2,0},{4,6},{6,4},{8,10},{10,8},{12,14},{14,12},{16,18},{18,... | collective-permute-start | bytes 712712 | tf_op jit(solution)/shard_map/ppermute | solution.py:714
  63.9 0.9 %shard_map.67 = (f32[32,8,512]{2,1,0:T(8,128)S(1)}, f32[32,8,512]{2,1,0:T(8,128)S(1)}, f32[32,8,512]{2,1,0:T(8,128)S(1)}, f32[32,8,512]{2,1,0:T(8,128)S(1)}, f32...) custom-call(f32[4,8,512]{2,1,0:T(8,128)S(1)} %get-tuple-element.58.r, ...), custom_call_target="tpu_custom_call" | custom-call | tf_op jit(solution)/shard_map/pallas_call | solution.py:661
  64.7 0.7 collective-permute-done.2.odd_ref
  65.4 3.4 %collective-permute-done.3.even_ref = f32[464,128]{1,0:T(8,128)S(1)} collective-permute-done((f32[464,128]{1,0:T(8,128)S(1)}, f32[464,128]{1,0:T(8,128)S(1)}, u32[]{:S(2)}, u32[]{:S(2)}) %collective-permute-start.3) | collective-permute-done | bytes 237600 | tf_op jit(solution)/shard_map/ppermute | solution.py:714
  68.8 3.0 %shard_map.68 = (f32[2,32,1536]{2,1,0:T(8,128)}, f32[40,8,512]{2,1,0:T(8,128)S(1)}, f32[40,8,512]{2,1,0:T(8,128)S(1)}, f32[40,8,512]{2,1,0:T(8,128)S(1)}, f32[40...) custom-call(f32[464,128]{1,0:T(8,128)S(1)} %collective-permute-done., ...), custom_call_target="tpu_custom_call", output_to_operand_aliasing={{1}: (3, {}), {2}: (4, {}), {3}: (5, {}), {4}: (6, {}), {5}... | custom-call | tf_op jit(solution)/shard_map/pallas_call | solution.py:661
Async XLA Ops:
  1.7 50.7 %collective-permute-start = (f32[136,128]{1,0:T(8,128)S(1)}, f32[136,128]{1,0:T(8,128)S(1)}, u32[]{:S(2)}, u32[]{:S(2)}) collective-permute-start(f32[136,128]{1,0:T(8,128)S(1)} %get-tuple-element.52), channel_id=1, source_target_pairs={{0,1},{1,0},{2,3},{3,2},{4,5},{5,4},{6,7},{7,6},{8,9},{9,8},{10,11... | collective-permute-start | bytes 208904 | tf_op jit(solution)/shard_map/ppermute | solution.py:692
  45.1 8.7 %collective-permute-start.1 = (f32[136,128]{1,0:T(8,128)S(1)}, f32[136,128]{1,0:T(8,128)S(1)}, u32[]{:S(2)}, u32[]{:S(2)}) collective-permute-start(f32[136,128]{1,0:T(8,128)S(1)} %get-tuple-element.53), channel_id=1, source_target_pairs={{1,255},{3,253},{5,251},{7,249},{9,247},{11,245},{13,243},{15,241}... | collective-permute-start | bytes 208904 | tf_op jit(solution)/shard_map/ppermute | solution.py:689
  55.2 10.2 %collective-permute-start.2 = (f32[464,128]{1,0:T(8,128)S(1)}, f32[464,128]{1,0:T(8,128)S(1)}, u32[]{:S(2)}, u32[]{:S(2)}) collective-permute-start(f32[464,128]{1,0:T(8,128)S(1)} %get-tuple-element.56), channel_id=1, source_target_pairs={{0,254},{2,4},{4,2},{6,8},{8,6},{10,12},{12,10},{14,16},{16,14},{1... | collective-permute-start | bytes 712712 | tf_op jit(solution)/shard_map/ppermute | solution.py:713
  61.9 6.9 %collective-permute-start.3 = (f32[464,128]{1,0:T(8,128)S(1)}, f32[464,128]{1,0:T(8,128)S(1)}, u32[]{:S(2)}, u32[]{:S(2)}) collective-permute-start(f32[464,128]{1,0:T(8,128)S(1)} %get-tuple-element.57), channel_id=1, source_target_pairs={{0,2},{2,0},{4,6},{6,4},{8,10},{10,8},{12,14},{14,12},{16,18},{18,... | collective-permute-start | bytes 712712 | tf_op jit(solution)/shard_map/ppermute | solution.py:714

commit v9 on v8

--- a/solution.py
+++ b/solution.py
@@ -51,11 +51,23 @@
 
 
 def prepare_kernel(*refs):
-    held = (refs[15],) + refs[9:14]
-    copies = fetch(refs[:6], held, refs[16])
+    hbm, sems = refs[:6], refs[20]
     edge_ref, mirror_ref, wall_ref, ice_ref = refs[6:9] + refs[14:15]
-    forcing_ref, visc_ref, mass_ref, land_ref, cor_ref = refs[9:14]
-    ice_place = refs[15]
+    _, visc_ref, _, _, cor_ref = refs[9:14]
+    ice_place, forcing_end, visc_end, mass_end, land_end = refs[15:20]
+    last_tile = visc_ref.shape[1] - LANES
+    sources, held = [hbm[0], hbm[5]], [ice_place, cor_ref]
+    for n in range(2):
+        cols = pl.ds(n * last_tile, LANES)
+        sources += [hbm[1].at[:, :, cols]] + [ref.at[:, cols] for ref in hbm[2:5]]
+        held += [ref.at[n] for ref in (forcing_end, visc_end, mass_end, land_end)]
+    copies = fetch(sources, held, sems)
+    bulk = [
+        pltpu.make_async_copy(a, b, sems.at[len(copies) + n])
+        for n, (a, b) in enumerate(zip(hbm[1:5], refs[9:13]))
+    ]
+    for copy in bulk:
+        copy.start()
     width = visc_ref.shape[0]
     tiles = visc_ref.shape[1] // LANES
     tile_x = lax.axis_index("gx") * width // TILE
@@ -74,15 +86,14 @@
     for i in range(width // 8):
         rows = slice(8 * i, 8 * i + 8)
         ends = []
-        for t in (0, tiles - 1):
-            cols = slice(t * LANES, (t + 1) * LANES)
+        for n, t in enumerate((0, tiles - 1)):
             ends.append(
                 masked(
                     ice_place[tile_y + t, tile_x].astype(f32),
-                    visc_ref[rows, cols],
-                    mass_ref[rows, cols],
-                    land_ref[rows, cols],
-                    [forcing_ref[c, rows, cols] for c in range(2)],
+                    visc_end[n, rows, :],
+                    mass_end[n, rows, :],
+                    land_end[n, rows, :],
+                    [forcing_end[n, c, rows, :] for c in range(2)],
                 )
             )
         for a in range(4):
@@ -102,6 +113,8 @@
     mirror_ref[main : main + 8, :] = jnp.dot(
         edge_ref[main : main + 8, :], flip, precision=exact, preferred_element_type=f32
     )
+    for copy in bulk:
+        copy.wait()
 
 
 def pack_kernel(forcing_ref, visc_ref, mass_ref, land_ref, ice_ref, packed_ref):
@@ -252,24 +265,32 @@
         east[first + j] = 0.5 * (value[j] + value[j + 1])
 
 
-def unpack(move, visc, top, load, base, ext, index, x):
+def unpack(move, visc, top, load, bases, ext, x, with_right=(True, True)):
     tps = move.tps
-    rows = [jnp.broadcast_to(ext[4 * index + a : 4 * index + a + 1], (8, LANES)) for a in range(4)]
-    both = move.with_halo(
-        [load(pl.ds(base + 8 * k, 8)) for k in range(tps)], jnp.where(move.low, rows[0], rows[1])
-    )
-    turned = [other(part) for part in both]
-    value = jnp.concatenate([jnp.where(move.low, a, b) for a, b in zip(both, turned)], 1)
-    visc[x] = value
-    top["mass"][x] = jnp.concatenate([jnp.where(move.low, b, a) for a, b in zip(both, turned)], 1)
-    top["right"][x] = jnp.concatenate(
-        move.with_halo(
-            [load(pl.ds(base + 8 * (tps + k), 8)) for k in range(tps)],
-            jnp.where(move.low, rows[2], rows[3]),
-        ),
-        1,
-    )
-    top["north"][x] = 0.5 * (value + move.roll(value, -1))
+    for index, base in enumerate(bases):
+        rows = [jnp.broadcast_to(ext[4 * index + a : 4 * index + a + 1], (8, LANES)) for a in range(4)]
+        both = move.with_halo(
+            [load(pl.ds(base + 8 * k, 8)) for k in range(tps)], jnp.where(move.low, rows[0], rows[1])
+        )
+        turned = [other(part) for part in both]
+        value = jnp.concatenate([jnp.where(move.low, a, b) for a, b in zip(both, turned)], 1)
+        visc[x + index] = value
+        top["north"][x + index] = 0.5 * (value + move.roll(value, -1))
+        top["mass"][x + index] = jnp.concatenate(
+            [jnp.where(move.low, b, a) for a, b in zip(both, turned)], 1
+        )
+        if with_right[index]:
+            top["right"][x + index] = jnp.concatenate(
+                move.with_halo(
+                    [load(pl.ds(base + 8 * (tps + k), 8)) for k in range(tps)],
+                    jnp.where(move.low, rows[2], rows[3]),
+                ),
+                1,
+            )
+
+
+def fine_rows(tps):
+    return (FINE - 1) * 2 * tps * 8 + tps * 8
 
 
 def coarsen(move, now, coarse, first, group, skip, step, with_east=True, with_sums=True):
@@ -388,15 +409,20 @@
     )
     even = is_even()
     each = 2 * tps * 8
-    side, total = FINE * each, width * each
-    parts = (
-        (slice(0, side), own_ref[0:side, :], own_ref[total - side : total, :]),
-        (
-            slice(side, side + 4 * FINE),
-            ext_ref[0 : 4 * FINE, :],
-            ext_ref[main - 4 * FINE : main, :],
-        ),
-    )
+    side = fine_rows(tps)
+    parts = [
+        (slice(side, side + 4 * FINE), ext_ref[0 : 4 * FINE, :], ext_ref[main - 4 * FINE : main, :])
+    ]
+    for q in range(FINE):
+        size = each if q < FINE - 1 else tps * 8
+        start = (width - 1 - q) * each
+        parts.append(
+            (
+                slice(q * each, q * each + size),
+                own_ref[q * each : q * each + size, :],
+                own_ref[start : start + size, :],
+            )
+        )
     for rows, low, high in parts:
         odd_ref[rows, :] = jnp.where(even, low, high)
         even_ref[rows, :] = jnp.where(even, high, low)
@@ -408,11 +434,8 @@
         for j in range(0, group, 2):
             x = first + j
             ext = ext_ref[pl.ds(pl.multiple_of(4 * x, 8), 8), :]
-            for index in range(2):
-                base = pl.multiple_of((x + index) * each, 8)
-                unpack(
-                    move, visc, top, lambda rows: own_ref[rows, :], base, ext, index, FINE + x + index
-                )
+            bases = [pl.multiple_of((x + index) * each, 8) for index in range(2)]
+            unpack(move, visc, top, lambda rows: own_ref[rows, :], bases, ext, FINE + x)
 
     loop(0, width, own, width)
     loop(FINE, width - 1, lambda x, n: faces(visc, top["east"], x, n), 31)
@@ -525,14 +548,24 @@
     def from_right(rows):
         return jnp.where(even, even_ref[rows, :], odd_ref[rows, :])
 
+    side = fine_rows(tps)
     for load, start in ((from_left, 0), (from_right, FINE + width)):
         for j in range(0, FINE, 2):
-            ext = load(pl.ds(FINE * each + 4 * j, 8))
-            for index in range(2):
-                unpack(move, visc, top, load, (j + index) * each, ext, index, start + j + index)
+            ext = load(pl.ds(side + 4 * j, 8))
+            places = [j + index if start else FINE - 1 - j - index for index in range(2)]
+            unpack(
+                move,
+                visc,
+                top,
+                load,
+                [place * each for place in places],
+                ext,
+                start + j,
+                [place < FINE - 1 for place in places],
+            )
 
     def received(load, column):
-        row = FINE * (each + 4) + column * (tps + 1) * 8
+        row = side + 4 * FINE + column * (tps + 1) * 8
         return jnp.concatenate([load(pl.ds(row + 8 * k, 8)) for k in range(tps + 1)], 1)
 
     middle_unpacked(move, level1, 1, [received(from_left, n) for n in range(3)], True)
@@ -681,7 +714,9 @@
         sources,
         scratch=[
             pltpu.SMEM(sources[0].shape, sources[0].dtype),
-            pltpu.SemaphoreType.DMA((len(sources),)),
+            pltpu.VMEM((2, 2, width, LANES), f32),
+            *(pltpu.VMEM((2, width, LANES), source.dtype) for source in sources[2:5]),
+            pltpu.SemaphoreType.DMA((14,)),
         ],
         space=pltpu.HBM,
     )
@@ -703,7 +738,7 @@
 
     kept = tuple(lines_of(columns[level]) for level in range(SPLIT) for _ in STATE)
     kept += (lines_of(columns[SPLIT]),) * len(COARSE) + (lines_of(columns[0]),)
-    message = here(FINE * (each + 4) + (count // 2 + 4) * (tps + 1) * 8, LANES)
+    message = here(fine_rows(tps) + 4 * FINE + (count // 2 + 4) * (tps + 1) * 8, LANES)
     *state, rotation, odd, even = call(
         own_kernel,
         kept + (lines_of(LEVELS), message, message),

time: 72.1 us -> 71.8 us (level)
  no operation moved by 1% of the time
where the time goes in v9:
time: 71.8 us; the launch traced here: 71.5 us
  starting transfers between devices  59 us (82%)
  Pallas kernels  7.12 us (10%)
  waiting for transfers between devices  5.34 us (7%)
    ppermute x1, starting transfers between devices, local(): swap = lax.ppermute(edge, 'gy', [(i, gy - 1 - i) for i in range(gy)])  43.4 us
    pallas_call x5, Pallas kernels, call(): pl.pallas_call(kernel, out_shape=outs, in_specs=[pl.BlockSpec(memory_spac...  7.12 us
    ppermute x1, starting transfers between devices, local(): lax.ppermute(mirror, ('gx', 'gy'), [(i * gy + top, (gx - 1 - i) * gy + to...  7 us
    ppermute x1, starting transfers between devices, local(): by_odd = lax.ppermute(odd, 'gx', odd_pairs)  6.7 us
    ppermute x1, waiting for transfers between devices, local(): by_even = lax.ppermute(even, 'gx', even_pairs)  3.39 us
    ppermute x1, starting transfers between devices, local(): by_even = lax.ppermute(even, 'gx', even_pairs)  1.95 us
  transfers between devices with their start and end apart: 4, of which 3 were waited for; matrix products, arithmetic and copies ran while one was open for 0% of the time, Pallas kernels for 2%

profile of v9, /device:TPU:65, one launch (start us, length us, event | category | flops | bytes accessed | tf_op | source)
XLA Modules:
  0.0 71.5 jit_solution(16334212380585152163)
XLA Ops:
  0.0 1.5 %shard_map.64 = (f32[136,128]{1,0:T(8,128)S(1)}, f32[136,128]{1,0:T(8,128)S(1)}, f32[136,128]{1,0:T(8,128)S(1)}, f32[2,32,1536]{2,1,0:T(8,128)S(1)}, f32[32,1536...) custom-call(s32[24,32]{1,0:T(8,128)} %bitcast.2, ...), custom_call_target="tpu_custom_call" | custom-call | tf_op jit(solution)/shard_map/pallas_call | solution.py:694
  1.5 43.4 %collective-permute-start = (f32[136,128]{1,0:T(8,128)S(1)}, f32[136,128]{1,0:T(8,128)S(1)}, u32[]{:S(2)}, u32[]{:S(2)}) collective-permute-start(f32[136,128]{1,0:T(8,128)S(1)} %get-tuple-element.52), channel_id=1, source_target_pairs={{0,1},{1,0},{2,3},{3,2},{4,5},{5,4},{6,7},{7,6},{8,9},{9,8},{10,11... | collective-permute-start | bytes 208904 | tf_op jit(solution)/shard_map/ppermute | solution.py:727
  44.8 7.0 %collective-permute-start.1 = (f32[136,128]{1,0:T(8,128)S(1)}, f32[136,128]{1,0:T(8,128)S(1)}, u32[]{:S(2)}, u32[]{:S(2)}) collective-permute-start(f32[136,128]{1,0:T(8,128)S(1)} %get-tuple-element.53), channel_id=1, source_target_pairs={{1,255},{3,253},{5,251},{7,249},{9,247},{11,245},{13,243},{15,241}... | collective-permute-start | bytes 208904 | tf_op jit(solution)/shard_map/ppermute | solution.py:724
  51.8 0.3 shard_map.65.own_ref
  52.1 0.0 collective-permute-done.swap_ref
  52.1 1.4 %collective-permute-done.1.folded_ref = f32[136,128]{1,0:T(8,128)S(1)} collective-permute-done((f32[136,128]{1,0:T(8,128)S(1)}, f32[136,128]{1,0:T(8,128)S(1)}, u32[]{:S(2)}, u32[]{:S(2)}) %collective-permute-start.1) | collective-permute-done | bytes 69664 | tf_op jit(solution)/shard_map/ppermute | solution.py:724
  53.5 1.5 %shard_map.66 = (f32[40,8,512]{2,1,0:T(8,128)S(1)}, f32[40,8,512]{2,1,0:T(8,128)S(1)}, f32[40,8,512]{2,1,0:T(8,128)S(1)}, f32[40,8,512]{2,1,0:T(8,128)S(1)}, f32...) custom-call(f32[1536,128]{1,0:T(8,128)S(1)} %shard_map.65.own_ref, ...), custom_call_target="tpu_custom_call" | custom-call | tf_op jit(solution)/shard_map/pallas_call | solution.py:694
  55.0 6.7 %collective-permute-start.2 = (f32[440,128]{1,0:T(8,128)S(1)}, f32[440,128]{1,0:T(8,128)S(1)}, u32[]{:S(2)}, u32[]{:S(2)}) collective-permute-start(f32[440,128]{1,0:T(8,128)S(1)} %get-tuple-element.56), channel_id=1, source_target_pairs={{0,254},{2,4},{4,2},{6,8},{8,6},{10,12},{12,10},{14,16},{16,14},{1... | collective-permute-start | bytes 675848 | tf_op jit(solution)/shard_map/ppermute | solution.py:748
  61.7 2.0 %collective-permute-start.3 = (f32[440,128]{1,0:T(8,128)S(1)}, f32[440,128]{1,0:T(8,128)S(1)}, u32[]{:S(2)}, u32[]{:S(2)}) collective-permute-start(f32[440,128]{1,0:T(8,128)S(1)} %get-tuple-element.57), channel_id=1, source_target_pairs={{0,2},{2,0},{4,6},{6,4},{8,10},{10,8},{12,14},{14,12},{16,18},{18,... | collective-permute-start | bytes 675848 | tf_op jit(solution)/shard_map/ppermute | solution.py:749
  63.7 0.9 %shard_map.67 = (f32[32,8,512]{2,1,0:T(8,128)S(1)}, f32[32,8,512]{2,1,0:T(8,128)S(1)}, f32[32,8,512]{2,1,0:T(8,128)S(1)}, f32[32,8,512]{2,1,0:T(8,128)S(1)}, f32...) custom-call(f32[4,8,512]{2,1,0:T(8,128)S(1)} %get-tuple-element.58.r, ...), custom_call_target="tpu_custom_call" | custom-call | tf_op jit(solution)/shard_map/pallas_call | solution.py:694
  64.5 0.5 collective-permute-done.2.odd_ref
  65.1 3.4 %collective-permute-done.3.even_ref = f32[440,128]{1,0:T(8,128)S(1)} collective-permute-done((f32[440,128]{1,0:T(8,128)S(1)}, f32[440,128]{1,0:T(8,128)S(1)}, u32[]{:S(2)}, u32[]{:S(2)}) %collective-permute-start.3) | collective-permute-done | bytes 225312 | tf_op jit(solution)/shard_map/ppermute | solution.py:749
  68.5 3.1 %shard_map.68 = (f32[2,32,1536]{2,1,0:T(8,128)}, f32[40,8,512]{2,1,0:T(8,128)S(1)}, f32[40,8,512]{2,1,0:T(8,128)S(1)}, f32[40,8,512]{2,1,0:T(8,128)S(1)}, f32[40...) custom-call(f32[440,128]{1,0:T(8,128)S(1)} %collective-permute-done., ...), custom_call_target="tpu_custom_call", output_to_operand_aliasing={{1}: (3, {}), {2}: (4, {}), {3}: (5, {}), {4}: (6, {}), {5}... | custom-call | tf_op jit(solution)/shard_map/pallas_call | solution.py:694
Async XLA Ops:
  1.5 50.7 %collective-permute-start = (f32[136,128]{1,0:T(8,128)S(1)}, f32[136,128]{1,0:T(8,128)S(1)}, u32[]{:S(2)}, u32[]{:S(2)}) collective-permute-start(f32[136,128]{1,0:T(8,128)S(1)} %get-tuple-element.52), channel_id=1, source_target_pairs={{0,1},{1,0},{2,3},{3,2},{4,5},{5,4},{6,7},{7,6},{8,9},{9,8},{10,11... | collective-permute-start | bytes 208904 | tf_op jit(solution)/shard_map/ppermute | solution.py:727
  44.8 8.7 %collective-permute-start.1 = (f32[136,128]{1,0:T(8,128)S(1)}, f32[136,128]{1,0:T(8,128)S(1)}, u32[]{:S(2)}, u32[]{:S(2)}) collective-permute-start(f32[136,128]{1,0:T(8,128)S(1)} %get-tuple-element.53), channel_id=1, source_target_pairs={{1,255},{3,253},{5,251},{7,249},{9,247},{11,245},{13,243},{15,241}... | collective-permute-start | bytes 208904 | tf_op jit(solution)/shard_map/ppermute | solution.py:724
  55.0 10.1 %collective-permute-start.2 = (f32[440,128]{1,0:T(8,128)S(1)}, f32[440,128]{1,0:T(8,128)S(1)}, u32[]{:S(2)}, u32[]{:S(2)}) collective-permute-start(f32[440,128]{1,0:T(8,128)S(1)} %get-tuple-element.56), channel_id=1, source_target_pairs={{0,254},{2,4},{4,2},{6,8},{8,6},{10,12},{12,10},{14,16},{16,14},{1... | collective-permute-start | bytes 675848 | tf_op jit(solution)/shard_map/ppermute | solution.py:748
  61.7 6.8 %collective-permute-start.3 = (f32[440,128]{1,0:T(8,128)S(1)}, f32[440,128]{1,0:T(8,128)S(1)}, u32[]{:S(2)}, u32[]{:S(2)}) collective-permute-start(f32[440,128]{1,0:T(8,128)S(1)} %get-tuple-element.57), channel_id=1, source_target_pairs={{0,2},{2,0},{4,6},{6,4},{8,10},{10,8},{12,14},{14,12},{16,18},{18,... | collective-permute-start | bytes 675848 | tf_op jit(solution)/shard_map/ppermute | solution.py:749
